TPU v7x, 32 devices: a whole 2x2x4 slice. The times are simulated.
32 devices in a mesh: sub: 16 (over z, x, core), panel: 2 (over y).
Axes of the slice: x: 2, y: 2, z: 4, core: 2. Of those that a mesh axis runs over, the one named last changes fastest.
Arguments:
- solution: float32 [16384, 256], P('sub', 'panel'), may hold values from -6 to 6
- residual: float32 [16384, 256], P('sub', 'panel'), may hold values from -25 to 25
- shadow: float32 [16384, 256], P('sub', 'panel'), may hold values from -120 to 120
- direction: float32 [16384, 256], P('sub', 'panel'), may hold values from -6 to 6
- old_image: float32 [16384, 256], P('sub', 'panel'), may hold values from -6 to 6
- rho_prev: float32 [256], P('panel'), may hold values from 1 to 4
- alpha_prev: float32 [256], P('panel'), may hold values from 0.5 to 2
- omega_prev: float32 [256], P('panel'), may hold values from 0.5 to 2
- lower_inverse: bfloat16 [16, 1792, 1792], P('sub', None, 'panel'), may hold values from -0.4 to 0.4, as said below
- upper_inverse: bfloat16 [16, 1792, 1792], P('sub', None, 'panel'), may hold values from -0.4 to 0.4, as said below
- neighbours: int32 [16, 16384], P(None, 'sub'), may hold values from 0 to 1792, as said below
- edge_weight: float32 [16, 16384], P(None, 'sub'), may hold values from 0.1 to 1
- node_shift: float32 [16384], P('sub'), may hold values from 3 to 12
- send_rows: int32 [16, 2, 384], P('sub'), may hold values from 0 to 1023
Outputs:
- new_solution: float32 [16384, 256], P('sub', 'panel')
- new_residual: float32 [16384, 256], P('sub', 'panel')
- step_alpha: float32 [256], P('panel')
- step_omega: float32 [256], P('panel')
- next_rho: float32 [256], P('panel')
Inputs may be any that keep to these rules, and one draw needn't show every extreme that they name: lower_inverse[s] is zero above its diagonal. upper_inverse[s] is zero below its diagonal. `neighbours`: an entry below 1024 is an owned node, from 1024 a ghost node from the lower neighbour's list, from 1408 one from the upper neighbour's list; 1792 marks an empty slot. send_rows[s, 0] lists the rows of subdomain s that subdomain s - 1 holds as ghosts, send_rows[s, 1] those that subdomain s + 1 holds, modulo 16.
All inputs are finite; a program needn't handle non-finite values.
Results may differ from a plain program's by a relative error of at most 0.0097.
Values may be sent and summed in bfloat16 or wider, within the bound.
No kernel may reach another device: no remote copies, remote signals or barrier semaphores. Data moves between devices by JAX's collectives and lax.ppermute only.
A program may use at most 64 MiB of HBM per device.

v0:
```python
import jax
import jax.numpy as jnp
from jax import lax
from jax.experimental import pallas as pl
from jax.experimental.pallas import tpu as pltpu
from jax.sharding import PartitionSpec as P

FLOOR_SHARE = 0.3
EPSILON = 1e-06
AXES = ("sub", "panel")


def send(values, route):
    subs = lax.axis_size("sub")
    panels = lax.axis_size("panel")
    pairs = []
    for s in range(subs):
        for p in range(panels):
            target = route(s, p)
            if target is not None:
                pairs.append((s * panels + p, (target[0] % subs) * panels + target[1]))
    return lax.ppermute(values, AXES, pairs)


def merge_repeated(links, weights):
    merged = []
    for k in range(links.shape[0]):
        total = weights[k : k + 1]
        for j in range(k):
            total += jnp.where(links[j : j + 1] == links[k : k + 1], weights[j : j + 1], 0.0)
        merged.append(total)
    return jnp.concatenate(merged, axis=0)


def coupling_kernel(neighbours_ref, weight_ref, out_ref, link_rows, weight_rows):
    links = neighbours_ref[...]
    link_rows[...] = links.T
    weight_rows[...] = merge_repeated(links, weight_ref[...]).T
    group, lanes = 16, 128
    shape = (group, out_ref.shape[1])
    repeats = shape[1] // lanes
    columns = lax.broadcasted_iota(jnp.int32, shape, 1).astype(jnp.int16)

    def body(index, carry):
        rows = pl.ds(index * group, group)
        links, weights = link_rows[rows, :], weight_rows[rows, :]
        total = jnp.zeros(shape, jnp.bfloat16)
        for k in range(links.shape[1]):
            link = jnp.broadcast_to(links[:, k : k + 1], (group, lanes)).astype(jnp.int16)
            weight = jnp.broadcast_to(weights[:, k : k + 1], (group, lanes)).astype(jnp.bfloat16)
            hit = jnp.concatenate([link] * repeats, axis=1) == columns
            total = jnp.where(hit, jnp.concatenate([weight] * repeats, axis=1), total)
        out_ref[rows, :] = total
        return carry

    lax.fori_loop(0, out_ref.shape[0] // group, body, 0, unroll=4)


def coupling_rows(neighbours, edge_weight, ext, begin, count):
    slots = neighbours.shape[0]
    rows = 128
    return pl.pallas_call(
        coupling_kernel,
        grid=(count,),
        in_specs=[pl.BlockSpec((slots, rows), lambda i: (0, i + begin))] * 2,
        out_specs=pl.BlockSpec((rows, ext), lambda i: (i, 0)),
        out_shape=jax.ShapeDtypeStruct((rows * count, ext), jnp.bfloat16),
        scratch_shapes=[
            pltpu.VMEM((rows, slots), jnp.int32),
            pltpu.VMEM((rows, slots), jnp.float32),
        ],
        cost_estimate=pl.CostEstimate(
            flops=50 * slots * rows * count * ext,
            bytes_accessed=2 * rows * count * ext,
            transcendentals=0,
        ),
        compiler_params=pltpu.CompilerParams(vmem_limit_bytes=8 << 20),
    )(neighbours, edge_weight)


def operate_kernel(closing, *refs):
    part, swapped, same_up, cross_up, same_down, cross_down, diagonal, shadow = refs[:8]
    refs = refs[8:]
    if closing:
        middle, refs = refs[0], refs[1:]
    *weights, hat_ref, image_ref, sums_ref, extended = refs
    own, border = part.shape[0], same_up.shape[0]
    hat = part[...] + swapped[...].astype(jnp.float32)
    hat_ref[...] = hat
    extended[:own] = hat.astype(jnp.bfloat16)
    for at, (same, cross) in enumerate(((same_up, cross_up), (same_down, cross_down))):
        ghost = same[...].astype(jnp.float32) + cross[...].astype(jnp.float32)
        extended[own + at * border : own + (at + 1) * border] = ghost.astype(jnp.bfloat16)
    begin = 0
    sums = 0.0
    for weight in weights:
        rows = slice(begin, begin + weight.shape[0])
        begin += weight.shape[0]
        coupled = jnp.dot(weight[...], extended[...], preferred_element_type=jnp.float32)
        image = diagonal[rows] * hat_ref[rows] - coupled
        image_ref[rows] = image
        if closing:
            pairs = (
                (image, middle[rows]),
                (image, image),
                (shadow[rows], middle[rows]),
                (shadow[rows], image),
            )
        else:
            pairs = ((shadow[rows], image), (image, image))
        sums += jnp.concatenate([jnp.sum(a * b, axis=0, keepdims=True) for a, b in pairs], axis=0)
    sums_ref[...] = jnp.broadcast_to(sums[None], sums_ref.shape)


def operate(parts, diagonal, shadow, middle, coupling, copies):
    closing = middle is not None
    operands = [*parts, diagonal, shadow] + ([middle] if closing else []) + list(coupling)
    own, cols = shadow.shape
    vector = jax.ShapeDtypeStruct((own, cols), jnp.float32)
    count = 4 if closing else 2
    ext = coupling[0].shape[1]
    in_vmem = pl.BlockSpec(memory_space=pltpu.VMEM)
    return pl.pallas_call(
        lambda *refs: operate_kernel(closing, *refs),
        in_specs=[in_vmem] * len(operands),
        out_specs=[in_vmem] * 3,
        out_shape=[vector, vector, jax.ShapeDtypeStruct((copies, count, cols), jnp.float32)],
        scratch_shapes=[pltpu.VMEM((ext, cols), jnp.bfloat16)],
        cost_estimate=pl.CostEstimate(
            flops=2 * own * ext * cols, bytes_accessed=2 * own * ext, transcendentals=0
        ),
        compiler_params=pltpu.CompilerParams(vmem_limit_bytes=24 << 20),
        name="operate_closing" if closing else "operate_second",
    )(*operands)


def matmul(left, right):
    return jnp.dot(left, right, preferred_element_type=jnp.float32)


def per_device(
    solution,
    residual,
    shadow,
    direction,
    old_image,
    rho_prev,
    alpha_prev,
    omega_prev,
    lower_inverse,
    upper_inverse,
    neighbours,
    edge_weight,
    node_shift,
    send_rows,
):
    panel = lax.axis_index("panel")
    first = panel == 0
    own, cols = residual.shape
    node_count = own * lax.axis_size("sub")
    lower = lower_inverse[0]
    ext, half = lower.shape
    upper = upper_inverse[0, :own]
    border = send_rows.shape[2]
    tail = own - half

    blocks = own // 128
    cuts = (0, blocks // 2, blocks)
    coupling = []

    def next_coupling(trigger):
        begin, end = cuts[len(coupling) : len(coupling) + 2]
        trigger, links = lax.optimization_barrier((trigger, neighbours))
        coupling.append(coupling_rows(links, edge_weight, ext, begin, end - begin))
        return trigger

    def meet(arrived, value):
        return lax.optimization_barrier((arrived, value))

    present = jnp.where(neighbours < ext, edge_weight, 0.0)
    diagonal = jnp.broadcast_to((node_shift + jnp.sum(present, axis=0))[:, None], (own, cols))
    rows = lax.broadcasted_iota(jnp.int32, (1, own), 1)
    select = (send_rows[0].reshape(2 * border, 1) == rows).astype(jnp.bfloat16)

    def by_panel(zero, one):
        return jnp.where(first, zero, one)

    diagonal_rows = lax.dynamic_slice_in_dim(lower, panel * half, half, axis=0)

    def precondition(vector, chosen_upper):
        rounded = vector.astype(jnp.bfloat16)
        ghosts = matmul(select, rounded).astype(jnp.bfloat16)
        head, rest = rounded[:half], jnp.concatenate([rounded[half:], ghosts], axis=0)
        mine, payload = by_panel(head, rest), by_panel(rest, head)
        build = chosen_upper is None
        if build:
            payload, chosen = lax.optimization_barrier((payload, select))
            chosen_upper = matmul(chosen, upper).astype(jnp.bfloat16)
        received = send(payload, lambda s, p: (s, 1 - p))
        early = matmul(lower[half:], mine).astype(jnp.bfloat16)
        passed_others = send(early, lambda s, p: (s, 1) if p == 0 else None)
        if build:
            received, chosen_upper = meet(received, chosen_upper)
        pair = jnp.concatenate([received, mine], axis=1)
        up, down = pair[tail + border :], pair[tail : tail + border]
        from_lower = send(up, lambda s, p: (s + 1, 1) if p == 1 else None)
        from_upper = send(down, lambda s, p: (s - 1, 1) if p == 1 else None)
        late = matmul(lower[half:], received).astype(jnp.bfloat16)
        if build:
            late = next_coupling(late)
        passed_mine = send(late, lambda s, p: (s, 1) if p == 0 else None)
        if build:
            passed_mine, coupling[-1] = meet(passed_mine, coupling[-1])
        rhs = by_panel(pair, jnp.concatenate([pair[:tail], from_lower, from_upper], axis=0))
        passed = jnp.concatenate([passed_others, passed_mine], axis=1).astype(jnp.float32)
        inner = (matmul(diagonal_rows, rhs) + passed).astype(jnp.bfloat16)
        inner = lax.optimization_barrier(inner)
        others, mine = inner[:, :cols], inner[:, cols:]
        other_part = matmul(upper, others).astype(jnp.bfloat16)
        other_edge = matmul(chosen_upper, others).astype(jnp.bfloat16)
        swapped = send(other_part, lambda s, p: (s, 1 - p))
        cross_up = send(other_edge[border:], lambda s, p: (s + 1, 1 - p))
        cross_down = send(other_edge[:border], lambda s, p: (s - 1, 1 - p))
        edge = matmul(chosen_upper, mine).astype(jnp.bfloat16)
        part = matmul(upper, mine)
        same_up = send(edge[border:], lambda s, p: (s + 1, p))
        same_down = send(edge[:border], lambda s, p: (s - 1, p))
        return (part, swapped, same_up, cross_up, same_down, cross_down), chosen_upper

    copies = lax.axis_size("sub")

    def sub_mean(values):
        return jnp.sum(lax.all_to_all(values, "sub", 0, 0), axis=0) / node_count

    sums = jnp.stack([jnp.sum(shadow * residual, axis=0), jnp.sum(shadow * shadow, axis=0)])
    sums = next_coupling(jnp.broadcast_to(sums[None], (copies, 2, cols)))
    opening, coupling[-1] = meet(sub_mean(sums), coupling[-1])
    rho_now, shadow_square = opening[0], opening[1]
    step_beta = rho_now / rho_prev * (alpha_prev / omega_prev)
    new_direction = residual + step_beta * (direction - omega_prev * old_image)
    parts, chosen_upper = precondition(new_direction, None)
    direction_hat, image_new, sums = operate(parts, diagonal, shadow, None, coupling, copies)
    second = sub_mean(sums)
    step_alpha = rho_now / jnp.maximum(second[0], FLOOR_SHARE * jnp.sqrt(shadow_square * second[1]))
    middle = residual - step_alpha * image_new
    parts, _ = precondition(middle, chosen_upper)
    middle_hat, tested, sums = operate(parts, diagonal, shadow, middle, coupling, copies)
    closing = sub_mean(sums)
    step_omega = closing[0] / (closing[1] + EPSILON)
    next_rho = closing[2] - step_omega * closing[3]
    new_residual = middle - step_omega * tested
    new_solution = solution + step_alpha * direction_hat + step_omega * middle_hat
    return (new_solution, new_residual, step_alpha, step_omega, next_rho)


def solution(mesh):
    assert mesh.shape["panel"] == 2
    placed = (
        P("sub", "panel"),
        P("sub", "panel"),
        P("sub", "panel"),
        P("sub", "panel"),
        P("sub", "panel"),
        P("panel"),
        P("panel"),
        P("panel"),
        P("sub", None, "panel"),
        P("sub", None, "panel"),
        P(None, "sub"),
        P(None, "sub"),
        P("sub"),
        P("sub", None, None),
    )
    return jax.shard_map(
        per_device,
        mesh=mesh,
        in_specs=placed,
        out_specs=(P("sub", "panel"), P("sub", "panel"), P("panel"), P("panel"), P("panel")),
        check_vma=False,
    )
```

profile of v0, /device:TPU:0, one launch (start us, length us, event | category | flops | bytes accessed | tf_op | source)
XLA Modules:
  0.0 148.7 jit_solution(12344702330580993145)
XLA Ops:
  0.7 1.4 multiply_reduce_fusion.1
  2.1 0.6 broadcast_in_dim.8
  2.7 7.4 %all-to-all-start = ((f32[16,2,128]{2,1,0:T(2,128)}), f32[16,2,128]{2,1,0:T(2,128)S(1)}, u32[]{:S(2)}, u32[]{:S(2)}) async-start(f32[16,2,128]{2,1,0:T(2,128)} %broadcast_in_dim.8), calls=%async_computation | async-start | bytes 32768 | tf_op jit(solution)/shard_map/all_to_all | solution.py:233
  10.1 0.7 eq.19
  10.8 0.6 copy-done.19
  11.3 1.5 %fusion.1 = bf16[768,1024]{1,0:T(8,128)(2,1)} fusion(s32[768]{0:T(1024)S(1)} %eq.19), kind=kLoop, calls=%fused_computation.2 | loop fusion | flops 1572864 | bytes 1575936 | tf_op jit(solution)/shard_map/convert_element_type | solution.py:183
  12.9 3.9 %shard_map.173.refs_8_.refs_9_ = bf16[512,1792]{1,0:T(8,128)(2,1)S(1)} custom-call(s32[16,1024]{1,0:T(8,128)S(1)} %copy-done.8, f32[16,1024]{1,0:T(8,128)S(1)} %copy-done.7), custom_call_target="tpu_custom_call" | custom-call | flops 734003200 | bytes 1835008 | tf_op jit(solution)/shard_map/pallas_call | solution.py:62
  16.8 0.6 reduce_sum.56
  17.4 0.7 broadcast_multiply_fusion.2
  18.1 0.7 fusion.128
  18.8 0.9 add_convert_fusion
  19.7 0.7 fusion.68
  20.7 1.3 fusion.76
  22.0 4.1 %collective-permute-start.3 = (bf16[896,128]{1,0:T(8,128)(2,1)}, bf16[896,128]{1,0:T(8,128)(2,1)}, u32[]{:S(2)}, u32[]{:S(2)}) collective-permute-start(bf16[896,128]{1,0:T(8,128)(2,1)} %fusion.76), channel_id=1, source_target_pairs={{0,1},{2,3},{4,5},{6,7},{8,9},{10,11},{12,13},{14,15},{16,17},{18,... | collective-permute-start | bytes 688136 | tf_op jit(solution)/shard_map/ppermute | solution.py:22
  26.1 3.3 %fusion.13 = bf16[768,896]{1,0:T(8,128)(2,1)S(1)} fusion(bf16[768,1024]{1,0:T(8,128)(2,1)S(1)} %copy-done.14, bf16[1,1792,896]{2,1,0:T(8,128)(2,1)} %param.23), kind=kOutput, calls=%fused_computation.14 | convolution fusion | flops 1409974272 | bytes 4784128 | tf_op jit(solution)/shard_map/dot_general | solution.py:138
  29.4 6.5 %collective-permute-done = bf16[896,128]{1,0:T(8,128)(2,1)S(1)} collective-permute-done((bf16[896,128]{1,0:T(8,128)(2,1)S(1)}, bf16[896,128]{1,0:T(8,128)(2,1)S(1)}, u32[]{:S(2)}, u32[]{:S(2)}) %collective-permute-start) | collective-permute-done | bytes 229408 | tf_op jit(solution)/shard_map/ppermute | solution.py:22
  35.9 1.3 fusion.79
  37.2 0.7 fusion.123
  37.9 5.1 %collective-permute-start.4 = (bf16[896,128]{1,0:T(8,128)(2,1)}, bf16[896,128]{1,0:T(8,128)(2,1)}, u32[]{:S(2)}, u32[]{:S(2)}) collective-permute-start(bf16[896,128]{1,0:T(8,128)(2,1)} %fusion.79), channel_id=1, source_target_pairs={{0,1},{2,3},{4,5},{6,7},{8,9},{10,11},{12,13},{14,15},{16,17},{18,... | collective-permute-start | bytes 688136 | tf_op jit(solution)/shard_map/ppermute | solution.py:22
  43.0 1.3 collective-permute-start.1
  44.4 1.4 collective-permute-start.2
  45.8 3.9 %shard_map.174.refs_9_.refs_10_ = bf16[512,1792]{1,0:T(8,128)(2,1)S(1)} custom-call(s32[16,1024]{1,0:T(8,128)S(1)} %copy-done.8, f32[16,1024]{1,0:T(8,128)S(1)} %copy-done.7), custom_call_target="tpu_custom_call" | custom-call | flops 734003200 | bytes 1835008 | tf_op jit(solution)/shard_map/pallas_call | solution.py:62
  49.8 2.9 %fusion.41 = bf16[896,256]{1,0:T(8,128)(2,1)S(1)} fusion(bf16[1,1792,896]{2,1,0:T(8,128)(2,1)} %param.22, s32[]{:T(128)S(6)} %select_n.39, bf16[896,128]{1,0:T(8,128)(2,1)S(1)} %copy-done.13, bf16[896,128]{1,0:T(8,128)(2,1)S(1)} %copy-done.16, bf16[384,256]{1,0:T(8,128)(2,1)} %collective-permute-done.2, bf16[384,256]{1,0:T(8,128)(2,1)} %collective-permute-done.1, ...), kind=kOutput, calls=%fused_computation.34 | convolution fusion | flops 414941184 | bytes 3440645 | tf_op jit(solution)/shard_map/dot_general | solution.py:138
  52.7 0.5 convolution_convert_fusion.3
  53.2 0.5 convolution_convert_fusion.2
  53.8 0.8 copy-done.25
  54.6 0.6 fusion.70
  55.3 3.0 %collective-permute-start.8 = (bf16[384,128]{1,0:T(8,128)(2,1)S(1)}, bf16[384,128]{1,0:T(8,128)(2,1)S(1)}, u32[]{:S(2)}, u32[]{:S(2)}) collective-permute-start(bf16[384,128]{1,0:T(8,128)(2,1)S(1)} %get-tuple-element.63), channel_id=1, source_target_pairs={{0,30},{1,31},{2,0},{3,1},{4,2},{5,3},{6,4},{7,5},{8,6},{9,7},{10,... | collective-permute-start | bytes 294920 | tf_op jit(solution)/shard_map/ppermute | solution.py:22
  58.3 8.5 %collective-permute-start.9 = (bf16[384,128]{1,0:T(8,128)(2,1)S(1)}, bf16[384,128]{1,0:T(8,128)(2,1)S(1)}, u32[]{:S(2)}, u32[]{:S(2)}) collective-permute-start(bf16[384,128]{1,0:T(8,128)(2,1)S(1)} %get-tuple-element.61), channel_id=1, source_target_pairs={{0,31},{1,30},{2,1},{3,0},{4,3},{5,2},{6,5},{7,4},{8,7},{9,6},{10,... | collective-permute-start | bytes 294920 | tf_op jit(solution)/shard_map/ppermute | solution.py:22
  66.8 0.6 fusion.47.refs_0_
  67.4 1.5 %collective-permute-done.9.refs_5_ = bf16[384,128]{1,0:T(8,128)(2,1)S(1)} collective-permute-done((bf16[384,128]{1,0:T(8,128)(2,1)S(1)}, bf16[384,128]{1,0:T(8,128)(2,1)S(1)}, u32[]{:S(2)}, u32[]{:S(2)}) %collective-permute-start.9) | collective-permute-done | bytes 98336 | tf_op jit(solution)/shard_map/ppermute | solution.py:22
  69.0 5.4 %collective-permute-done.7.refs_3_ = bf16[384,128]{1,0:T(8,128)(2,1)S(1)} collective-permute-done((bf16[384,128]{1,0:T(8,128)(2,1)S(1)}, bf16[384,128]{1,0:T(8,128)(2,1)S(1)}, u32[]{:S(2)}, u32[]{:S(2)}) %collective-permute-start.7) | collective-permute-done | bytes 98336 | tf_op jit(solution)/shard_map/ppermute | solution.py:22
  74.6 1.2 operate_second.1
  75.8 0.8 copy-done.3
  76.6 0.8 copy-done.6
  77.4 9.4 %all_to_all.15 = f32[16,2,128]{2,1,0:T(2,128)S(1)} all-to-all(f32[16,2,128]{2,1,0:T(2,128)S(1)} %get-tuple-element.35), channel_id=1, replica_groups=mesh['sub'=16,'panel'=2] {'sub'}, dimensions={0} | all-to-all | bytes 32768 | tf_op jit(solution)/shard_map/all_to_all | solution.py:233
  86.9 0.5 bitcast_divide_fusion
  87.4 1.4 fusion.135
  88.9 0.7 fusion.69
  89.6 2.0 %collective-permute-start.10 = (bf16[896,128]{1,0:T(8,128)(2,1)S(1)}, bf16[896,128]{1,0:T(8,128)(2,1)S(1)}, u32[]{:S(2)}, u32[]{:S(2)}) collective-permute-start(bf16[896,128]{1,0:T(8,128)(2,1)S(1)} %get-tuple-element.49), channel_id=1, source_target_pairs={{0,1},{1,0},{2,3},{3,2},{4,5},{5,4},{6,7},{7,6},{8,9},{9,8},{10,11... | collective-permute-start | bytes 688136 | tf_op jit(solution)/shard_map/ppermute | solution.py:22
  91.7 0.6 fusion.82
  92.3 2.0 %collective-permute-start.13 = (bf16[896,128]{1,0:T(8,128)(2,1)S(1)}, bf16[896,128]{1,0:T(8,128)(2,1)S(1)}, u32[]{:S(2)}, u32[]{:S(2)}) collective-permute-start(bf16[896,128]{1,0:T(8,128)(2,1)S(1)} %fusion.82), channel_id=1, source_target_pairs={{0,1},{2,3},{4,5},{6,7},{8,9},{10,11},{12,13},{14,15},{16,17},{18,... | collective-permute-start | bytes 688136 | tf_op jit(solution)/shard_map/ppermute | solution.py:22
  94.3 3.4 %collective-permute-done.10 = bf16[896,128]{1,0:T(8,128)(2,1)S(1)} collective-permute-done((bf16[896,128]{1,0:T(8,128)(2,1)S(1)}, bf16[896,128]{1,0:T(8,128)(2,1)S(1)}, u32[]{:S(2)}, u32[]{:S(2)}) %collective-permute-start.10) | collective-permute-done | bytes 229408 | tf_op jit(solution)/shard_map/ppermute | solution.py:22
  97.7 0.6 fusion.85
  98.2 4.6 %collective-permute-start.14 = (bf16[896,128]{1,0:T(8,128)(2,1)S(1)}, bf16[896,128]{1,0:T(8,128)(2,1)S(1)}, u32[]{:S(2)}, u32[]{:S(2)}) collective-permute-start(bf16[896,128]{1,0:T(8,128)(2,1)S(1)} %fusion.85), channel_id=1, source_target_pairs={{0,1},{2,3},{4,5},{6,7},{8,9},{10,11},{12,13},{14,15},{16,17},{18,... | collective-permute-start | bytes 688136 | tf_op jit(solution)/shard_map/ppermute | solution.py:22
  102.9 0.7 collective-permute-start.11
  103.6 0.7 collective-permute-start.12
  104.3 2.0 %collective-permute-done.14 = bf16[896,128]{1,0:T(8,128)(2,1)S(1)} collective-permute-done((bf16[896,128]{1,0:T(8,128)(2,1)S(1)}, bf16[896,128]{1,0:T(8,128)(2,1)S(1)}, u32[]{:S(2)}, u32[]{:S(2)}) %collective-permute-start.14) | collective-permute-done | bytes 229408 | tf_op jit(solution)/shard_map/ppermute | solution.py:22
  106.3 0.7 fusion.38
  107.0 0.5 convolution_convert_fusion.1
  107.5 0.5 convolution_convert_fusion
  108.0 0.8 copy-done.26
  108.9 0.6 fusion.73
  109.6 0.5 collective-permute-start.16
  110.1 15.4 %collective-permute-start.19 = (bf16[384,128]{1,0:T(8,128)(2,1)S(1)}, bf16[384,128]{1,0:T(8,128)(2,1)S(1)}, u32[]{:S(2)}, u32[]{:S(2)}) collective-permute-start(bf16[384,128]{1,0:T(8,128)(2,1)S(1)} %get-tuple-element.57), channel_id=1, source_target_pairs={{0,31},{1,30},{2,1},{3,0},{4,3},{5,2},{6,5},{7,4},{8,7},{9,6},{10,... | collective-permute-start | bytes 294920 | tf_op jit(solution)/shard_map/ppermute | solution.py:22
  125.6 0.6 fusion.44.refs_0_
  126.2 1.5 %collective-permute-done.19.refs_5_ = bf16[384,128]{1,0:T(8,128)(2,1)S(1)} collective-permute-done((bf16[384,128]{1,0:T(8,128)(2,1)S(1)}, bf16[384,128]{1,0:T(8,128)(2,1)S(1)}, u32[]{:S(2)}, u32[]{:S(2)}) %collective-permute-start.19) | collective-permute-done | bytes 98336 | tf_op jit(solution)/shard_map/ppermute | solution.py:22
  127.8 5.4 %collective-permute-done.17.refs_3_ = bf16[384,128]{1,0:T(8,128)(2,1)S(1)} collective-permute-done((bf16[384,128]{1,0:T(8,128)(2,1)S(1)}, bf16[384,128]{1,0:T(8,128)(2,1)S(1)}, u32[]{:S(2)}, u32[]{:S(2)}) %collective-permute-start.17) | collective-permute-done | bytes 98336 | tf_op jit(solution)/shard_map/ppermute | solution.py:22
  133.2 1.2 operate_closing.1
  134.4 0.8 copy-done.4
  135.2 0.8 copy-done.5
  136.0 9.5 %all_to_all.16 = f32[16,4,128]{2,1,0:T(4,128)S(1)} all-to-all(f32[16,4,128]{2,1,0:T(4,128)S(1)} %get-tuple-element.38), channel_id=1, replica_groups=mesh['sub'=16,'panel'=2] {'sub'}, dimensions={0} | all-to-all | bytes 65536 | tf_op jit(solution)/shard_map/all_to_all | solution.py:233
  145.6 0.5 fusion.127
  146.1 2.6 %multiply_subtract_fusion = (f32[1024,128]{1,0:T(8,128)}, f32[1024,128]{1,0:T(8,128)}) fusion(f32[1024,128]{1,0:T(8,128)S(1)} %get-tuple-element.48.refs_8_, f32[1024,128]{1,0:T(8,128)} %copy-done.5, f32[128]{0:T(128)S(1)} %get-tuple-element.44, f32[1024,128]{1,0:T(8,128)} %copy-done.4, f32[1024,128]{1,0:T(8,128)} %param.14, f32[1024,128]{1,0:T(8,128)} %copy-done.3, ...), kind=kLoop, calls=%fused_computation.78 | loop fusion | flops 786432 | bytes 3671040 | tf_op jit(solution)/shard_map/sub | solution.py:251
  (88 shorter events, 1.0 us)
Async XLA Ops:
  0.6 12.2 %copy-start.8 = (s32[16,1024]{1,0:T(8,128)S(1)}, s32[16,1024]{1,0:T(8,128)}, u32[]{:S(2)}) copy-start(s32[16,1024]{1,0:T(8,128)} %neighbours_ref.1) | copy-start | bytes 196612
  0.6 12.2 %copy-start.7 = (f32[16,1024]{1,0:T(8,128)S(1)}, f32[16,1024]{1,0:T(8,128)}, u32[]{:S(2)}) copy-start(f32[16,1024]{1,0:T(8,128)} %weight_ref.3) | copy-start | bytes 196612
  2.7 14.1 %all-to-all-start = ((f32[16,2,128]{2,1,0:T(2,128)}), f32[16,2,128]{2,1,0:T(2,128)S(1)}, u32[]{:S(2)}, u32[]{:S(2)}) async-start(f32[16,2,128]{2,1,0:T(2,128)} %broadcast_in_dim.8), calls=%async_computation | async-start | bytes 32768 | tf_op jit(solution)/shard_map/all_to_all | solution.py:233
  10.8 0.6 copy-start.19
  11.3 7.4 %copy-start.11 = (f32[1024,128]{1,0:T(8,128)S(1)}, f32[1024,128]{1,0:T(8,128)}, u32[]{:S(2)}) copy-start(f32[1024,128]{1,0:T(8,128)} %param.15) | copy-start | bytes 1572868
  11.3 7.4 %copy-start.17 = (f32[1024,128]{1,0:T(8,128)S(1)}, f32[1024,128]{1,0:T(8,128)}, u32[]{:S(2)}) copy-start(f32[1024,128]{1,0:T(8,128)} %param.17) | copy-start | bytes 1572868
  11.3 7.4 %copy-start.18 = (f32[1024,128]{1,0:T(8,128)S(1)}, f32[1024,128]{1,0:T(8,128)}, u32[]{:S(2)}) copy-start(f32[1024,128]{1,0:T(8,128)} %param.18) | copy-start | bytes 1572868
  17.4 2.3 %copy-start.20 = (s32[768]{0:T(1024)S(1)}, s32[768]{0:T(1024)}, u32[]{:S(2)}) copy-start(s32[768]{0:T(1024)} %copy-done.19) | copy-start | bytes 9220
  18.8 1.9 %copy-start.23 = (bf16[1,1792,896]{2,1,0:T(8,128)(2,1)S(1)}, bf16[1,1792,896]{2,1,0:T(8,128)(2,1)}, u32[]{:S(2)}) copy-start(bf16[1,1792,896]{2,1,0:T(8,128)(2,1)} %param.22) | copy-start | bytes 9633796
  20.4 5.7 %copy-start.14 = (bf16[768,1024]{1,0:T(8,128)(2,1)S(1)}, bf16[768,1024]{1,0:T(8,128)(2,1)}, u32[]{:S(2)}) copy-start(bf16[768,1024]{1,0:T(8,128)(2,1)} %fusion.1) | copy-start | bytes 4718596
  20.5 16.7 %copy-start.12 = (bf16[896,128]{1,0:T(8,128)(2,1)}, bf16[896,128]{1,0:T(8,128)(2,1)S(1)}, u32[]{:S(2)}) copy-start(bf16[896,128]{1,0:T(8,128)(2,1)S(1)} %get-tuple-element.52) | copy-start | bytes 688132
  22.0 27.8 %collective-permute-start.3 = (bf16[896,128]{1,0:T(8,128)(2,1)}, bf16[896,128]{1,0:T(8,128)(2,1)}, u32[]{:S(2)}, u32[]{:S(2)}) collective-permute-start(bf16[896,128]{1,0:T(8,128)(2,1)} %fusion.76), channel_id=1, source_target_pairs={{0,1},{2,3},{4,5},{6,7},{8,9},{10,11},{12,13},{14,15},{16,17},{18,... | collective-permute-start | bytes 688136 | tf_op jit(solution)/shard_map/ppermute | solution.py:22
  26.1 9.8 %collective-permute-start = (bf16[896,128]{1,0:T(8,128)(2,1)S(1)}, bf16[896,128]{1,0:T(8,128)(2,1)S(1)}, u32[]{:S(2)}, u32[]{:S(2)}) collective-permute-start(bf16[896,128]{1,0:T(8,128)(2,1)S(1)} %get-tuple-element.26), channel_id=1, source_target_pairs={{0,1},{1,0},{2,3},{3,2},{4,5},{5,4},{6,7},{7,6},{8,9},{9,8},{10,11... | collective-permute-start | bytes 688136 | tf_op jit(solution)/shard_map/ppermute | solution.py:22
  29.4 23.9 %copy-start.9 = (bf16[768,896]{1,0:T(8,128)(2,1)}, bf16[768,896]{1,0:T(8,128)(2,1)S(1)}, u32[]{:S(2)}) copy-start(bf16[768,896]{1,0:T(8,128)(2,1)S(1)} %fusion.13) | copy-start | bytes 4128772
  29.4 16.3 %copy-start.21 = (f32[1024]{0:T(1024)S(1)}, f32[1024]{0:T(1024)}, u32[]{:S(2)}) copy-start(f32[1024]{0:T(1024)} %param.26) | copy-start | bytes 12292
  35.9 2.0 %copy-start.15 = (bf16[896,128]{1,0:T(8,128)(2,1)}, bf16[896,128]{1,0:T(8,128)(2,1)S(1)}, u32[]{:S(2)}) copy-start(bf16[896,128]{1,0:T(8,128)(2,1)S(1)} %collective-permute-done) | copy-start | bytes 688132
  37.9 11.8 %collective-permute-start.4 = (bf16[896,128]{1,0:T(8,128)(2,1)}, bf16[896,128]{1,0:T(8,128)(2,1)}, u32[]{:S(2)}, u32[]{:S(2)}) collective-permute-start(bf16[896,128]{1,0:T(8,128)(2,1)} %fusion.79), channel_id=1, source_target_pairs={{0,1},{2,3},{4,5},{6,7},{8,9},{10,11},{12,13},{14,15},{16,17},{18,... | collective-permute-start | bytes 688136 | tf_op jit(solution)/shard_map/ppermute | solution.py:22
  43.0 6.8 %collective-permute-start.1 = (bf16[384,256]{1,0:T(8,128)(2,1)}, bf16[384,256]{1,0:T(8,128)(2,1)}, u32[]{:S(2)}, u32[]{:S(2)}) collective-permute-start(bf16[384,256]{1,0:T(8,128)(2,1)} %get-tuple-element.55), channel_id=1, source_target_pairs={{1,3},{3,5},{5,7},{7,9},{9,11},{11,13},{13,15},{15,17},{17,19},{19... | collective-permute-start | bytes 589832 | tf_op jit(solution)/shard_map/ppermute | solution.py:22
  44.4 5.4 %collective-permute-start.2 = (bf16[384,256]{1,0:T(8,128)(2,1)S(1)}, bf16[384,256]{1,0:T(8,128)(2,1)}, u32[]{:S(2)}, u32[]{:S(2)}) collective-permute-start(bf16[384,256]{1,0:T(8,128)(2,1)S(1)} %get-tuple-element.56), channel_id=1, source_target_pairs={{1,31},{3,1},{5,3},{7,5},{9,7},{11,9},{13,11},{15,13},{17,15},{19,... | collective-permute-start | bytes 589832 | tf_op jit(solution)/shard_map/ppermute | solution.py:22
  45.7 4.0 %copy-start.13 = (bf16[896,128]{1,0:T(8,128)(2,1)S(1)}, bf16[896,128]{1,0:T(8,128)(2,1)}, u32[]{:S(2)}) copy-start(bf16[896,128]{1,0:T(8,128)(2,1)} %copy-done.12) | copy-start | bytes 688132
  45.8 3.9 %copy-start.16 = (bf16[896,128]{1,0:T(8,128)(2,1)S(1)}, bf16[896,128]{1,0:T(8,128)(2,1)}, u32[]{:S(2)}) copy-start(bf16[896,128]{1,0:T(8,128)(2,1)} %copy-done.15) | copy-start | bytes 688132
  49.7 24.9 %copy-start = (bf16[512,1792]{1,0:T(8,128)(2,1)}, bf16[512,1792]{1,0:T(8,128)(2,1)S(1)}, u32[]{:S(2)}) copy-start(bf16[512,1792]{1,0:T(8,128)(2,1)S(1)} %shard_map.174.refs_9_.refs_10_) | copy-start | bytes 5505028
  52.7 1.9 %copy-start.25 = (bf16[1,1792,896]{2,1,0:T(8,128)(2,1)S(1)}, bf16[1,1792,896]{2,1,0:T(8,128)(2,1)}, u32[]{:S(2)}) copy-start(bf16[1,1792,896]{2,1,0:T(8,128)(2,1)} %param.23) | copy-start | bytes 9633796
  55.3 12.1 %collective-permute-start.8 = (bf16[384,128]{1,0:T(8,128)(2,1)S(1)}, bf16[384,128]{1,0:T(8,128)(2,1)S(1)}, u32[]{:S(2)}, u32[]{:S(2)}) collective-permute-start(bf16[384,128]{1,0:T(8,128)(2,1)S(1)} %get-tuple-element.63), channel_id=1, source_target_pairs={{0,30},{1,31},{2,0},{3,1},{4,2},{5,3},{6,4},{7,5},{8,6},{9,7},{10,... | collective-permute-start | bytes 294920 | tf_op jit(solution)/shard_map/ppermute | solution.py:22
  58.2 9.2 %collective-permute-start.6 = (bf16[384,128]{1,0:T(8,128)(2,1)S(1)}, bf16[384,128]{1,0:T(8,128)(2,1)S(1)}, u32[]{:S(2)}, u32[]{:S(2)}) collective-permute-start(bf16[384,128]{1,0:T(8,128)(2,1)S(1)} %get-tuple-element.64), channel_id=1, source_target_pairs={{0,2},{1,3},{2,4},{3,5},{4,6},{5,7},{6,8},{7,9},{8,10},{9,11},{10,... | collective-permute-start | bytes 294920 | tf_op jit(solution)/shard_map/ppermute | solution.py:22
  58.3 16.3 %copy-start.2 = (f32[1024,128]{1,0:T(8,128)S(1)}, f32[1024,128]{1,0:T(8,128)}, u32[]{:S(2)}) copy-start(f32[1024,128]{1,0:T(8,128)} %refs_7_.3) | copy-start | bytes 1572868
  58.3 10.7 %collective-permute-start.9 = (bf16[384,128]{1,0:T(8,128)(2,1)S(1)}, bf16[384,128]{1,0:T(8,128)(2,1)S(1)}, u32[]{:S(2)}, u32[]{:S(2)}) collective-permute-start(bf16[384,128]{1,0:T(8,128)(2,1)S(1)} %get-tuple-element.61), channel_id=1, source_target_pairs={{0,31},{1,30},{2,1},{3,0},{4,3},{5,2},{6,5},{7,4},{8,7},{9,6},{10,... | collective-permute-start | bytes 294920 | tf_op jit(solution)/shard_map/ppermute | solution.py:22
  66.8 7.6 %collective-permute-start.7 = (bf16[384,128]{1,0:T(8,128)(2,1)S(1)}, bf16[384,128]{1,0:T(8,128)(2,1)S(1)}, u32[]{:S(2)}, u32[]{:S(2)}) collective-permute-start(bf16[384,128]{1,0:T(8,128)(2,1)S(1)} %get-tuple-element.62), channel_id=1, source_target_pairs={{0,3},{1,2},{2,5},{3,4},{4,7},{5,6},{6,9},{7,8},{8,11},{9,10},{10,... | collective-permute-start | bytes 294920 | tf_op jit(solution)/shard_map/ppermute | solution.py:22
  66.8 7.6 %collective-permute-start.5 = (bf16[1024,128]{1,0:T(8,128)(2,1)S(1)}, bf16[1024,128]{1,0:T(8,128)(2,1)S(1)}, u32[]{:S(2)}, u32[]{:S(2)}) collective-permute-start(bf16[1024,128]{1,0:T(8,128)(2,1)S(1)} %fusion.70), channel_id=1, source_target_pairs={{0,1},{1,0},{2,3},{3,2},{4,5},{5,4},{6,7},{7,6},{8,9},{9,8},{10,11... | collective-permute-start | bytes 786440 | tf_op jit(solution)/shard_map/ppermute | solution.py:22
  75.8 0.8 copy-start.3
  76.6 0.8 copy-start.6
  87.4 4.3 %copy-start.24 = (bf16[1,1792,896]{2,1,0:T(8,128)(2,1)S(1)}, bf16[1,1792,896]{2,1,0:T(8,128)(2,1)}, u32[]{:S(2)}) copy-start(bf16[1,1792,896]{2,1,0:T(8,128)(2,1)} %param.22) | copy-start | bytes 9633796
  89.6 8.0 %collective-permute-start.10 = (bf16[896,128]{1,0:T(8,128)(2,1)S(1)}, bf16[896,128]{1,0:T(8,128)(2,1)S(1)}, u32[]{:S(2)}, u32[]{:S(2)}) collective-permute-start(bf16[896,128]{1,0:T(8,128)(2,1)S(1)} %get-tuple-element.49), channel_id=1, source_target_pairs={{0,1},{1,0},{2,3},{3,2},{4,5},{5,4},{6,7},{7,6},{8,9},{9,8},{10,11... | collective-permute-start | bytes 688136 | tf_op jit(solution)/shard_map/ppermute | solution.py:22
  92.3 12.0 %collective-permute-start.13 = (bf16[896,128]{1,0:T(8,128)(2,1)S(1)}, bf16[896,128]{1,0:T(8,128)(2,1)S(1)}, u32[]{:S(2)}, u32[]{:S(2)}) collective-permute-start(bf16[896,128]{1,0:T(8,128)(2,1)S(1)} %fusion.82), channel_id=1, source_target_pairs={{0,1},{2,3},{4,5},{6,7},{8,9},{10,11},{12,13},{14,15},{16,17},{18,... | collective-permute-start | bytes 688136 | tf_op jit(solution)/shard_map/ppermute | solution.py:22
  98.2 8.0 %collective-permute-start.14 = (bf16[896,128]{1,0:T(8,128)(2,1)S(1)}, bf16[896,128]{1,0:T(8,128)(2,1)S(1)}, u32[]{:S(2)}, u32[]{:S(2)}) collective-permute-start(bf16[896,128]{1,0:T(8,128)(2,1)S(1)} %fusion.85), channel_id=1, source_target_pairs={{0,1},{2,3},{4,5},{6,7},{8,9},{10,11},{12,13},{14,15},{16,17},{18,... | collective-permute-start | bytes 688136 | tf_op jit(solution)/shard_map/ppermute | solution.py:22
  102.9 1.4 collective-permute-start.11
  103.6 0.7 collective-permute-start.12
  104.3 2.7 %copy-start.10 = (bf16[768,896]{1,0:T(8,128)(2,1)S(1)}, bf16[768,896]{1,0:T(8,128)(2,1)}, u32[]{:S(2)}) copy-start(bf16[768,896]{1,0:T(8,128)(2,1)} %copy-done.9) | copy-start | bytes 4128772
  107.0 1.9 %copy-start.26 = (bf16[1,1792,896]{2,1,0:T(8,128)(2,1)S(1)}, bf16[1,1792,896]{2,1,0:T(8,128)(2,1)}, u32[]{:S(2)}) copy-start(bf16[1,1792,896]{2,1,0:T(8,128)(2,1)} %param.23) | copy-start | bytes 9633796
  109.5 23.6 %copy-start.1 = (bf16[512,1792]{1,0:T(8,128)(2,1)S(1)}, bf16[512,1792]{1,0:T(8,128)(2,1)}, u32[]{:S(2)}) copy-start(bf16[512,1792]{1,0:T(8,128)(2,1)} %copy-done) | copy-start | bytes 5505028
  109.6 16.6 %collective-permute-start.18 = (bf16[384,128]{1,0:T(8,128)(2,1)S(1)}, bf16[384,128]{1,0:T(8,128)(2,1)S(1)}, u32[]{:S(2)}, u32[]{:S(2)}) collective-permute-start(bf16[384,128]{1,0:T(8,128)(2,1)S(1)} %get-tuple-element.59), channel_id=1, source_target_pairs={{0,30},{1,31},{2,0},{3,1},{4,2},{5,3},{6,4},{7,5},{8,6},{9,7},{10,... | collective-permute-start | bytes 294920 | tf_op jit(solution)/shard_map/ppermute | solution.py:22
  109.6 16.6 %collective-permute-start.16 = (bf16[384,128]{1,0:T(8,128)(2,1)S(1)}, bf16[384,128]{1,0:T(8,128)(2,1)S(1)}, u32[]{:S(2)}, u32[]{:S(2)}) collective-permute-start(bf16[384,128]{1,0:T(8,128)(2,1)S(1)} %get-tuple-element.60), channel_id=1, source_target_pairs={{0,2},{1,3},{2,4},{3,5},{4,6},{5,7},{6,8},{7,9},{8,10},{9,11},{10,... | collective-permute-start | bytes 294920 | tf_op jit(solution)/shard_map/ppermute | solution.py:22
  110.1 17.6 %collective-permute-start.19 = (bf16[384,128]{1,0:T(8,128)(2,1)S(1)}, bf16[384,128]{1,0:T(8,128)(2,1)S(1)}, u32[]{:S(2)}, u32[]{:S(2)}) collective-permute-start(bf16[384,128]{1,0:T(8,128)(2,1)S(1)} %get-tuple-element.57), channel_id=1, source_target_pairs={{0,31},{1,30},{2,1},{3,0},{4,3},{5,2},{6,5},{7,4},{8,7},{9,6},{10,... | collective-permute-start | bytes 294920 | tf_op jit(solution)/shard_map/ppermute | solution.py:22
  125.6 7.6 %collective-permute-start.17 = (bf16[384,128]{1,0:T(8,128)(2,1)S(1)}, bf16[384,128]{1,0:T(8,128)(2,1)S(1)}, u32[]{:S(2)}, u32[]{:S(2)}) collective-permute-start(bf16[384,128]{1,0:T(8,128)(2,1)S(1)} %get-tuple-element.58), channel_id=1, source_target_pairs={{0,3},{1,2},{2,5},{3,4},{4,7},{5,6},{6,9},{7,8},{8,11},{9,10},{10,... | collective-permute-start | bytes 294920 | tf_op jit(solution)/shard_map/ppermute | solution.py:22
  125.6 7.6 %collective-permute-start.15 = (bf16[1024,128]{1,0:T(8,128)(2,1)S(1)}, bf16[1024,128]{1,0:T(8,128)(2,1)S(1)}, u32[]{:S(2)}, u32[]{:S(2)}) collective-permute-start(bf16[1024,128]{1,0:T(8,128)(2,1)S(1)} %fusion.73), channel_id=1, source_target_pairs={{0,1},{1,0},{2,3},{3,2},{4,5},{5,4},{6,7},{7,6},{8,9},{9,8},{10,11... | collective-permute-start | bytes 786440 | tf_op jit(solution)/shard_map/ppermute | solution.py:22
  134.4 0.8 copy-start.4
  135.2 0.8 copy-start.5
  146.1 2.6 %copy-start.22 = (f32[128]{0:T(128)}, f32[128]{0:T(128)S(1)}, u32[]{:S(2)}) copy-start(f32[128]{0:T(128)S(1)} %get-tuple-element.44) | copy-start | bytes 1540
where the time goes:
time: 149 us
  starting transfers between devices  56.6 us (38%)
  waiting for transfers between devices  25.8 us (17%)
  blocking collectives  19 us (13%)
  matrix products  16.6 us (11%)
  other arithmetic  11.9 us (8%)
  Pallas kernels  10.2 us (7%)
  local copies, waits for them, and re-layouts  7.25 us (5%)
    ppermute x20, starting transfers between devices, send(): return lax.ppermute(values, AXES, pairs)  49.3 us
    ppermute x20, waiting for transfers between devices, send(): return lax.ppermute(values, AXES, pairs)  25.8 us
    all_to_all x2, blocking collectives, sub_mean(): return jnp.sum(lax.all_to_all(values, 'sub', 0, 0), axis=0) / node_count  19 us
    dot_general x17, matrix products, matmul(): return jnp.dot(left, right, preferred_element_type=jnp.float32)  16.6 us
    pallas_call x2, Pallas kernels, coupling_rows(): pl.pallas_call(coupling_kernel, grid=(count,), in_specs=[pl.BlockSpec((sl...  7.79 us
    all_to_all x1, starting transfers between devices, sub_mean(): return jnp.sum(lax.all_to_all(values, 'sub', 0, 0), axis=0) / node_count  7.39 us
    unnamed x54, local copies, waits for them, and re-layouts  5.69 us
  transfers between devices with their start and end apart: 21, of which 7 were waited for; matrix products, arithmetic and copies ran while one was open for 7% of the time, Pallas kernels for 5%

commit v1 on v0

--- a/solution.py
+++ b/solution.py
@@ -79,16 +79,16 @@
 
 
 def operate_kernel(closing, *refs):
-    part, swapped, same_up, cross_up, same_down, cross_down, diagonal, shadow = refs[:8]
+    part, swapped, same_near, cross_near, same_far, cross_far, diagonal, shadow = refs[:8]
     refs = refs[8:]
     if closing:
         middle, refs = refs[0], refs[1:]
     *weights, hat_ref, image_ref, sums_ref, extended = refs
-    own, border = part.shape[0], same_up.shape[0]
+    own, border = part.shape[0], same_near.shape[0]
     hat = part[...] + swapped[...].astype(jnp.float32)
     hat_ref[...] = hat
     extended[:own] = hat.astype(jnp.bfloat16)
-    for at, (same, cross) in enumerate(((same_up, cross_up), (same_down, cross_down))):
+    for at, (same, cross) in enumerate(((same_near, cross_near), (same_far, cross_far))):
         ghost = same[...].astype(jnp.float32) + cross[...].astype(jnp.float32)
         extended[own + at * border : own + (at + 1) * border] = ghost.astype(jnp.bfloat16)
     begin = 0
@@ -132,6 +132,14 @@
         compiler_params=pltpu.CompilerParams(vmem_limit_bytes=24 << 20),
         name="operate_closing" if closing else "operate_second",
     )(*operands)
+
+
+def near(s):
+    return s ^ 1
+
+
+def far(s):
+    return s - 1 if s % 2 == 0 else s + 1
 
 
 def matmul(left, right):
@@ -177,10 +185,19 @@
     def meet(arrived, value):
         return lax.optimization_barrier((arrived, value))
 
+    even = lax.axis_index("sub") % 2 == 0
+
+    def by_parity(zero, one):
+        return jnp.where(even, zero, one)
+
     present = jnp.where(neighbours < ext, edge_weight, 0.0)
+    turned = jnp.where(neighbours < own + border, neighbours + border, neighbours - border)
+    ghost = even & (neighbours >= own) & (neighbours < ext)
+    neighbours = jnp.where(ghost, turned, neighbours)
+    near_far = by_parity(send_rows[0, ::-1], send_rows[0])
     diagonal = jnp.broadcast_to((node_shift + jnp.sum(present, axis=0))[:, None], (own, cols))
     rows = lax.broadcasted_iota(jnp.int32, (1, own), 1)
-    select = (send_rows[0].reshape(2 * border, 1) == rows).astype(jnp.bfloat16)
+    select = (near_far.reshape(2 * border, 1) == rows).astype(jnp.bfloat16)
 
     def by_panel(zero, one):
         return jnp.where(first, zero, one)
@@ -193,24 +210,21 @@
         head, rest = rounded[:half], jnp.concatenate([rounded[half:], ghosts], axis=0)
         mine, payload = by_panel(head, rest), by_panel(rest, head)
         build = chosen_upper is None
-        if build:
-            payload, chosen = lax.optimization_barrier((payload, select))
-            chosen_upper = matmul(chosen, upper).astype(jnp.bfloat16)
         received = send(payload, lambda s, p: (s, 1 - p))
         early = matmul(lower[half:], mine).astype(jnp.bfloat16)
         passed_others = send(early, lambda s, p: (s, 1) if p == 0 else None)
-        if build:
-            received, chosen_upper = meet(received, chosen_upper)
         pair = jnp.concatenate([received, mine], axis=1)
-        up, down = pair[tail + border :], pair[tail : tail + border]
-        from_lower = send(up, lambda s, p: (s + 1, 1) if p == 1 else None)
-        from_upper = send(down, lambda s, p: (s - 1, 1) if p == 1 else None)
         late = matmul(lower[half:], received).astype(jnp.bfloat16)
         if build:
-            late = next_coupling(late)
+            late, chosen = lax.optimization_barrier((next_coupling(late), select))
+            chosen_upper = matmul(chosen, upper).astype(jnp.bfloat16)
         passed_mine = send(late, lambda s, p: (s, 1) if p == 0 else None)
+        from_far = send(pair[tail + border :], lambda s, p: (far(s), 1) if p == 1 else None)
+        from_near = send(pair[tail : tail + border], lambda s, p: (near(s), 1) if p == 1 else None)
         if build:
             passed_mine, coupling[-1] = meet(passed_mine, coupling[-1])
+            passed_mine, chosen_upper = meet(passed_mine, chosen_upper)
+        from_lower, from_upper = by_parity(from_far, from_near), by_parity(from_near, from_far)
         rhs = by_panel(pair, jnp.concatenate([pair[:tail], from_lower, from_upper], axis=0))
         passed = jnp.concatenate([passed_others, passed_mine], axis=1).astype(jnp.float32)
         inner = (matmul(diagonal_rows, rhs) + passed).astype(jnp.bfloat16)
@@ -219,13 +233,13 @@
         other_part = matmul(upper, others).astype(jnp.bfloat16)
         other_edge = matmul(chosen_upper, others).astype(jnp.bfloat16)
         swapped = send(other_part, lambda s, p: (s, 1 - p))
-        cross_up = send(other_edge[border:], lambda s, p: (s + 1, 1 - p))
-        cross_down = send(other_edge[:border], lambda s, p: (s - 1, 1 - p))
+        cross_far = send(other_edge[border:], lambda s, p: (far(s), 1 - p))
         edge = matmul(chosen_upper, mine).astype(jnp.bfloat16)
         part = matmul(upper, mine)
-        same_up = send(edge[border:], lambda s, p: (s + 1, p))
-        same_down = send(edge[:border], lambda s, p: (s - 1, p))
-        return (part, swapped, same_up, cross_up, same_down, cross_down), chosen_upper
+        same_far = send(edge[border:], lambda s, p: (far(s), p))
+        cross_near = send(other_edge[:border], lambda s, p: (near(s), 1 - p))
+        same_near = send(edge[:border], lambda s, p: (near(s), p))
+        return (part, swapped, same_near, cross_near, same_far, cross_far), chosen_upper
 
     copies = lax.axis_size("sub")
 
@@ -254,7 +268,7 @@
 
 
 def solution(mesh):
-    assert mesh.shape["panel"] == 2
+    assert mesh.shape["panel"] == 2 and mesh.shape["sub"] % 2 == 0
     placed = (
         P("sub", "panel"),
         P("sub", "panel"),

time: 149 us -> 143 us (0.960)
  starting transfers between devices: 56.6 us -> 46.1 us
  matrix products: 16.6 us -> 11.5 us
  waiting for transfers between devices: 25.8 us -> 29.8 us
  other arithmetic: 11.9 us -> 14.9 us
  blocking collectives: 19 us -> 21.6 us
    ppermute x20, starting transfers between devices: 49.3 us -> 38.7 us  [send(): return lax.ppermute(values, AXES, pairs)]
    dot_general x17, matrix products: 16.6 us -> 11.5 us  [matmul(): return jnp.dot(left, right, preferred_element_type=jnp.float32)]
    ppermute x20, waiting for transfers between devices: 25.8 us -> 29.8 us  [send(): return lax.ppermute(values, AXES, pairs)]
    all_to_all x2, blocking collectives: 19 us -> 21.6 us  [sub_mean(): return jnp.sum(lax.all_to_all(values, 'sub', 0, 0), axis=0) / node_count]
    unnamed x54 -> x44, local copies, waits for them, and re-layouts: 5.69 us -> 4.74 us
  transfers between devices with their start and end apart: 21 -> 21, of which waited for: 7 -> 9; matrix products, arithmetic and copies ran while one was open for 7% -> 8% of each run, Pallas kernels for 5% -> 5%
where the time goes in v1:
time: 143 us; the launch traced here: 142 us
  starting transfers between devices  46.1 us (32%)
  waiting for transfers between devices  29.8 us (21%)
  blocking collectives  21.6 us (15%)
  other arithmetic  14.9 us (10%)
  matrix products  11.5 us (8%)
  Pallas kernels  10.2 us (7%)
  local copies, waits for them, and re-layouts  7.02 us (5%)
    ppermute x20, starting transfers between devices, send(): return lax.ppermute(values, AXES, pairs)  38.7 us
    ppermute x20, waiting for transfers between devices, send(): return lax.ppermute(values, AXES, pairs)  29.8 us
    all_to_all x2, blocking collectives, sub_mean(): return jnp.sum(lax.all_to_all(values, 'sub', 0, 0), axis=0) / node_count  21.6 us
    dot_general x17, matrix products, matmul(): return jnp.dot(left, right, preferred_element_type=jnp.float32)  11.5 us
    pallas_call x2, Pallas kernels, coupling_rows(): pl.pallas_call(coupling_kernel, grid=(count,), in_specs=[pl.BlockSpec((sl...  7.78 us
    all_to_all x1, starting transfers between devices, sub_mean(): return jnp.sum(lax.all_to_all(values, 'sub', 0, 0), axis=0) / node_count  7.39 us
    unnamed x44, local copies, waits for them, and re-layouts  4.74 us
  transfers between devices with their start and end apart: 21, of which 9 were waited for; matrix products, arithmetic and copies ran while one was open for 8% of the time, Pallas kernels for 5%

profile of v1, /device:TPU:0, one launch (start us, length us, event | category | flops | bytes accessed | tf_op | source)
XLA Modules:
  0.0 142.3 jit_solution(13406699007998891666)
XLA Ops:
  0.7 1.4 multiply_reduce_fusion.1
  2.1 0.9 select_select_fusion.neighbours_ref
  2.9 0.6 broadcast_in_dim.8
  3.5 7.4 %all-to-all-start = ((f32[16,2,128]{2,1,0:T(2,128)}), f32[16,2,128]{2,1,0:T(2,128)S(1)}, u32[]{:S(2)}, u32[]{:S(2)}) async-start(f32[16,2,128]{2,1,0:T(2,128)} %broadcast_in_dim.8), calls=%async_computation | async-start | bytes 32768 | tf_op jit(solution)/shard_map/all_to_all | solution.py:247
  10.9 1.4 rev.3
  12.4 1.5 %select_reduce_fusion = f32[1024]{0:T(1024)} fusion(f32[16,1024]{1,0:T(8,128)} %weight_ref.3, s32[16,1024]{1,0:T(8,128)} %param.24), kind=kLoop, calls=%fused_computation.122 | loop fusion | flops 48128 | bytes 135168 | tf_op jit(solution)/shard_map/reduce_sum | solution.py:198
  13.8 1.5 %fusion.1 = bf16[768,1024]{1,0:T(8,128)(2,1)} fusion(s32[768]{0:T(1024)S(1)} %select_n.96), kind=kLoop, calls=%fused_computation.2 | loop fusion | flops 1572864 | bytes 1575936 | tf_op jit(solution)/shard_map/convert_element_type | solution.py:200
  15.3 3.9 %shard_map.173.refs_8_.refs_9_ = bf16[512,1792]{1,0:T(8,128)(2,1)S(1)} custom-call(s32[16,1024]{1,0:T(8,128)S(1)} %select_select_fusion.neighbours_ref, f32[16,1024]{1,0:T(8,128)S(1)} %copy-done.7), custom_call_target="tpu_custom_call" | custom-call | flops 734003200 | bytes 1835008 | tf_op jit(solution)/shard_map/pallas_call | solution.py:62
  19.2 1.3 add.42
  20.5 0.6 reduce_sum.56
  21.1 0.7 broadcast_multiply_fusion.2
  21.8 0.7 fusion.128
  22.5 0.9 add_convert_fusion
  23.4 0.7 fusion.68
  24.2 1.6 %collective-permute-start = (bf16[896,128]{1,0:T(8,128)(2,1)S(1)}, bf16[896,128]{1,0:T(8,128)(2,1)S(1)}, u32[]{:S(2)}, u32[]{:S(2)}) collective-permute-start(bf16[896,128]{1,0:T(8,128)(2,1)S(1)} %get-tuple-element.51), channel_id=1, source_target_pairs={{0,1},{1,0},{2,3},{3,2},{4,5},{5,4},{6,7},{7,6},{8,9},{9,8},{10,11... | collective-permute-start | bytes 688136 | tf_op jit(solution)/shard_map/ppermute | solution.py:22
  25.8 0.6 fusion.76
  26.4 2.7 %collective-permute-start.3 = (bf16[896,128]{1,0:T(8,128)(2,1)S(1)}, bf16[896,128]{1,0:T(8,128)(2,1)S(1)}, u32[]{:S(2)}, u32[]{:S(2)}) collective-permute-start(bf16[896,128]{1,0:T(8,128)(2,1)S(1)} %fusion.76), channel_id=1, source_target_pairs={{0,1},{2,3},{4,5},{6,7},{8,9},{10,11},{12,13},{14,15},{16,17},{18,... | collective-permute-start | bytes 688136 | tf_op jit(solution)/shard_map/ppermute | solution.py:22
  29.1 3.5 %collective-permute-done = bf16[896,128]{1,0:T(8,128)(2,1)S(1)} collective-permute-done((bf16[896,128]{1,0:T(8,128)(2,1)S(1)}, bf16[896,128]{1,0:T(8,128)(2,1)S(1)}, u32[]{:S(2)}, u32[]{:S(2)}) %collective-permute-start) | collective-permute-done | bytes 229408 | tf_op jit(solution)/shard_map/ppermute | solution.py:22
  32.7 0.6 fusion.79
  33.2 3.4 %collective-permute-start.4 = (bf16[896,128]{1,0:T(8,128)(2,1)S(1)}, bf16[896,128]{1,0:T(8,128)(2,1)S(1)}, u32[]{:S(2)}, u32[]{:S(2)}) collective-permute-start(bf16[896,128]{1,0:T(8,128)(2,1)S(1)} %fusion.79), channel_id=1, source_target_pairs={{0,1},{2,3},{4,5},{6,7},{8,9},{10,11},{12,13},{14,15},{16,17},{18,... | collective-permute-start | bytes 688136 | tf_op jit(solution)/shard_map/ppermute | solution.py:22
  36.7 0.7 collective-permute-start.1
  37.4 0.7 collective-permute-start.2
  38.1 1.8 %fusion.13 = bf16[768,896]{1,0:T(8,128)(2,1)S(1)} fusion(bf16[768,1024]{1,0:T(8,128)(2,1)S(1)} %copy-done.11, bf16[1,1792,896]{2,1,0:T(8,128)(2,1)S(1)} %copy-done.20), kind=kOutput, calls=%fused_computation.14 | convolution fusion | flops 1409974272 | bytes 4784128 | tf_op jit(solution)/shard_map/dot_general | solution.py:146
  39.9 3.9 %shard_map.174.refs_9_.refs_10_ = bf16[512,1792]{1,0:T(8,128)(2,1)S(1)} custom-call(s32[16,1024]{1,0:T(8,128)S(1)} %select_select_fusion.neighbours_ref, f32[16,1024]{1,0:T(8,128)S(1)} %copy-done.7), custom_call_target="tpu_custom_call" | custom-call | flops 734003200 | bytes 1835008 | tf_op jit(solution)/shard_map/pallas_call | solution.py:62
  44.0 0.7 fusion.41
  45.7 0.6 fusion.70
  46.4 3.9 %collective-permute-start.8 = (bf16[384,128]{1,0:T(8,128)(2,1)S(1)}, bf16[384,128]{1,0:T(8,128)(2,1)S(1)}, u32[]{:S(2)}, u32[]{:S(2)}) collective-permute-start(bf16[384,128]{1,0:T(8,128)(2,1)S(1)} %get-tuple-element.67), channel_id=1, source_target_pairs={{0,30},{1,31},{2,4},{3,5},{4,2},{5,3},{6,8},{7,9},{8,6},{9,7},{10,... | collective-permute-start | bytes 294920 | tf_op jit(solution)/shard_map/ppermute | solution.py:22
  50.3 6.1 %collective-permute-start.9 = (bf16[384,128]{1,0:T(8,128)(2,1)S(1)}, bf16[384,128]{1,0:T(8,128)(2,1)S(1)}, u32[]{:S(2)}, u32[]{:S(2)}) collective-permute-start(bf16[384,128]{1,0:T(8,128)(2,1)S(1)} %get-tuple-element.65), channel_id=1, source_target_pairs={{0,31},{1,30},{2,5},{3,4},{4,3},{5,2},{6,9},{7,8},{8,7},{9,6},{10,... | collective-permute-start | bytes 294920 | tf_op jit(solution)/shard_map/ppermute | solution.py:22
  56.4 0.6 fusion.47.refs_0_
  57.1 2.7 %collective-permute-done.9.refs_5_ = bf16[384,128]{1,0:T(8,128)(2,1)S(1)} collective-permute-done((bf16[384,128]{1,0:T(8,128)(2,1)S(1)}, bf16[384,128]{1,0:T(8,128)(2,1)S(1)}, u32[]{:S(2)}, u32[]{:S(2)}) %collective-permute-start.9) | collective-permute-done | bytes 98336 | tf_op jit(solution)/shard_map/ppermute | solution.py:22
  59.8 1.8 %collective-permute-done.7.refs_3_ = bf16[384,128]{1,0:T(8,128)(2,1)S(1)} collective-permute-done((bf16[384,128]{1,0:T(8,128)(2,1)S(1)}, bf16[384,128]{1,0:T(8,128)(2,1)S(1)}, u32[]{:S(2)}, u32[]{:S(2)}) %collective-permute-start.7) | collective-permute-done | bytes 98336 | tf_op jit(solution)/shard_map/ppermute | solution.py:22
  61.6 4.0 %collective-permute-done.5.refs_1_ = bf16[1024,128]{1,0:T(8,128)(2,1)S(1)} collective-permute-done((bf16[1024,128]{1,0:T(8,128)(2,1)S(1)}, bf16[1024,128]{1,0:T(8,128)(2,1)S(1)}, u32[]{:S(2)}, u32[]{:S(2)}) %collective-permute-start.5) | collective-permute-done | bytes 262176 | tf_op jit(solution)/shard_map/ppermute | solution.py:22
  65.8 1.2 operate_second.1
  67.0 0.8 copy-done.3
  67.8 0.8 copy-done.6
  68.6 10.1 %all_to_all.15 = f32[16,2,128]{2,1,0:T(2,128)S(1)} all-to-all(f32[16,2,128]{2,1,0:T(2,128)S(1)} %get-tuple-element.35), channel_id=1, replica_groups=mesh['sub'=16,'panel'=2] {'sub'}, dimensions={0} | all-to-all | bytes 32768 | tf_op jit(solution)/shard_map/all_to_all | solution.py:247
  78.8 0.5 bitcast_divide_fusion
  79.3 1.4 %fusion.135 = (bf16[1024,128]{1,0:T(8,128)(2,1)S(1)}, f32[1024,128]{1,0:T(8,128)S(1)}) fusion(f32[1024,128]{1,0:T(8,128)} %param.15, f32[1024,128]{1,0:T(8,128)} %copy-done.6, f32[128]{0:T(128)S(1)} %divide_bitcast_fusion), kind=kLoop, calls=%fused_computation.143 | loop fusion | flops 393216 | bytes 1835520 | tf_op jit(solution)/shard_map/convert_element_type | solution.py:208
  80.7 0.7 fusion.69
  81.5 2.3 %collective-permute-start.10 = (bf16[896,128]{1,0:T(8,128)(2,1)S(1)}, bf16[896,128]{1,0:T(8,128)(2,1)S(1)}, u32[]{:S(2)}, u32[]{:S(2)}) collective-permute-start(bf16[896,128]{1,0:T(8,128)(2,1)S(1)} %get-tuple-element.49), channel_id=1, source_target_pairs={{0,1},{1,0},{2,3},{3,2},{4,5},{5,4},{6,7},{7,6},{8,9},{9,8},{10,11... | collective-permute-start | bytes 688136 | tf_op jit(solution)/shard_map/ppermute | solution.py:22
  83.8 0.6 fusion.82
  84.4 1.9 %collective-permute-start.13 = (bf16[896,128]{1,0:T(8,128)(2,1)S(1)}, bf16[896,128]{1,0:T(8,128)(2,1)S(1)}, u32[]{:S(2)}, u32[]{:S(2)}) collective-permute-start(bf16[896,128]{1,0:T(8,128)(2,1)S(1)} %fusion.82), channel_id=1, source_target_pairs={{0,1},{2,3},{4,5},{6,7},{8,9},{10,11},{12,13},{14,15},{16,17},{18,... | collective-permute-start | bytes 688136 | tf_op jit(solution)/shard_map/ppermute | solution.py:22
  86.4 3.5 %collective-permute-done.10 = bf16[896,128]{1,0:T(8,128)(2,1)S(1)} collective-permute-done((bf16[896,128]{1,0:T(8,128)(2,1)S(1)}, bf16[896,128]{1,0:T(8,128)(2,1)S(1)}, u32[]{:S(2)}, u32[]{:S(2)}) %collective-permute-start.10) | collective-permute-done | bytes 229408 | tf_op jit(solution)/shard_map/ppermute | solution.py:22
  89.9 0.7 collective-permute-start.11
  90.5 0.9 collective-permute-start.12
  91.4 0.6 fusion.85
  92.0 7.4 %collective-permute-start.14 = (bf16[896,128]{1,0:T(8,128)(2,1)S(1)}, bf16[896,128]{1,0:T(8,128)(2,1)S(1)}, u32[]{:S(2)}, u32[]{:S(2)}) collective-permute-start(bf16[896,128]{1,0:T(8,128)(2,1)S(1)} %fusion.85), channel_id=1, source_target_pairs={{0,1},{2,3},{4,5},{6,7},{8,9},{10,11},{12,13},{14,15},{16,17},{18,... | collective-permute-start | bytes 688136 | tf_op jit(solution)/shard_map/ppermute | solution.py:22
  99.5 4.9 %collective-permute-done.14 = bf16[896,128]{1,0:T(8,128)(2,1)S(1)} collective-permute-done((bf16[896,128]{1,0:T(8,128)(2,1)S(1)}, bf16[896,128]{1,0:T(8,128)(2,1)S(1)}, u32[]{:S(2)}, u32[]{:S(2)}) %collective-permute-start.14) | collective-permute-done | bytes 229408 | tf_op jit(solution)/shard_map/ppermute | solution.py:22
  104.5 0.7 fusion.38
  105.1 0.7 copy-done.9
  106.9 0.8 copy-done.21
  107.7 0.6 fusion.73
  108.4 3.1 %collective-permute-start.18 = (bf16[384,128]{1,0:T(8,128)(2,1)S(1)}, bf16[384,128]{1,0:T(8,128)(2,1)S(1)}, u32[]{:S(2)}, u32[]{:S(2)}) collective-permute-start(bf16[384,128]{1,0:T(8,128)(2,1)S(1)} %get-tuple-element.63), channel_id=1, source_target_pairs={{0,30},{1,31},{2,4},{3,5},{4,2},{5,3},{6,8},{7,9},{8,6},{9,7},{10,... | collective-permute-start | bytes 294920 | tf_op jit(solution)/shard_map/ppermute | solution.py:22
  111.5 3.3 %collective-permute-start.19 = (bf16[384,128]{1,0:T(8,128)(2,1)S(1)}, bf16[384,128]{1,0:T(8,128)(2,1)S(1)}, u32[]{:S(2)}, u32[]{:S(2)}) collective-permute-start(bf16[384,128]{1,0:T(8,128)(2,1)S(1)} %get-tuple-element.61), channel_id=1, source_target_pairs={{0,31},{1,30},{2,5},{3,4},{4,3},{5,2},{6,9},{7,8},{8,7},{9,6},{10,... | collective-permute-start | bytes 294920 | tf_op jit(solution)/shard_map/ppermute | solution.py:22
  114.9 0.6 fusion.44.refs_0_
  115.5 3.8 %collective-permute-done.19.refs_5_ = bf16[384,128]{1,0:T(8,128)(2,1)S(1)} collective-permute-done((bf16[384,128]{1,0:T(8,128)(2,1)S(1)}, bf16[384,128]{1,0:T(8,128)(2,1)S(1)}, u32[]{:S(2)}, u32[]{:S(2)}) %collective-permute-start.19) | collective-permute-done | bytes 98336 | tf_op jit(solution)/shard_map/ppermute | solution.py:22
  119.3 2.0 %collective-permute-done.17.refs_3_ = bf16[384,128]{1,0:T(8,128)(2,1)S(1)} collective-permute-done((bf16[384,128]{1,0:T(8,128)(2,1)S(1)}, bf16[384,128]{1,0:T(8,128)(2,1)S(1)}, u32[]{:S(2)}, u32[]{:S(2)}) %collective-permute-start.17) | collective-permute-done | bytes 98336 | tf_op jit(solution)/shard_map/ppermute | solution.py:22
  121.3 3.6 %collective-permute-done.15.refs_1_ = bf16[1024,128]{1,0:T(8,128)(2,1)S(1)} collective-permute-done((bf16[1024,128]{1,0:T(8,128)(2,1)S(1)}, bf16[1024,128]{1,0:T(8,128)(2,1)S(1)}, u32[]{:S(2)}, u32[]{:S(2)}) %collective-permute-start.15) | collective-permute-done | bytes 262176 | tf_op jit(solution)/shard_map/ppermute | solution.py:22
  124.9 1.2 operate_closing.1
  126.1 0.8 copy-done.4
  126.9 0.8 copy-done.5
  127.7 11.4 %all_to_all.16 = f32[16,4,128]{2,1,0:T(4,128)S(1)} all-to-all(f32[16,4,128]{2,1,0:T(4,128)S(1)} %get-tuple-element.38), channel_id=1, replica_groups=mesh['sub'=16,'panel'=2] {'sub'}, dimensions={0} | all-to-all | bytes 65536 | tf_op jit(solution)/shard_map/all_to_all | solution.py:247
  139.2 0.5 fusion.127
  139.7 2.6 %multiply_subtract_fusion = (f32[1024,128]{1,0:T(8,128)}, f32[1024,128]{1,0:T(8,128)}) fusion(f32[1024,128]{1,0:T(8,128)S(1)} %get-tuple-element.48.refs_8_, f32[1024,128]{1,0:T(8,128)} %copy-done.5, f32[128]{0:T(128)S(1)} %get-tuple-element.44, f32[1024,128]{1,0:T(8,128)} %copy-done.4, f32[1024,128]{1,0:T(8,128)} %param.14, f32[1024,128]{1,0:T(8,128)} %copy-done.3, ...), kind=kLoop, calls=%fused_computation.78 | loop fusion | flops 786432 | bytes 3671040 | tf_op jit(solution)/shard_map/sub | solution.py:265
  (83 shorter events, 2.9 us)
Async XLA Ops:
  0.6 14.7 %copy-start.7 = (f32[16,1024]{1,0:T(8,128)S(1)}, f32[16,1024]{1,0:T(8,128)}, u32[]{:S(2)}) copy-start(f32[16,1024]{1,0:T(8,128)} %weight_ref.3) | copy-start | bytes 196612
  3.5 17.0 %all-to-all-start = ((f32[16,2,128]{2,1,0:T(2,128)}), f32[16,2,128]{2,1,0:T(2,128)S(1)}, u32[]{:S(2)}, u32[]{:S(2)}) async-start(f32[16,2,128]{2,1,0:T(2,128)} %broadcast_in_dim.8), calls=%async_computation | async-start | bytes 32768 | tf_op jit(solution)/shard_map/all_to_all | solution.py:247
  12.4 1.5 %copy-start.15 = (s32[768]{0:T(1024)}, s32[768]{0:T(1024)S(1)}, u32[]{:S(2)}) copy-start(s32[768]{0:T(1024)S(1)} %select_n.96) | copy-start | bytes 9220
  13.8 8.6 %copy-start.10 = (f32[1024,128]{1,0:T(8,128)S(1)}, f32[1024,128]{1,0:T(8,128)}, u32[]{:S(2)}) copy-start(f32[1024,128]{1,0:T(8,128)} %param.15) | copy-start | bytes 1572868
  13.8 8.7 %copy-start.12 = (f32[1024,128]{1,0:T(8,128)S(1)}, f32[1024,128]{1,0:T(8,128)}, u32[]{:S(2)}) copy-start(f32[1024,128]{1,0:T(8,128)} %param.17) | copy-start | bytes 1572868
  13.8 8.7 %copy-start.13 = (f32[1024,128]{1,0:T(8,128)S(1)}, f32[1024,128]{1,0:T(8,128)}, u32[]{:S(2)}) copy-start(f32[1024,128]{1,0:T(8,128)} %param.18) | copy-start | bytes 1572868
  21.1 2.3 %copy-start.16 = (s32[768]{0:T(1024)S(1)}, s32[768]{0:T(1024)}, u32[]{:S(2)}) copy-start(s32[768]{0:T(1024)} %copy-done.15) | copy-start | bytes 9220
  22.5 3.3 %copy-start.18 = (bf16[1,1792,896]{2,1,0:T(8,128)(2,1)S(1)}, bf16[1,1792,896]{2,1,0:T(8,128)(2,1)}, u32[]{:S(2)}) copy-start(bf16[1,1792,896]{2,1,0:T(8,128)(2,1)} %param.22) | copy-start | bytes 9633796
  24.2 8.4 %collective-permute-start = (bf16[896,128]{1,0:T(8,128)(2,1)S(1)}, bf16[896,128]{1,0:T(8,128)(2,1)S(1)}, u32[]{:S(2)}, u32[]{:S(2)}) collective-permute-start(bf16[896,128]{1,0:T(8,128)(2,1)S(1)} %get-tuple-element.51), channel_id=1, source_target_pairs={{0,1},{1,0},{2,3},{3,2},{4,5},{5,4},{6,7},{7,6},{8,9},{9,8},{10,11... | collective-permute-start | bytes 688136 | tf_op jit(solution)/shard_map/ppermute | solution.py:22
  25.8 12.3 %copy-start.20 = (bf16[1,1792,896]{2,1,0:T(8,128)(2,1)S(1)}, bf16[1,1792,896]{2,1,0:T(8,128)(2,1)}, u32[]{:S(2)}) copy-start(bf16[1,1792,896]{2,1,0:T(8,128)(2,1)} %param.23) | copy-start | bytes 9633796
  26.4 11.7 %copy-start.11 = (bf16[768,1024]{1,0:T(8,128)(2,1)S(1)}, bf16[768,1024]{1,0:T(8,128)(2,1)}, u32[]{:S(2)}) copy-start(bf16[768,1024]{1,0:T(8,128)(2,1)} %fusion.1) | copy-start | bytes 4718596
  26.4 17.5 %collective-permute-start.3 = (bf16[896,128]{1,0:T(8,128)(2,1)S(1)}, bf16[896,128]{1,0:T(8,128)(2,1)S(1)}, u32[]{:S(2)}, u32[]{:S(2)}) collective-permute-start(bf16[896,128]{1,0:T(8,128)(2,1)S(1)} %fusion.76), channel_id=1, source_target_pairs={{0,1},{2,3},{4,5},{6,7},{8,9},{10,11},{12,13},{14,15},{16,17},{18,... | collective-permute-start | bytes 688136 | tf_op jit(solution)/shard_map/ppermute | solution.py:22
  33.2 10.7 %collective-permute-start.4 = (bf16[896,128]{1,0:T(8,128)(2,1)S(1)}, bf16[896,128]{1,0:T(8,128)(2,1)S(1)}, u32[]{:S(2)}, u32[]{:S(2)}) collective-permute-start(bf16[896,128]{1,0:T(8,128)(2,1)S(1)} %fusion.79), channel_id=1, source_target_pairs={{0,1},{2,3},{4,5},{6,7},{8,9},{10,11},{12,13},{14,15},{16,17},{18,... | collective-permute-start | bytes 688136 | tf_op jit(solution)/shard_map/ppermute | solution.py:22
  36.7 7.1 %collective-permute-start.1 = (bf16[384,256]{1,0:T(8,128)(2,1)S(1)}, bf16[384,256]{1,0:T(8,128)(2,1)S(1)}, u32[]{:S(2)}, u32[]{:S(2)}) collective-permute-start(bf16[384,256]{1,0:T(8,128)(2,1)S(1)} %get-tuple-element.55), channel_id=1, source_target_pairs={{1,31},{3,5},{5,3},{7,9},{9,7},{11,13},{13,11},{15,17},{17,15},{19... | collective-permute-start | bytes 589832 | tf_op jit(solution)/shard_map/ppermute | solution.py:22
  37.4 6.5 %collective-permute-start.2 = (bf16[384,256]{1,0:T(8,128)(2,1)S(1)}, bf16[384,256]{1,0:T(8,128)(2,1)S(1)}, u32[]{:S(2)}, u32[]{:S(2)}) collective-permute-start(bf16[384,256]{1,0:T(8,128)(2,1)S(1)} %get-tuple-element.56), channel_id=1, source_target_pairs={{1,3},{3,1},{5,7},{7,5},{9,11},{11,9},{13,15},{15,13},{17,19},{19,... | collective-permute-start | bytes 589832 | tf_op jit(solution)/shard_map/ppermute | solution.py:22
  39.9 5.2 %copy-start.8 = (bf16[768,896]{1,0:T(8,128)(2,1)}, bf16[768,896]{1,0:T(8,128)(2,1)S(1)}, u32[]{:S(2)}) copy-start(bf16[768,896]{1,0:T(8,128)(2,1)S(1)} %fusion.13) | copy-start | bytes 4128772
  43.9 21.9 %copy-start = (bf16[512,1792]{1,0:T(8,128)(2,1)}, bf16[512,1792]{1,0:T(8,128)(2,1)S(1)}, u32[]{:S(2)}) copy-start(bf16[512,1792]{1,0:T(8,128)(2,1)S(1)} %shard_map.174.refs_9_.refs_10_) | copy-start | bytes 5505028
  46.4 19.2 %copy-start.14 = (f32[1024]{0:T(1024)S(1)}, f32[1024]{0:T(1024)}, u32[]{:S(2)}) copy-start(f32[1024]{0:T(1024)} %add.42) | copy-start | bytes 12292
  46.4 10.7 %collective-permute-start.8 = (bf16[384,128]{1,0:T(8,128)(2,1)S(1)}, bf16[384,128]{1,0:T(8,128)(2,1)S(1)}, u32[]{:S(2)}, u32[]{:S(2)}) collective-permute-start(bf16[384,128]{1,0:T(8,128)(2,1)S(1)} %get-tuple-element.67), channel_id=1, source_target_pairs={{0,30},{1,31},{2,4},{3,5},{4,2},{5,3},{6,8},{7,9},{8,6},{9,7},{10,... | collective-permute-start | bytes 294920 | tf_op jit(solution)/shard_map/ppermute | solution.py:22
  50.3 6.8 %collective-permute-start.6 = (bf16[384,128]{1,0:T(8,128)(2,1)S(1)}, bf16[384,128]{1,0:T(8,128)(2,1)S(1)}, u32[]{:S(2)}, u32[]{:S(2)}) collective-permute-start(bf16[384,128]{1,0:T(8,128)(2,1)S(1)} %get-tuple-element.68), channel_id=1, source_target_pairs={{0,2},{1,3},{2,0},{3,1},{4,6},{5,7},{6,4},{7,5},{8,10},{9,11},{10,... | collective-permute-start | bytes 294920 | tf_op jit(solution)/shard_map/ppermute | solution.py:22
  50.3 15.5 %copy-start.2 = (f32[1024,128]{1,0:T(8,128)S(1)}, f32[1024,128]{1,0:T(8,128)}, u32[]{:S(2)}) copy-start(f32[1024,128]{1,0:T(8,128)} %refs_7_.3) | copy-start | bytes 1572868
  50.3 9.5 %collective-permute-start.9 = (bf16[384,128]{1,0:T(8,128)(2,1)S(1)}, bf16[384,128]{1,0:T(8,128)(2,1)S(1)}, u32[]{:S(2)}, u32[]{:S(2)}) collective-permute-start(bf16[384,128]{1,0:T(8,128)(2,1)S(1)} %get-tuple-element.65), channel_id=1, source_target_pairs={{0,31},{1,30},{2,5},{3,4},{4,3},{5,2},{6,9},{7,8},{8,7},{9,6},{10,... | collective-permute-start | bytes 294920 | tf_op jit(solution)/shard_map/ppermute | solution.py:22
  56.4 5.2 %collective-permute-start.7 = (bf16[384,128]{1,0:T(8,128)(2,1)S(1)}, bf16[384,128]{1,0:T(8,128)(2,1)S(1)}, u32[]{:S(2)}, u32[]{:S(2)}) collective-permute-start(bf16[384,128]{1,0:T(8,128)(2,1)S(1)} %get-tuple-element.66), channel_id=1, source_target_pairs={{0,3},{1,2},{2,1},{3,0},{4,7},{5,6},{6,5},{7,4},{8,11},{9,10},{10,... | collective-permute-start | bytes 294920 | tf_op jit(solution)/shard_map/ppermute | solution.py:22
  56.4 9.2 %collective-permute-start.5 = (bf16[1024,128]{1,0:T(8,128)(2,1)S(1)}, bf16[1024,128]{1,0:T(8,128)(2,1)S(1)}, u32[]{:S(2)}, u32[]{:S(2)}) collective-permute-start(bf16[1024,128]{1,0:T(8,128)(2,1)S(1)} %fusion.70), channel_id=1, source_target_pairs={{0,1},{1,0},{2,3},{3,2},{4,5},{5,4},{6,7},{7,6},{8,9},{9,8},{10,11... | collective-permute-start | bytes 786440 | tf_op jit(solution)/shard_map/ppermute | solution.py:22
  67.0 0.8 copy-start.3
  67.8 0.8 copy-start.6
  79.3 4.5 %copy-start.19 = (bf16[1,1792,896]{2,1,0:T(8,128)(2,1)S(1)}, bf16[1,1792,896]{2,1,0:T(8,128)(2,1)}, u32[]{:S(2)}) copy-start(bf16[1,1792,896]{2,1,0:T(8,128)(2,1)} %param.22) | copy-start | bytes 9633796
  81.5 8.3 %collective-permute-start.10 = (bf16[896,128]{1,0:T(8,128)(2,1)S(1)}, bf16[896,128]{1,0:T(8,128)(2,1)S(1)}, u32[]{:S(2)}, u32[]{:S(2)}) collective-permute-start(bf16[896,128]{1,0:T(8,128)(2,1)S(1)} %get-tuple-element.49), channel_id=1, source_target_pairs={{0,1},{1,0},{2,3},{3,2},{4,5},{5,4},{6,7},{7,6},{8,9},{9,8},{10,11... | collective-permute-start | bytes 688136 | tf_op jit(solution)/shard_map/ppermute | solution.py:22
  84.4 15.1 %collective-permute-start.13 = (bf16[896,128]{1,0:T(8,128)(2,1)S(1)}, bf16[896,128]{1,0:T(8,128)(2,1)S(1)}, u32[]{:S(2)}, u32[]{:S(2)}) collective-permute-start(bf16[896,128]{1,0:T(8,128)(2,1)S(1)} %fusion.82), channel_id=1, source_target_pairs={{0,1},{2,3},{4,5},{6,7},{8,9},{10,11},{12,13},{14,15},{16,17},{18,... | collective-permute-start | bytes 688136 | tf_op jit(solution)/shard_map/ppermute | solution.py:22
  89.9 9.6 %collective-permute-start.11 = (bf16[384,256]{1,0:T(8,128)(2,1)S(1)}, bf16[384,256]{1,0:T(8,128)(2,1)S(1)}, u32[]{:S(2)}, u32[]{:S(2)}) collective-permute-start(bf16[384,256]{1,0:T(8,128)(2,1)S(1)} %get-tuple-element.53), channel_id=1, source_target_pairs={{1,31},{3,5},{5,3},{7,9},{9,7},{11,13},{13,11},{15,17},{17,15},{19... | collective-permute-start | bytes 589832 | tf_op jit(solution)/shard_map/ppermute | solution.py:22
  90.5 8.9 %collective-permute-start.12 = (bf16[384,256]{1,0:T(8,128)(2,1)S(1)}, bf16[384,256]{1,0:T(8,128)(2,1)S(1)}, u32[]{:S(2)}, u32[]{:S(2)}) collective-permute-start(bf16[384,256]{1,0:T(8,128)(2,1)S(1)} %get-tuple-element.54), channel_id=1, source_target_pairs={{1,3},{3,1},{5,7},{7,5},{9,11},{11,9},{13,15},{15,13},{17,19},{19,... | collective-permute-start | bytes 589832 | tf_op jit(solution)/shard_map/ppermute | solution.py:22
  92.0 12.5 %collective-permute-start.14 = (bf16[896,128]{1,0:T(8,128)(2,1)S(1)}, bf16[896,128]{1,0:T(8,128)(2,1)S(1)}, u32[]{:S(2)}, u32[]{:S(2)}) collective-permute-start(bf16[896,128]{1,0:T(8,128)(2,1)S(1)} %fusion.85), channel_id=1, source_target_pairs={{0,1},{2,3},{4,5},{6,7},{8,9},{10,11},{12,13},{14,15},{16,17},{18,... | collective-permute-start | bytes 688136 | tf_op jit(solution)/shard_map/ppermute | solution.py:22
  104.4 1.3 copy-start.9
  105.8 1.9 %copy-start.21 = (bf16[1,1792,896]{2,1,0:T(8,128)(2,1)S(1)}, bf16[1,1792,896]{2,1,0:T(8,128)(2,1)}, u32[]{:S(2)}) copy-start(bf16[1,1792,896]{2,1,0:T(8,128)(2,1)} %param.23) | copy-start | bytes 9633796
  108.4 16.5 %copy-start.1 = (bf16[512,1792]{1,0:T(8,128)(2,1)S(1)}, bf16[512,1792]{1,0:T(8,128)(2,1)}, u32[]{:S(2)}) copy-start(bf16[512,1792]{1,0:T(8,128)(2,1)} %copy-done) | copy-start | bytes 5505028
  108.4 7.1 %collective-permute-start.18 = (bf16[384,128]{1,0:T(8,128)(2,1)S(1)}, bf16[384,128]{1,0:T(8,128)(2,1)S(1)}, u32[]{:S(2)}, u32[]{:S(2)}) collective-permute-start(bf16[384,128]{1,0:T(8,128)(2,1)S(1)} %get-tuple-element.63), channel_id=1, source_target_pairs={{0,30},{1,31},{2,4},{3,5},{4,2},{5,3},{6,8},{7,9},{8,6},{9,7},{10,... | collective-permute-start | bytes 294920 | tf_op jit(solution)/shard_map/ppermute | solution.py:22
  111.5 4.0 %collective-permute-start.16 = (bf16[384,128]{1,0:T(8,128)(2,1)S(1)}, bf16[384,128]{1,0:T(8,128)(2,1)S(1)}, u32[]{:S(2)}, u32[]{:S(2)}) collective-permute-start(bf16[384,128]{1,0:T(8,128)(2,1)S(1)} %get-tuple-element.64), channel_id=1, source_target_pairs={{0,2},{1,3},{2,0},{3,1},{4,6},{5,7},{6,4},{7,5},{8,10},{9,11},{10,... | collective-permute-start | bytes 294920 | tf_op jit(solution)/shard_map/ppermute | solution.py:22
  111.5 7.8 %collective-permute-start.19 = (bf16[384,128]{1,0:T(8,128)(2,1)S(1)}, bf16[384,128]{1,0:T(8,128)(2,1)S(1)}, u32[]{:S(2)}, u32[]{:S(2)}) collective-permute-start(bf16[384,128]{1,0:T(8,128)(2,1)S(1)} %get-tuple-element.61), channel_id=1, source_target_pairs={{0,31},{1,30},{2,5},{3,4},{4,3},{5,2},{6,9},{7,8},{8,7},{9,6},{10,... | collective-permute-start | bytes 294920 | tf_op jit(solution)/shard_map/ppermute | solution.py:22
  114.9 6.4 %collective-permute-start.17 = (bf16[384,128]{1,0:T(8,128)(2,1)S(1)}, bf16[384,128]{1,0:T(8,128)(2,1)S(1)}, u32[]{:S(2)}, u32[]{:S(2)}) collective-permute-start(bf16[384,128]{1,0:T(8,128)(2,1)S(1)} %get-tuple-element.62), channel_id=1, source_target_pairs={{0,3},{1,2},{2,1},{3,0},{4,7},{5,6},{6,5},{7,4},{8,11},{9,10},{10,... | collective-permute-start | bytes 294920 | tf_op jit(solution)/shard_map/ppermute | solution.py:22
  114.9 10.0 %collective-permute-start.15 = (bf16[1024,128]{1,0:T(8,128)(2,1)S(1)}, bf16[1024,128]{1,0:T(8,128)(2,1)S(1)}, u32[]{:S(2)}, u32[]{:S(2)}) collective-permute-start(bf16[1024,128]{1,0:T(8,128)(2,1)S(1)} %fusion.73), channel_id=1, source_target_pairs={{0,1},{1,0},{2,3},{3,2},{4,5},{5,4},{6,7},{7,6},{8,9},{9,8},{10,11... | collective-permute-start | bytes 786440 | tf_op jit(solution)/shard_map/ppermute | solution.py:22
  126.1 0.8 copy-start.4
  126.9 0.8 copy-start.5
  139.7 2.6 %copy-start.17 = (f32[128]{0:T(128)}, f32[128]{0:T(128)S(1)}, u32[]{:S(2)}) copy-start(f32[128]{0:T(128)S(1)} %get-tuple-element.44) | copy-start | bytes 1540

commit v2 on v1

--- a/solution.py
+++ b/solution.py
@@ -83,7 +83,7 @@
     refs = refs[8:]
     if closing:
         middle, refs = refs[0], refs[1:]
-    *weights, hat_ref, image_ref, sums_ref, extended = refs
+    *weights, hat_out, image_out, sums_ref, extended, hat_ref, image_ref, done = refs
     own, border = part.shape[0], same_near.shape[0]
     hat = part[...] + swapped[...].astype(jnp.float32)
     hat_ref[...] = hat
@@ -93,12 +93,18 @@
         extended[own + at * border : own + (at + 1) * border] = ghost.astype(jnp.bfloat16)
     begin = 0
     sums = 0.0
+    leaving = [pltpu.make_async_copy(hat_ref, hat_out, done.at[0])]
+    leaving[0].start()
     for weight in weights:
         rows = slice(begin, begin + weight.shape[0])
         begin += weight.shape[0]
         coupled = jnp.dot(weight[...], extended[...], preferred_element_type=jnp.float32)
         image = diagonal[rows] * hat_ref[rows] - coupled
         image_ref[rows] = image
+        leaving.append(
+            pltpu.make_async_copy(image_ref.at[rows], image_out.at[rows], done.at[len(leaving)])
+        )
+        leaving[-1].start()
         if closing:
             pairs = (
                 (image, middle[rows]),
@@ -110,6 +116,8 @@
             pairs = ((shadow[rows], image), (image, image))
         sums += jnp.concatenate([jnp.sum(a * b, axis=0, keepdims=True) for a, b in pairs], axis=0)
     sums_ref[...] = jnp.broadcast_to(sums[None], sums_ref.shape)
+    for copy in leaving:
+        copy.wait()
 
 
 def operate(parts, diagonal, shadow, middle, coupling, copies):
@@ -123,15 +131,68 @@
     return pl.pallas_call(
         lambda *refs: operate_kernel(closing, *refs),
         in_specs=[in_vmem] * len(operands),
-        out_specs=[in_vmem] * 3,
+        out_specs=[pl.BlockSpec(memory_space=pltpu.HBM)] * 2 + [in_vmem],
         out_shape=[vector, vector, jax.ShapeDtypeStruct((copies, count, cols), jnp.float32)],
-        scratch_shapes=[pltpu.VMEM((ext, cols), jnp.bfloat16)],
+        scratch_shapes=[
+            pltpu.VMEM((ext, cols), jnp.bfloat16),
+            pltpu.VMEM((own, cols), jnp.float32),
+            pltpu.VMEM((own, cols), jnp.float32),
+            pltpu.SemaphoreType.DMA((1 + len(coupling),)),
+        ],
         cost_estimate=pl.CostEstimate(
             flops=2 * own * ext * cols, bytes_accessed=2 * own * ext, transcendentals=0
         ),
         compiler_params=pltpu.CompilerParams(vmem_limit_bytes=24 << 20),
         name="operate_closing" if closing else "operate_second",
     )(*operands)
+
+
+def split_rows(vector, select, panel, mine_ref, payload_ref):
+    rounded = vector.astype(jnp.bfloat16)
+    half = mine_ref.shape[0]
+    tail = rounded.shape[0] - half
+    ghosts = jnp.dot(select[...], rounded, preferred_element_type=jnp.float32)
+    ghosts = ghosts.astype(jnp.bfloat16)
+
+    def put(head_ref, rest_ref):
+        head_ref[...] = rounded[:half]
+        rest_ref[:tail] = rounded[half:]
+        rest_ref[tail:] = ghosts
+
+    pl.when(panel[0] == 0)(lambda: put(mine_ref, payload_ref))
+    pl.when(panel[0] != 0)(lambda: put(payload_ref, mine_ref))
+
+
+def direction_kernel(node_count, panel, sums, past, residual, direction, old_image, select, *outs):
+    means_ref, mine_ref, payload_ref = outs
+    means = jnp.sum(sums[...], axis=0) / node_count
+    means_ref[...] = means
+    rho_prev, alpha_prev, omega_prev = past[0:1], past[1:2], past[2:3]
+    step_beta = means[0:1] / rho_prev * (alpha_prev / omega_prev)
+    vector = residual[...] + step_beta * (direction[...] - omega_prev * old_image[...])
+    split_rows(vector, select, panel, mine_ref, payload_ref)
+
+
+def middle_kernel(node_count, panel, sums, opening, residual, image, select, *outs):
+    alpha_ref, middle_ref, mine_ref, payload_ref = outs
+    means = jnp.sum(sums[...], axis=0) / node_count
+    floor = FLOOR_SHARE * jnp.sqrt(opening[1:2] * means[1:2])
+    step_alpha = opening[0:1] / jnp.maximum(means[0:1], floor)
+    alpha_ref[...] = step_alpha
+    middle = residual[...] - step_alpha * image[...]
+    middle_ref[...] = middle
+    split_rows(middle, select, panel, mine_ref, payload_ref)
+
+
+def small_call(kernel, panel, operands, outs):
+    in_vmem = pl.BlockSpec(memory_space=pltpu.VMEM)
+    return pl.pallas_call(
+        kernel,
+        in_specs=[pl.BlockSpec(memory_space=pltpu.SMEM)] + [in_vmem] * len(operands),
+        out_specs=[in_vmem] * len(outs),
+        out_shape=outs,
+        compiler_params=pltpu.CompilerParams(vmem_limit_bytes=12 << 20),
+    )(panel.reshape(1), *operands)
 
 
 def near(s):
@@ -190,49 +251,59 @@
     def by_parity(zero, one):
         return jnp.where(even, zero, one)
 
-    present = jnp.where(neighbours < ext, edge_weight, 0.0)
     turned = jnp.where(neighbours < own + border, neighbours + border, neighbours - border)
     ghost = even & (neighbours >= own) & (neighbours < ext)
     neighbours = jnp.where(ghost, turned, neighbours)
     near_far = by_parity(send_rows[0, ::-1], send_rows[0])
-    diagonal = jnp.broadcast_to((node_shift + jnp.sum(present, axis=0))[:, None], (own, cols))
     rows = lax.broadcasted_iota(jnp.int32, (1, own), 1)
-    select = (near_far.reshape(2 * border, 1) == rows).astype(jnp.bfloat16)
 
     def by_panel(zero, one):
         return jnp.where(first, zero, one)
 
     diagonal_rows = lax.dynamic_slice_in_dim(lower, panel * half, half, axis=0)
 
-    def precondition(vector, chosen_upper):
-        rounded = vector.astype(jnp.bfloat16)
-        ghosts = matmul(select, rounded).astype(jnp.bfloat16)
-        head, rest = rounded[:half], jnp.concatenate([rounded[half:], ghosts], axis=0)
-        mine, payload = by_panel(head, rest), by_panel(rest, head)
+    def precondition(mine, payload, chosen_upper):
         build = chosen_upper is None
+        if build:
+            payload = next_coupling(payload)
         received = send(payload, lambda s, p: (s, 1 - p))
         early = matmul(lower[half:], mine).astype(jnp.bfloat16)
         passed_others = send(early, lambda s, p: (s, 1) if p == 0 else None)
-        pair = jnp.concatenate([received, mine], axis=1)
+        if build:
+            received, coupling[-1] = meet(received, coupling[-1])
         late = matmul(lower[half:], received).astype(jnp.bfloat16)
         if build:
             late, chosen = lax.optimization_barrier((next_coupling(late), select))
             chosen_upper = matmul(chosen, upper).astype(jnp.bfloat16)
         passed_mine = send(late, lambda s, p: (s, 1) if p == 0 else None)
-        from_far = send(pair[tail + border :], lambda s, p: (far(s), 1) if p == 1 else None)
-        from_near = send(pair[tail : tail + border], lambda s, p: (near(s), 1) if p == 1 else None)
+        near_rows, far_rows = slice(tail, tail + border), slice(tail + border, half)
+
+        def both(part):
+            return jnp.concatenate([received[part], mine[part]], axis=1)
+
+        from_far = send(both(far_rows), lambda s, p: (far(s), 1) if p == 1 else None)
+        from_near = send(both(near_rows), lambda s, p: (near(s), 1) if p == 1 else None)
         if build:
             passed_mine, coupling[-1] = meet(passed_mine, coupling[-1])
             passed_mine, chosen_upper = meet(passed_mine, chosen_upper)
         from_lower, from_upper = by_parity(from_far, from_near), by_parity(from_near, from_far)
-        rhs = by_panel(pair, jnp.concatenate([pair[:tail], from_lower, from_upper], axis=0))
-        passed = jnp.concatenate([passed_others, passed_mine], axis=1).astype(jnp.float32)
-        inner = (matmul(diagonal_rows, rhs) + passed).astype(jnp.bfloat16)
-        inner = lax.optimization_barrier(inner)
-        others, mine = inner[:, :cols], inner[:, cols:]
+
+        def solve(kept, ghost_columns, passed):
+            ghosts = [from_lower[:, ghost_columns], from_upper[:, ghost_columns]]
+            rhs = by_panel(kept, jnp.concatenate([kept[:tail], *ghosts], axis=0))
+            product = matmul(diagonal_rows, rhs) + passed.astype(jnp.float32)
+            return lax.optimization_barrier(product.astype(jnp.bfloat16))
+
+        others = solve(received, slice(0, cols), passed_others)
+        if build:
+            others, links = lax.optimization_barrier((others, neighbours))
+            present = jnp.where(links < ext, edge_weight, 0.0)
+            scale = jnp.broadcast_to((node_shift + jnp.sum(present, axis=0))[:, None], (own, cols))
+            diagonal.append(scale)
         other_part = matmul(upper, others).astype(jnp.bfloat16)
+        swapped = send(other_part, lambda s, p: (s, 1 - p))
+        mine = solve(mine, slice(cols, 2 * cols), passed_mine)
         other_edge = matmul(chosen_upper, others).astype(jnp.bfloat16)
-        swapped = send(other_part, lambda s, p: (s, 1 - p))
         cross_far = send(other_edge[border:], lambda s, p: (far(s), 1 - p))
         edge = matmul(chosen_upper, mine).astype(jnp.bfloat16)
         part = matmul(upper, mine)
@@ -243,23 +314,35 @@
 
     copies = lax.axis_size("sub")
 
-    def sub_mean(values):
-        return jnp.sum(lax.all_to_all(values, "sub", 0, 0), axis=0) / node_count
-
+    def exchange(values):
+        return lax.all_to_all(values, "sub", 0, 0)
+
+    diagonal = []
+    vector = jax.ShapeDtypeStruct((own, cols), jnp.float32)
+    panel_rows = jax.ShapeDtypeStruct((half, cols), jnp.bfloat16)
     sums = jnp.stack([jnp.sum(shadow * residual, axis=0), jnp.sum(shadow * shadow, axis=0)])
-    sums = next_coupling(jnp.broadcast_to(sums[None], (copies, 2, cols)))
-    opening, coupling[-1] = meet(sub_mean(sums), coupling[-1])
-    rho_now, shadow_square = opening[0], opening[1]
-    step_beta = rho_now / rho_prev * (alpha_prev / omega_prev)
-    new_direction = residual + step_beta * (direction - omega_prev * old_image)
-    parts, chosen_upper = precondition(new_direction, None)
-    direction_hat, image_new, sums = operate(parts, diagonal, shadow, None, coupling, copies)
-    second = sub_mean(sums)
-    step_alpha = rho_now / jnp.maximum(second[0], FLOOR_SHARE * jnp.sqrt(shadow_square * second[1]))
-    middle = residual - step_alpha * image_new
-    parts, _ = precondition(middle, chosen_upper)
-    middle_hat, tested, sums = operate(parts, diagonal, shadow, middle, coupling, copies)
-    closing = sub_mean(sums)
+    sums = jnp.broadcast_to(sums[None], (copies, 2, cols))
+    sums, near_far = lax.optimization_barrier((sums, near_far))
+    select = (near_far.reshape(2 * border, 1) == rows).astype(jnp.bfloat16)
+    past = jnp.stack([rho_prev, alpha_prev, omega_prev])
+    opening, mine, payload = small_call(
+        lambda *refs: direction_kernel(node_count, *refs),
+        panel,
+        (exchange(sums), past, residual, direction, old_image, select),
+        [jax.ShapeDtypeStruct((2, cols), jnp.float32), panel_rows, panel_rows],
+    )
+    parts, chosen_upper = precondition(mine, payload, None)
+    direction_hat, image_new, sums = operate(parts, diagonal[0], shadow, None, coupling, copies)
+    step_alpha, middle, mine, payload = small_call(
+        lambda *refs: middle_kernel(node_count, *refs),
+        panel,
+        (exchange(sums), opening, residual, image_new, select),
+        [jax.ShapeDtypeStruct((1, cols), jnp.float32), vector, panel_rows, panel_rows],
+    )
+    step_alpha = step_alpha[0]
+    parts, _ = precondition(mine, payload, chosen_upper)
+    middle_hat, tested, sums = operate(parts, diagonal[0], shadow, middle, coupling, copies)
+    closing = jnp.sum(exchange(sums), axis=0) / node_count
     step_omega = closing[0] / (closing[1] + EPSILON)
     next_rho = closing[2] - step_omega * closing[3]
     new_residual = middle - step_omega * tested

time: 143 us -> 133 us (0.930)
  other arithmetic: 14.9 us -> 4.45 us
  Pallas kernels: 10.2 us -> 14.7 us
  local copies, waits for them, and re-layouts: 7.02 us -> 3.87 us
    ppermute x20, waiting for transfers between devices: 29.8 us -> 24.4 us  [send(): return lax.ppermute(values, AXES, pairs)]
    all_to_all x1, waiting for transfers between devices: 0.01 us -> 5.23 us  [exchange(): return lax.all_to_all(values, 'sub', 0, 0)]
    unnamed x44 -> x32, local copies, waits for them, and re-layouts: 4.74 us -> 1.31 us
    pallas_call x2, Pallas kernels: 2.42 us -> 5.07 us  [operate(): pl.pallas_call(lambda *refs: operate_kernel(closing, *refs), in_specs=[in...]
    convert_element_type x2 -> x0, other arithmetic: 2.32 us -> none  [precondition(): rounded = vector.astype(jnp.bfloat16)]
    reduce_sum x4 -> x2, other arithmetic: 2.11 us -> 0.05 us  [the longest x1 0.03 us: per_device(): closing = jnp.sum(exchange(sums), axis=0) / node_count]
    pallas_call x0 -> x2, Pallas kernels: none -> 1.78 us  [small_call(): pl.pallas_call(kernel, in_specs=[pl.BlockSpec(memory_space=pltpu.SMEM)] +...]
    sub x1, other arithmetic: 2.61 us -> 1.13 us  [per_device(): new_residual = middle - step_omega * tested]
  transfers between devices with their start and end apart: 21 -> 21, of which waited for: 9 -> 8; matrix products, arithmetic and copies ran while one was open for 8% -> 9% of each run, Pallas kernels for 5% -> 6%
where the time goes in v2:
time: 133 us; the launch traced here: 132 us
  starting transfers between devices  46.6 us (35%)
  waiting for transfers between devices  29.7 us (22%)
  blocking collectives  20.3 us (15%)
  Pallas kernels  14.7 us (11%)
  matrix products  11.2 us (8%)
  other arithmetic  4.45 us (3%)
  local copies, waits for them, and re-layouts  3.87 us (3%)
  between operations  1.36 us (1%)
    ppermute x20, starting transfers between devices, send(): return lax.ppermute(values, AXES, pairs)  39.1 us
    ppermute x20, waiting for transfers between devices, send(): return lax.ppermute(values, AXES, pairs)  24.4 us
    all_to_all x2, blocking collectives, exchange(): return lax.all_to_all(values, 'sub', 0, 0)  20.3 us
    dot_general x17, matrix products, matmul(): return jnp.dot(left, right, preferred_element_type=jnp.float32)  11.2 us
    pallas_call x2, Pallas kernels, coupling_rows(): pl.pallas_call(coupling_kernel, grid=(count,), in_specs=[pl.BlockSpec((sl...  7.81 us
    all_to_all x1, starting transfers between devices, exchange(): return lax.all_to_all(values, 'sub', 0, 0)  7.5 us
    all_to_all x1, waiting for transfers between devices, exchange(): return lax.all_to_all(values, 'sub', 0, 0)  5.23 us
    pallas_call x2, Pallas kernels, operate(): pl.pallas_call(lambda *refs: operate_kernel(closing, *refs), in_specs=[in...  5.07 us
  transfers between devices with their start and end apart: 21, of which 8 were waited for; matrix products, arithmetic and copies ran while one was open for 9% of the time, Pallas kernels for 6%

profile of v2, /device:TPU:0, one launch (start us, length us, event | category | flops | bytes accessed | tf_op | source)
XLA Modules:
  0.0 132.1 jit_solution(14231357494377736190)
XLA Ops:
  0.6 0.0 copy-start.1
  0.7 1.5 %rev.3 = s32[1,2,384]{2,1,0:T(2,128)S(1)} reverse(s32[1,2,384]{2,1,0:T(2,128)} %param.27), dimensions={1} | reverse | bytes 6144 | tf_op jit(solution)/shard_map/rev | solution.py:257
  2.2 1.3 %multiply_reduce_fusion.1 = (f32[128]{0:T(128)S(1)}, f32[128]{0:T(128)S(1)}) fusion(f32[1024,128]{1,0:T(8,128)} %refs_7_.3, f32[1024,128]{1,0:T(8,128)} %refs_3_.3), kind=kLoop, calls=%fused_computation.69 | loop fusion | flops 524032 | bytes 1049600 | tf_op jit(solution)/shard_map/reduce_sum | solution.py:323
  3.6 0.6 broadcast_in_dim.8
  4.2 7.5 %all-to-all-start = ((f32[16,2,128]{2,1,0:T(2,128)}), f32[16,2,128]{2,1,0:T(2,128)S(1)}, u32[]{:S(2)}, u32[]{:S(2)}) async-start(f32[16,2,128]{2,1,0:T(2,128)} %broadcast_in_dim.8), calls=%async_computation | async-start | bytes 32768 | tf_op jit(solution)/shard_map/all_to_all | solution.py:318
  11.7 0.9 select_select_fusion.neighbours_ref
  12.6 0.3 fusion.refs_6_.refs_5_
  13.0 5.2 %all-to-all-done.refs_1_ = f32[16,2,128]{2,1,0:T(2,128)S(1)} async-done(((f32[16,2,128]{2,1,0:T(2,128)}), f32[16,2,128]{2,1,0:T(2,128)S(1)}, u32[]{:S(2)}, u32[]{:S(2)}) %all-to-all-start) | async-done | bytes 16416 | tf_op jit(solution)/shard_map/all_to_all | solution.py:318
  18.2 0.6 shard_map.173
  18.9 0.0 copy-start.4
  18.9 1.2 copy-done.14
  20.1 0.6 fusion.81
  20.7 3.4 %collective-permute-start.4 = (bf16[896,128]{1,0:T(8,128)(2,1)S(1)}, bf16[896,128]{1,0:T(8,128)(2,1)S(1)}, u32[]{:S(2)}, u32[]{:S(2)}) collective-permute-start(bf16[896,128]{1,0:T(8,128)(2,1)S(1)} %fusion.81), channel_id=1, source_target_pairs={{0,1},{2,3},{4,5},{6,7},{8,9},{10,11},{12,13},{14,15},{16,17},{18,... | collective-permute-start | bytes 688136 | tf_op jit(solution)/shard_map/ppermute | solution.py:22
  24.2 0.1 collective-permute-start
  24.3 3.9 %shard_map.174.refs_8_.refs_9_ = bf16[512,1792]{1,0:T(8,128)(2,1)S(1)} custom-call(s32[16,1024]{1,0:T(8,128)S(1)} %select_select_fusion.neighbours_ref, f32[16,1024]{1,0:T(8,128)S(1)} %copy-done.4), custom_call_target="tpu_custom_call" | custom-call | flops 734003200 | bytes 1835008 | tf_op jit(solution)/shard_map/pallas_call | solution.py:62
  28.2 5.6 %collective-permute-done = bf16[896,128]{1,0:T(8,128)(2,1)S(1)} collective-permute-done((bf16[896,128]{1,0:T(8,128)(2,1)S(1)}, bf16[896,128]{1,0:T(8,128)(2,1)S(1)}, u32[]{:S(2)}, u32[]{:S(2)}) %collective-permute-start) | collective-permute-done | bytes 229408 | tf_op jit(solution)/shard_map/ppermute | solution.py:22
  33.9 0.0 copy-start.15
  33.9 0.6 fusion.78
  34.5 0.8 collective-permute-start.2
  35.3 0.7 collective-permute-start.1
  36.0 7.8 %collective-permute-start.3 = (bf16[896,128]{1,0:T(8,128)(2,1)S(1)}, bf16[896,128]{1,0:T(8,128)(2,1)S(1)}, u32[]{:S(2)}, u32[]{:S(2)}) collective-permute-start(bf16[896,128]{1,0:T(8,128)(2,1)S(1)} %fusion.78), channel_id=1, source_target_pairs={{0,1},{2,3},{4,5},{6,7},{8,9},{10,11},{12,13},{14,15},{16,17},{18,... | collective-permute-start | bytes 688136 | tf_op jit(solution)/shard_map/ppermute | solution.py:22
  43.9 1.8 %fusion.11 = bf16[768,896]{1,0:T(8,128)(2,1)S(1)} fusion(bf16[768,1024]{1,0:T(8,128)(2,1)S(1)} %fusion.refs_6_.refs_5_, bf16[1,1792,896]{2,1,0:T(8,128)(2,1)S(1)} %copy-done.15), kind=kOutput, calls=%fused_computation.12 | convolution fusion | flops 1409974272 | bytes 4784128 | tf_op jit(solution)/shard_map/dot_general | solution.py:207
  45.7 0.0 copy-start.7
  45.7 3.9 %shard_map.175.refs_9_.refs_10_ = bf16[512,1792]{1,0:T(8,128)(2,1)S(1)} custom-call(s32[16,1024]{1,0:T(8,128)S(1)} %select_select_fusion.neighbours_ref, f32[16,1024]{1,0:T(8,128)S(1)} %copy-done.4), custom_call_target="tpu_custom_call" | custom-call | flops 734003200 | bytes 1835008 | tf_op jit(solution)/shard_map/pallas_call | solution.py:62
  49.7 0.1 fusion.146
  49.8 0.6 fusion.66
  50.4 0.6 fusion.72
  51.1 0.1 collective-permute-start.5
  51.2 0.5 convolution_convert_fusion.2
  51.7 0.6 fusion.69
  52.4 4.4 %collective-permute-start.9 = (bf16[384,128]{1,0:T(8,128)(2,1)S(1)}, bf16[384,128]{1,0:T(8,128)(2,1)S(1)}, u32[]{:S(2)}, u32[]{:S(2)}) collective-permute-start(bf16[384,128]{1,0:T(8,128)(2,1)S(1)} %get-tuple-element.87), channel_id=1, source_target_pairs={{0,31},{1,30},{2,5},{3,4},{4,3},{5,2},{6,9},{7,8},{8,7},{9,6},{10,... | collective-permute-start | bytes 294920 | tf_op jit(solution)/shard_map/ppermute | solution.py:22
  56.8 0.5 convolution_convert_fusion.3
  57.4 1.6 %collective-permute-start.8 = (bf16[384,128]{1,0:T(8,128)(2,1)S(1)}, bf16[384,128]{1,0:T(8,128)(2,1)S(1)}, u32[]{:S(2)}, u32[]{:S(2)}) collective-permute-start(bf16[384,128]{1,0:T(8,128)(2,1)S(1)} %get-tuple-element.89), channel_id=1, source_target_pairs={{0,30},{1,31},{2,4},{3,5},{4,2},{5,3},{6,8},{7,9},{8,6},{9,7},{10,... | collective-permute-start | bytes 294920 | tf_op jit(solution)/shard_map/ppermute | solution.py:22
  59.0 0.6 fusion.33.refs_0_
  59.6 0.6 collective-permute-done.9.refs_5_
  60.2 2.1 %collective-permute-done.7.refs_3_ = bf16[384,128]{1,0:T(8,128)(2,1)S(1)} collective-permute-done((bf16[384,128]{1,0:T(8,128)(2,1)S(1)}, bf16[384,128]{1,0:T(8,128)(2,1)S(1)}, u32[]{:S(2)}, u32[]{:S(2)}) %collective-permute-start.7) | collective-permute-done | bytes 98336 | tf_op jit(solution)/shard_map/ppermute | solution.py:22
  62.3 1.9 %collective-permute-done.8.refs_4_ = bf16[384,128]{1,0:T(8,128)(2,1)S(1)} collective-permute-done((bf16[384,128]{1,0:T(8,128)(2,1)S(1)}, bf16[384,128]{1,0:T(8,128)(2,1)S(1)}, u32[]{:S(2)}, u32[]{:S(2)}) %collective-permute-start.8) | collective-permute-done | bytes 98336 | tf_op jit(solution)/shard_map/ppermute | solution.py:22
  64.2 0.2 broadcast_in_dim.10.refs_6_
  64.4 2.5 %operate_second.1 = (f32[1024,128]{1,0:T(8,128)S(1)}, f32[1024,128]{1,0:T(8,128)S(1)}, f32[16,2,128]{2,1,0:T(2,128)S(1)}) custom-call(f32[1024,128]{1,0:T(8,128)S(1)} %fusion.33.refs_0_, bf16[1024,128]{1,0:T(8,128)(2,1)S(1)} %collective-permute-done.5.refs_1_, bf16[384,128]{1,0:T(8,128)(2,1)S(1)} %collective-permute-done.6.refs_2_, ...), custom_call_target="tpu_custom_call" | custom-call | flops 469762048 | bytes 3670016 | tf_op jit(solution)/shard_map/operate_second/pallas_call | solution.py:131
  66.9 9.5 %all_to_all.15.refs_1_ = f32[16,2,128]{2,1,0:T(2,128)S(1)} all-to-all(f32[16,2,128]{2,1,0:T(2,128)S(1)} %get-tuple-element.52), channel_id=1, replica_groups=mesh['sub'=16,'panel'=2] {'sub'}, dimensions={0} | all-to-all | bytes 32768 | tf_op jit(solution)/shard_map/all_to_all | solution.py:318
  76.4 1.1 shard_map.176
  77.6 0.6 fusion.87
  78.1 2.5 %collective-permute-start.14 = (bf16[896,128]{1,0:T(8,128)(2,1)S(1)}, bf16[896,128]{1,0:T(8,128)(2,1)S(1)}, u32[]{:S(2)}, u32[]{:S(2)}) collective-permute-start(bf16[896,128]{1,0:T(8,128)(2,1)S(1)} %fusion.87), channel_id=1, source_target_pairs={{0,1},{2,3},{4,5},{6,7},{8,9},{10,11},{12,13},{14,15},{16,17},{18,... | collective-permute-start | bytes 688136 | tf_op jit(solution)/shard_map/ppermute | solution.py:22
  80.6 0.1 collective-permute-start.10
  80.7 9.6 %collective-permute-done.10 = bf16[896,128]{1,0:T(8,128)(2,1)S(1)} collective-permute-done((bf16[896,128]{1,0:T(8,128)(2,1)S(1)}, bf16[896,128]{1,0:T(8,128)(2,1)S(1)}, u32[]{:S(2)}, u32[]{:S(2)}) %collective-permute-start.10) | collective-permute-done | bytes 229408 | tf_op jit(solution)/shard_map/ppermute | solution.py:22
  90.3 0.7 collective-permute-start.12
  91.0 0.9 collective-permute-start.11
  91.9 0.6 fusion.84
  92.5 7.8 %collective-permute-start.13 = (bf16[896,128]{1,0:T(8,128)(2,1)S(1)}, bf16[896,128]{1,0:T(8,128)(2,1)S(1)}, u32[]{:S(2)}, u32[]{:S(2)}) collective-permute-start(bf16[896,128]{1,0:T(8,128)(2,1)S(1)} %fusion.84), channel_id=1, source_target_pairs={{0,1},{2,3},{4,5},{6,7},{8,9},{10,11},{12,13},{14,15},{16,17},{18,... | collective-permute-start | bytes 688136 | tf_op jit(solution)/shard_map/ppermute | solution.py:22
  100.5 0.6 fusion.63
  101.1 0.5 convolution_convert_fusion
  101.6 4.5 %collective-permute-start.19 = (bf16[384,128]{1,0:T(8,128)(2,1)S(1)}, bf16[384,128]{1,0:T(8,128)(2,1)S(1)}, u32[]{:S(2)}, u32[]{:S(2)}) collective-permute-start(bf16[384,128]{1,0:T(8,128)(2,1)S(1)} %get-tuple-element.79), channel_id=1, source_target_pairs={{0,31},{1,30},{2,5},{3,4},{4,3},{5,2},{6,9},{7,8},{8,7},{9,6},{10,... | collective-permute-start | bytes 294920 | tf_op jit(solution)/shard_map/ppermute | solution.py:22
  106.2 0.6 fusion.75
  106.8 1.1 collective-permute-start.15
  107.9 0.6 add_convert_fusion
  108.5 0.5 convolution_convert_fusion.1
  109.1 2.7 %collective-permute-start.18 = (bf16[384,128]{1,0:T(8,128)(2,1)S(1)}, bf16[384,128]{1,0:T(8,128)(2,1)S(1)}, u32[]{:S(2)}, u32[]{:S(2)}) collective-permute-start(bf16[384,128]{1,0:T(8,128)(2,1)S(1)} %get-tuple-element.81), channel_id=1, source_target_pairs={{0,30},{1,31},{2,4},{3,5},{4,2},{5,3},{6,8},{7,9},{8,6},{9,7},{10,... | collective-permute-start | bytes 294920 | tf_op jit(solution)/shard_map/ppermute | solution.py:22
  111.7 0.6 fusion.30.refs_0_
  112.4 3.5 %collective-permute-done.18.refs_4_ = bf16[384,128]{1,0:T(8,128)(2,1)S(1)} collective-permute-done((bf16[384,128]{1,0:T(8,128)(2,1)S(1)}, bf16[384,128]{1,0:T(8,128)(2,1)S(1)}, u32[]{:S(2)}, u32[]{:S(2)}) %collective-permute-start.18) | collective-permute-done | bytes 98336 | tf_op jit(solution)/shard_map/ppermute | solution.py:22
  115.9 1.2 collective-permute-done.15.refs_1_
  117.0 2.6 %operate_closing.1 = (f32[1024,128]{1,0:T(8,128)S(1)}, f32[1024,128]{1,0:T(8,128)S(1)}, f32[16,4,128]{2,1,0:T(4,128)S(1)}) custom-call(f32[1024,128]{1,0:T(8,128)S(1)} %fusion.30.refs_0_, bf16[1024,128]{1,0:T(8,128)(2,1)S(1)} %collective-permute-done.15.refs_1_, bf16[384,128]{1,0:T(8,128)(2,1)S(1)} %collective-permute-done.16.refs_2_, ...), custom_call_target="tpu_custom_call" | custom-call | flops 469762048 | bytes 3670016 | tf_op jit(solution)/shard_map/operate_closing/pallas_call | solution.py:131
  119.6 10.8 %all_to_all.16 = f32[16,4,128]{2,1,0:T(4,128)S(1)} all-to-all(f32[16,4,128]{2,1,0:T(4,128)S(1)} %get-tuple-element.60), channel_id=1, replica_groups=mesh['sub'=16,'panel'=2] {'sub'}, dimensions={0} | all-to-all | bytes 65536 | tf_op jit(solution)/shard_map/all_to_all | solution.py:318
  130.4 0.5 fusion.125
  130.9 1.1 multiply_subtract_fusion
  (73 shorter events, 0.5 us)
Async XLA Ops:
  0.6 17.6 %copy-start.1 = (f32[1024,128]{1,0:T(8,128)S(1)}, f32[1024,128]{1,0:T(8,128)}, u32[]{:S(2)}) copy-start(f32[1024,128]{1,0:T(8,128)} %refs_3_.3) | copy-start | bytes 1572868
  0.6 12.3 %copy-start.11 = (f32[128]{0:T(128)S(1)}, f32[128]{0:T(128)}, u32[]{:S(2)}) copy-start(f32[128]{0:T(128)} %param.21) | copy-start | bytes 1540
  0.7 12.3 %copy-start.12 = (f32[128]{0:T(128)S(1)}, f32[128]{0:T(128)}, u32[]{:S(2)}) copy-start(f32[128]{0:T(128)} %param.20) | copy-start | bytes 1540
  0.7 12.3 %copy-start.13 = (f32[128]{0:T(128)S(1)}, f32[128]{0:T(128)}, u32[]{:S(2)}) copy-start(f32[128]{0:T(128)} %param.19) | copy-start | bytes 1540
  0.7 17.6 %copy-start.3 = (f32[1024,128]{1,0:T(8,128)S(1)}, f32[1024,128]{1,0:T(8,128)}, u32[]{:S(2)}) copy-start(f32[1024,128]{1,0:T(8,128)} %refs_5_.1) | copy-start | bytes 1572868
  0.7 17.6 %copy-start.2 = (f32[1024,128]{1,0:T(8,128)S(1)}, f32[1024,128]{1,0:T(8,128)}, u32[]{:S(2)}) copy-start(f32[1024,128]{1,0:T(8,128)} %refs_4_.1) | copy-start | bytes 1572868
  4.2 14.0 %all-to-all-start = ((f32[16,2,128]{2,1,0:T(2,128)}), f32[16,2,128]{2,1,0:T(2,128)S(1)}, u32[]{:S(2)}, u32[]{:S(2)}) async-start(f32[16,2,128]{2,1,0:T(2,128)} %broadcast_in_dim.8), calls=%async_computation | async-start | bytes 32768 | tf_op jit(solution)/shard_map/all_to_all | solution.py:318
  18.2 1.9 %copy-start.14 = (bf16[1,1792,896]{2,1,0:T(8,128)(2,1)S(1)}, bf16[1,1792,896]{2,1,0:T(8,128)(2,1)}, u32[]{:S(2)}) copy-start(bf16[1,1792,896]{2,1,0:T(8,128)(2,1)} %param.22) | copy-start | bytes 9633796
  18.9 5.4 %copy-start.4 = (f32[16,1024]{1,0:T(8,128)S(1)}, f32[16,1024]{1,0:T(8,128)}, u32[]{:S(2)}) copy-start(f32[16,1024]{1,0:T(8,128)} %weight_ref.3) | copy-start | bytes 196612
  20.7 29.0 %collective-permute-start.4 = (bf16[896,128]{1,0:T(8,128)(2,1)S(1)}, bf16[896,128]{1,0:T(8,128)(2,1)S(1)}, u32[]{:S(2)}, u32[]{:S(2)}) collective-permute-start(bf16[896,128]{1,0:T(8,128)(2,1)S(1)} %fusion.81), channel_id=1, source_target_pairs={{0,1},{2,3},{4,5},{6,7},{8,9},{10,11},{12,13},{14,15},{16,17},{18,... | collective-permute-start | bytes 688136 | tf_op jit(solution)/shard_map/ppermute | solution.py:22
  24.2 9.7 %collective-permute-start = (bf16[896,128]{1,0:T(8,128)(2,1)S(1)}, bf16[896,128]{1,0:T(8,128)(2,1)S(1)}, u32[]{:S(2)}, u32[]{:S(2)}) collective-permute-start(bf16[896,128]{1,0:T(8,128)(2,1)S(1)} %get-tuple-element.38), channel_id=1, source_target_pairs={{0,1},{1,0},{2,3},{3,2},{4,5},{5,4},{6,7},{7,6},{8,9},{9,8},{10,11... | collective-permute-start | bytes 688136 | tf_op jit(solution)/shard_map/ppermute | solution.py:22
  33.8 11.8 %copy-start.6 = (bf16[896,128]{1,0:T(8,128)(2,1)}, bf16[896,128]{1,0:T(8,128)(2,1)S(1)}, u32[]{:S(2)}) copy-start(bf16[896,128]{1,0:T(8,128)(2,1)S(1)} %collective-permute-done) | copy-start | bytes 688132
  33.9 10.0 %copy-start.15 = (bf16[1,1792,896]{2,1,0:T(8,128)(2,1)S(1)}, bf16[1,1792,896]{2,1,0:T(8,128)(2,1)}, u32[]{:S(2)}) copy-start(bf16[1,1792,896]{2,1,0:T(8,128)(2,1)} %param.23) | copy-start | bytes 9633796
  34.5 15.1 %collective-permute-start.2 = (bf16[384,256]{1,0:T(8,128)(2,1)S(1)}, bf16[384,256]{1,0:T(8,128)(2,1)S(1)}, u32[]{:S(2)}, u32[]{:S(2)}) collective-permute-start(bf16[384,256]{1,0:T(8,128)(2,1)S(1)} %pad_maximum_fusion.1), channel_id=1, source_target_pairs={{1,3},{3,1},{5,7},{7,5},{9,11},{11,9},{13,15},{15,13},{17,19},{19,... | collective-permute-start | bytes 589832 | tf_op jit(solution)/shard_map/ppermute | solution.py:22
  35.3 14.3 %collective-permute-start.1 = (bf16[384,256]{1,0:T(8,128)(2,1)S(1)}, bf16[384,256]{1,0:T(8,128)(2,1)S(1)}, u32[]{:S(2)}, u32[]{:S(2)}) collective-permute-start(bf16[384,256]{1,0:T(8,128)(2,1)S(1)} %pad_maximum_fusion), channel_id=1, source_target_pairs={{1,31},{3,5},{5,3},{7,9},{9,7},{11,13},{13,11},{15,17},{17,15},{19... | collective-permute-start | bytes 589832 | tf_op jit(solution)/shard_map/ppermute | solution.py:22
  36.0 15.2 %collective-permute-start.3 = (bf16[896,128]{1,0:T(8,128)(2,1)S(1)}, bf16[896,128]{1,0:T(8,128)(2,1)S(1)}, u32[]{:S(2)}, u32[]{:S(2)}) collective-permute-start(bf16[896,128]{1,0:T(8,128)(2,1)S(1)} %fusion.78), channel_id=1, source_target_pairs={{0,1},{2,3},{4,5},{6,7},{8,9},{10,11},{12,13},{14,15},{16,17},{18,... | collective-permute-start | bytes 688136 | tf_op jit(solution)/shard_map/ppermute | solution.py:22
  45.7 4.1 %copy-start.7 = (bf16[896,128]{1,0:T(8,128)(2,1)S(1)}, bf16[896,128]{1,0:T(8,128)(2,1)}, u32[]{:S(2)}) copy-start(bf16[896,128]{1,0:T(8,128)(2,1)} %copy-done.6) | copy-start | bytes 688132
  45.7 4.1 %slice-start = ((bf16[896,128]{1,0:T(8,128)(2,1)}), bf16[128,128]{1,0:T(8,128)(2,1)S(1)}, s32[]{:S(2)}) async-start(bf16[896,128]{1,0:T(8,128)(2,1)} %copy-done.6), calls=%async_computation.3 | async-start | bytes 65536 | tf_op jit(solution)/shard_map/slice | solution.py:293
  50.4 0.8 copy-start.8
  51.1 13.1 %collective-permute-start.5 = (bf16[1024,128]{1,0:T(8,128)(2,1)S(1)}, bf16[1024,128]{1,0:T(8,128)(2,1)S(1)}, u32[]{:S(2)}, u32[]{:S(2)}) collective-permute-start(bf16[1024,128]{1,0:T(8,128)(2,1)S(1)} %fusion.72), channel_id=1, source_target_pairs={{0,1},{1,0},{2,3},{3,2},{4,5},{5,4},{6,7},{7,6},{8,9},{9,8},{10,11... | collective-permute-start | bytes 786440 | tf_op jit(solution)/shard_map/ppermute | solution.py:22
  52.4 7.8 %collective-permute-start.9 = (bf16[384,128]{1,0:T(8,128)(2,1)S(1)}, bf16[384,128]{1,0:T(8,128)(2,1)S(1)}, u32[]{:S(2)}, u32[]{:S(2)}) collective-permute-start(bf16[384,128]{1,0:T(8,128)(2,1)S(1)} %get-tuple-element.87), channel_id=1, source_target_pairs={{0,31},{1,30},{2,5},{3,4},{4,3},{5,2},{6,9},{7,8},{8,7},{9,6},{10,... | collective-permute-start | bytes 294920 | tf_op jit(solution)/shard_map/ppermute | solution.py:22
  56.8 5.5 %collective-permute-start.7 = (bf16[384,128]{1,0:T(8,128)(2,1)S(1)}, bf16[384,128]{1,0:T(8,128)(2,1)S(1)}, u32[]{:S(2)}, u32[]{:S(2)}) collective-permute-start(bf16[384,128]{1,0:T(8,128)(2,1)S(1)} %get-tuple-element.88), channel_id=1, source_target_pairs={{0,3},{1,2},{2,1},{3,0},{4,7},{5,6},{6,5},{7,4},{8,11},{9,10},{10,... | collective-permute-start | bytes 294920 | tf_op jit(solution)/shard_map/ppermute | solution.py:22
  57.4 7.0 %copy-start = (f32[1024,128]{1,0:T(8,128)S(1)}, f32[1024,128]{1,0:T(8,128)}, u32[]{:S(2)}) copy-start(f32[1024,128]{1,0:T(8,128)} %refs_7_.3) | copy-start | bytes 1572868
  57.4 6.8 %collective-permute-start.8 = (bf16[384,128]{1,0:T(8,128)(2,1)S(1)}, bf16[384,128]{1,0:T(8,128)(2,1)S(1)}, u32[]{:S(2)}, u32[]{:S(2)}) collective-permute-start(bf16[384,128]{1,0:T(8,128)(2,1)S(1)} %get-tuple-element.89), channel_id=1, source_target_pairs={{0,30},{1,31},{2,4},{3,5},{4,2},{5,3},{6,8},{7,9},{8,6},{9,7},{10,... | collective-permute-start | bytes 294920 | tf_op jit(solution)/shard_map/ppermute | solution.py:22
  59.0 5.2 %collective-permute-start.6 = (bf16[384,128]{1,0:T(8,128)(2,1)S(1)}, bf16[384,128]{1,0:T(8,128)(2,1)S(1)}, u32[]{:S(2)}, u32[]{:S(2)}) collective-permute-start(bf16[384,128]{1,0:T(8,128)(2,1)S(1)} %get-tuple-element.90), channel_id=1, source_target_pairs={{0,2},{1,3},{2,0},{3,1},{4,6},{5,7},{6,4},{7,5},{8,10},{9,11},{10,... | collective-permute-start | bytes 294920 | tf_op jit(solution)/shard_map/ppermute | solution.py:22
  78.1 22.3 %collective-permute-start.14 = (bf16[896,128]{1,0:T(8,128)(2,1)S(1)}, bf16[896,128]{1,0:T(8,128)(2,1)S(1)}, u32[]{:S(2)}, u32[]{:S(2)}) collective-permute-start(bf16[896,128]{1,0:T(8,128)(2,1)S(1)} %fusion.87), channel_id=1, source_target_pairs={{0,1},{2,3},{4,5},{6,7},{8,9},{10,11},{12,13},{14,15},{16,17},{18,... | collective-permute-start | bytes 688136 | tf_op jit(solution)/shard_map/ppermute | solution.py:22
  80.6 9.7 %collective-permute-start.10 = (bf16[896,128]{1,0:T(8,128)(2,1)S(1)}, bf16[896,128]{1,0:T(8,128)(2,1)S(1)}, u32[]{:S(2)}, u32[]{:S(2)}) collective-permute-start(bf16[896,128]{1,0:T(8,128)(2,1)S(1)} %get-tuple-element.58), channel_id=1, source_target_pairs={{0,1},{1,0},{2,3},{3,2},{4,5},{5,4},{6,7},{7,6},{8,9},{9,8},{10,11... | collective-permute-start | bytes 688136 | tf_op jit(solution)/shard_map/ppermute | solution.py:22
  90.3 10.0 %collective-permute-start.12 = (bf16[384,256]{1,0:T(8,128)(2,1)S(1)}, bf16[384,256]{1,0:T(8,128)(2,1)S(1)}, u32[]{:S(2)}, u32[]{:S(2)}) collective-permute-start(bf16[384,256]{1,0:T(8,128)(2,1)S(1)} %pad_maximum_fusion.3), channel_id=1, source_target_pairs={{1,3},{3,1},{5,7},{7,5},{9,11},{11,9},{13,15},{15,13},{17,19},{19,... | collective-permute-start | bytes 589832 | tf_op jit(solution)/shard_map/ppermute | solution.py:22
  91.0 9.3 %collective-permute-start.11 = (bf16[384,256]{1,0:T(8,128)(2,1)S(1)}, bf16[384,256]{1,0:T(8,128)(2,1)S(1)}, u32[]{:S(2)}, u32[]{:S(2)}) collective-permute-start(bf16[384,256]{1,0:T(8,128)(2,1)S(1)} %pad_maximum_fusion.2), channel_id=1, source_target_pairs={{1,31},{3,5},{5,3},{7,9},{9,7},{11,13},{13,11},{15,17},{17,15},{19... | collective-permute-start | bytes 589832 | tf_op jit(solution)/shard_map/ppermute | solution.py:22
  92.5 15.4 %collective-permute-start.13 = (bf16[896,128]{1,0:T(8,128)(2,1)S(1)}, bf16[896,128]{1,0:T(8,128)(2,1)S(1)}, u32[]{:S(2)}, u32[]{:S(2)}) collective-permute-start(bf16[896,128]{1,0:T(8,128)(2,1)S(1)} %fusion.84), channel_id=1, source_target_pairs={{0,1},{2,3},{4,5},{6,7},{8,9},{10,11},{12,13},{14,15},{16,17},{18,... | collective-permute-start | bytes 688136 | tf_op jit(solution)/shard_map/ppermute | solution.py:22
  101.6 10.7 %collective-permute-start.19 = (bf16[384,128]{1,0:T(8,128)(2,1)S(1)}, bf16[384,128]{1,0:T(8,128)(2,1)S(1)}, u32[]{:S(2)}, u32[]{:S(2)}) collective-permute-start(bf16[384,128]{1,0:T(8,128)(2,1)S(1)} %get-tuple-element.79), channel_id=1, source_target_pairs={{0,31},{1,30},{2,5},{3,4},{4,3},{5,2},{6,9},{7,8},{8,7},{9,6},{10,... | collective-permute-start | bytes 294920 | tf_op jit(solution)/shard_map/ppermute | solution.py:22
  106.2 6.2 %collective-permute-start.17 = (bf16[384,128]{1,0:T(8,128)(2,1)S(1)}, bf16[384,128]{1,0:T(8,128)(2,1)S(1)}, u32[]{:S(2)}, u32[]{:S(2)}) collective-permute-start(bf16[384,128]{1,0:T(8,128)(2,1)S(1)} %get-tuple-element.80), channel_id=1, source_target_pairs={{0,3},{1,2},{2,1},{3,0},{4,7},{5,6},{6,5},{7,4},{8,11},{9,10},{10,... | collective-permute-start | bytes 294920 | tf_op jit(solution)/shard_map/ppermute | solution.py:22
  106.8 10.2 %collective-permute-start.15 = (bf16[1024,128]{1,0:T(8,128)(2,1)S(1)}, bf16[1024,128]{1,0:T(8,128)(2,1)S(1)}, u32[]{:S(2)}, u32[]{:S(2)}) collective-permute-start(bf16[1024,128]{1,0:T(8,128)(2,1)S(1)} %fusion.75), channel_id=1, source_target_pairs={{0,1},{1,0},{2,3},{3,2},{4,5},{5,4},{6,7},{7,6},{8,9},{9,8},{10,11... | collective-permute-start | bytes 786440 | tf_op jit(solution)/shard_map/ppermute | solution.py:22
  109.1 6.8 %collective-permute-start.18 = (bf16[384,128]{1,0:T(8,128)(2,1)S(1)}, bf16[384,128]{1,0:T(8,128)(2,1)S(1)}, u32[]{:S(2)}, u32[]{:S(2)}) collective-permute-start(bf16[384,128]{1,0:T(8,128)(2,1)S(1)} %get-tuple-element.81), channel_id=1, source_target_pairs={{0,30},{1,31},{2,4},{3,5},{4,2},{5,3},{6,8},{7,9},{8,6},{9,7},{10,... | collective-permute-start | bytes 294920 | tf_op jit(solution)/shard_map/ppermute | solution.py:22
  111.7 4.2 %collective-permute-start.16 = (bf16[384,128]{1,0:T(8,128)(2,1)S(1)}, bf16[384,128]{1,0:T(8,128)(2,1)S(1)}, u32[]{:S(2)}, u32[]{:S(2)}) collective-permute-start(bf16[384,128]{1,0:T(8,128)(2,1)S(1)} %get-tuple-element.82), channel_id=1, source_target_pairs={{0,2},{1,3},{2,0},{3,1},{4,6},{5,7},{6,4},{7,5},{8,10},{9,11},{10,... | collective-permute-start | bytes 294920 | tf_op jit(solution)/shard_map/ppermute | solution.py:22
  117.0 13.9 %copy-start.5 = (f32[1024,128]{1,0:T(8,128)S(1)}, f32[1024,128]{1,0:T(8,128)}, u32[]{:S(2)}) copy-start(f32[1024,128]{1,0:T(8,128)} %param.14) | copy-start | bytes 1572868
  117.0 13.9 %copy-start.10 = (f32[1,128]{1,0:T(1,128)S(1)}, f32[1,128]{1,0:T(1,128)}, u32[]{:S(2)}) copy-start(f32[1,128]{1,0:T(1,128)} %get-tuple-element.55) | copy-start | bytes 1540
  130.9 1.1 copy-start.9

commit v3 on v2

--- a/solution.py
+++ b/solution.py
@@ -147,52 +147,43 @@
     )(*operands)
 
 
-def split_rows(vector, select, panel, mine_ref, payload_ref):
+def round_and_select(vector, select, rounded_ref, ghosts_ref):
     rounded = vector.astype(jnp.bfloat16)
-    half = mine_ref.shape[0]
-    tail = rounded.shape[0] - half
+    rounded_ref[...] = rounded
     ghosts = jnp.dot(select[...], rounded, preferred_element_type=jnp.float32)
-    ghosts = ghosts.astype(jnp.bfloat16)
-
-    def put(head_ref, rest_ref):
-        head_ref[...] = rounded[:half]
-        rest_ref[:tail] = rounded[half:]
-        rest_ref[tail:] = ghosts
-
-    pl.when(panel[0] == 0)(lambda: put(mine_ref, payload_ref))
-    pl.when(panel[0] != 0)(lambda: put(payload_ref, mine_ref))
-
-
-def direction_kernel(node_count, panel, sums, past, residual, direction, old_image, select, *outs):
-    means_ref, mine_ref, payload_ref = outs
+    ghosts_ref[...] = ghosts.astype(jnp.bfloat16)
+
+
+def direction_kernel(node_count, sums, past, residual, direction, old_image, select, *outs):
+    means_ref, rounded_ref, ghosts_ref = outs
     means = jnp.sum(sums[...], axis=0) / node_count
     means_ref[...] = means
     rho_prev, alpha_prev, omega_prev = past[0:1], past[1:2], past[2:3]
     step_beta = means[0:1] / rho_prev * (alpha_prev / omega_prev)
     vector = residual[...] + step_beta * (direction[...] - omega_prev * old_image[...])
-    split_rows(vector, select, panel, mine_ref, payload_ref)
-
-
-def middle_kernel(node_count, panel, sums, opening, residual, image, select, *outs):
-    alpha_ref, middle_ref, mine_ref, payload_ref = outs
+    round_and_select(vector, select, rounded_ref, ghosts_ref)
+
+
+def middle_kernel(node_count, sums, opening, residual, image, select, *outs):
+    alpha_ref, middle_ref, rounded_ref, ghosts_ref = outs
     means = jnp.sum(sums[...], axis=0) / node_count
     floor = FLOOR_SHARE * jnp.sqrt(opening[1:2] * means[1:2])
     step_alpha = opening[0:1] / jnp.maximum(means[0:1], floor)
     alpha_ref[...] = step_alpha
     middle = residual[...] - step_alpha * image[...]
     middle_ref[...] = middle
-    split_rows(middle, select, panel, mine_ref, payload_ref)
-
-
-def small_call(kernel, panel, operands, outs):
+    round_and_select(middle, select, rounded_ref, ghosts_ref)
+
+
+def small_call(kernel, operands, outs):
     in_vmem = pl.BlockSpec(memory_space=pltpu.VMEM)
     return pl.pallas_call(
         kernel,
-        in_specs=[pl.BlockSpec(memory_space=pltpu.SMEM)] + [in_vmem] * len(operands),
+        in_specs=[in_vmem] * len(operands),
         out_specs=[in_vmem] * len(outs),
         out_shape=outs,
         compiler_params=pltpu.CompilerParams(vmem_limit_bytes=12 << 20),
-    )(panel.reshape(1), *operands)
+    )(*operands)
 
 
 def near(s):
@@ -231,17 +222,14 @@
     ext, half = lower.shape
     upper = upper_inverse[0, :own]
     border = send_rows.shape[2]
-    tail = own - half
 
     blocks = own // 128
     cuts = (0, blocks // 2, blocks)
     coupling = []
 
-    def next_coupling(trigger):
+    def next_coupling():
         begin, end = cuts[len(coupling) : len(coupling) + 2]
-        trigger, links = lax.optimization_barrier((trigger, neighbours))
-        coupling.append(coupling_rows(links, edge_weight, ext, begin, end - begin))
-        return trigger
+        coupling.append(coupling_rows(neighbours, edge_weight, ext, begin, end - begin))
 
     def meet(arrived, value):
         return lax.optimization_barrier((arrived, value))
@@ -254,7 +242,6 @@
     turned = jnp.where(neighbours < own + border, neighbours + border, neighbours - border)
     ghost = even & (neighbours >= own) & (neighbours < ext)
     neighbours = jnp.where(ghost, turned, neighbours)
-    near_far = by_parity(send_rows[0, ::-1], send_rows[0])
     rows = lax.broadcasted_iota(jnp.int32, (1, own), 1)
 
     def by_panel(zero, one):
@@ -262,39 +249,30 @@
 
     diagonal_rows = lax.dynamic_slice_in_dim(lower, panel * half, half, axis=0)
 
-    def precondition(mine, payload, chosen_upper):
-        build = chosen_upper is None
+    def precondition(rounded, ghosts, build):
+        head, rest = rounded[:half], rounded[half:]
+        near_rows, far_rows = ghosts[:border], ghosts[border:]
+        early = matmul(lower[half:], head).astype(jnp.bfloat16)
+        payload = by_panel(jnp.concatenate([early, rest], axis=0), rounded)
+        received = send(payload, lambda s, p: (s, 1 - p))
+        far_cross = send(far_rows, lambda s, p: (far(s), 1) if p == 0 else None)
+        far_same = send(far_rows, lambda s, p: (far(s), 1) if p == 1 else None)
+        near_cross = send(near_rows, lambda s, p: (near(s), 1) if p == 0 else None)
+        near_same = send(near_rows, lambda s, p: (near(s), 1) if p == 1 else None)
         if build:
-            payload = next_coupling(payload)
-        received = send(payload, lambda s, p: (s, 1 - p))
-        early = matmul(lower[half:], mine).astype(jnp.bfloat16)
-        passed_others = send(early, lambda s, p: (s, 1) if p == 0 else None)
-        if build:
+            next_coupling()
             received, coupling[-1] = meet(received, coupling[-1])
-        late = matmul(lower[half:], received).astype(jnp.bfloat16)
-        if build:
-            late, chosen = lax.optimization_barrier((next_coupling(late), select))
-            chosen_upper = matmul(chosen, upper).astype(jnp.bfloat16)
+        late = matmul(lower[half:], received[:half]).astype(jnp.bfloat16)
         passed_mine = send(late, lambda s, p: (s, 1) if p == 0 else None)
-        near_rows, far_rows = slice(tail, tail + border), slice(tail + border, half)
-
-        def both(part):
-            return jnp.concatenate([received[part], mine[part]], axis=1)
-
-        from_far = send(both(far_rows), lambda s, p: (far(s), 1) if p == 1 else None)
-        from_near = send(both(near_rows), lambda s, p: (near(s), 1) if p == 1 else None)
-        if build:
-            passed_mine, coupling[-1] = meet(passed_mine, coupling[-1])
-            passed_mine, chosen_upper = meet(passed_mine, chosen_upper)
-        from_lower, from_upper = by_parity(from_far, from_near), by_parity(from_near, from_far)
-
-        def solve(kept, ghost_columns, passed):
-            ghosts = [from_lower[:, ghost_columns], from_upper[:, ghost_columns]]
-            rhs = by_panel(kept, jnp.concatenate([kept[:tail], *ghosts], axis=0))
+
+        def solve(kept, last, from_far, from_near, passed):
+            lower_upper = [by_parity(from_far, from_near), by_parity(from_near, from_far)]
+            rhs = by_panel(kept, jnp.concatenate([last, *lower_upper], axis=0))
             product = matmul(diagonal_rows, rhs) + passed.astype(jnp.float32)
             return lax.optimization_barrier(product.astype(jnp.bfloat16))
 
-        others = solve(received, slice(0, cols), passed_others)
+        passed_others = by_panel(jnp.zeros_like(head), received[:half])
+        others = solve(received[:half], received[half:], far_cross, near_cross, passed_others)
         if build:
             others, links = lax.optimization_barrier((others, neighbours))
             present = jnp.where(links < ext, edge_weight, 0.0)
@@ -302,15 +280,18 @@
             diagonal.append(scale)
         other_part = matmul(upper, others).astype(jnp.bfloat16)
         swapped = send(other_part, lambda s, p: (s, 1 - p))
-        mine = solve(mine, slice(cols, 2 * cols), passed_mine)
         other_edge = matmul(chosen_upper, others).astype(jnp.bfloat16)
         cross_far = send(other_edge[border:], lambda s, p: (far(s), 1 - p))
+        cross_near = send(other_edge[:border], lambda s, p: (near(s), 1 - p))
+        mine = solve(head, rest, far_same, near_same, passed_mine)
         edge = matmul(chosen_upper, mine).astype(jnp.bfloat16)
         part = matmul(upper, mine)
         same_far = send(edge[border:], lambda s, p: (far(s), p))
-        cross_near = send(other_edge[:border], lambda s, p: (near(s), 1 - p))
         same_near = send(edge[:border], lambda s, p: (near(s), p))
-        return (part, swapped, same_near, cross_near, same_far, cross_far), chosen_upper
+        if build:
+            next_coupling()
+            swapped, coupling[-1] = meet(swapped, coupling[-1])
+        return part, swapped, same_near, cross_near, same_far, cross_far
 
     copies = lax.axis_size("sub")
 
@@ -319,28 +300,30 @@
 
     diagonal = []
     vector = jax.ShapeDtypeStruct((own, cols), jnp.float32)
-    panel_rows = jax.ShapeDtypeStruct((half, cols), jnp.bfloat16)
+    narrow = [jax.ShapeDtypeStruct((count, cols), jnp.bfloat16) for count in (own, 2 * border)]
     sums = jnp.stack([jnp.sum(shadow * residual, axis=0), jnp.sum(shadow * shadow, axis=0)])
     sums = jnp.broadcast_to(sums[None], (copies, 2, cols))
-    sums, near_far = lax.optimization_barrier((sums, near_far))
-    select = (near_far.reshape(2 * border, 1) == rows).astype(jnp.bfloat16)
+    sums, lists = lax.optimization_barrier((sums, send_rows))
+    near_far = [by_parity(lists[0, 1], lists[0, 0]), by_parity(lists[0, 0], lists[0, 1])]
+    select = jnp.concatenate(near_far)[:, None] == rows
+    select = select.astype(jnp.bfloat16)
+    chosen_upper = matmul(select, upper).astype(jnp.bfloat16)
+    opening_sums, chosen_upper = meet(exchange(sums), chosen_upper)
     past = jnp.stack([rho_prev, alpha_prev, omega_prev])
-    opening, mine, payload = small_call(
+    opening, rounded, ghosts = small_call(
         lambda *refs: direction_kernel(node_count, *refs),
-        panel,
-        (exchange(sums), past, residual, direction, old_image, select),
-        [jax.ShapeDtypeStruct((2, cols), jnp.float32), panel_rows, panel_rows],
+        (opening_sums, past, residual, direction, old_image, select),
+        [jax.ShapeDtypeStruct((2, cols), jnp.float32), *narrow],
     )
-    parts, chosen_upper = precondition(mine, payload, None)
+    parts = precondition(rounded, ghosts, True)
     direction_hat, image_new, sums = operate(parts, diagonal[0], shadow, None, coupling, copies)
-    step_alpha, middle, mine, payload = small_call(
+    step_alpha, middle, rounded, ghosts = small_call(
         lambda *refs: middle_kernel(node_count, *refs),
-        panel,
         (exchange(sums), opening, residual, image_new, select),
-        [jax.ShapeDtypeStruct((1, cols), jnp.float32), vector, panel_rows, panel_rows],
+        [jax.ShapeDtypeStruct((1, cols), jnp.float32), vector, *narrow],
     )
     step_alpha = step_alpha[0]
-    parts, _ = precondition(mine, payload, chosen_upper)
+    parts = precondition(rounded, ghosts, False)
     middle_hat, tested, sums = operate(parts, diagonal[0], shadow, middle, coupling, copies)
     closing = jnp.sum(exchange(sums), axis=0) / node_count
     step_omega = closing[0] / (closing[1] + EPSILON)

time: 133 us -> 143 us (1.075)
  local copies, waits for them, and re-layouts: 3.87 us -> 8.01 us
  waiting for transfers between devices: 29.7 us -> 33.1 us
  matrix products: 11.2 us -> 13.9 us
  other arithmetic: 4.45 us -> 7.02 us
  starting transfers between devices: 46.6 us -> 44.7 us
    ppermute x20 -> x22, waiting for transfers between devices: 24.4 us -> 33.1 us  [send(): return lax.ppermute(values, AXES, pairs)]
    unnamed x32 -> x42, local copies, waits for them, and re-layouts: 1.31 us -> 7.11 us
    all_to_all x1, waiting for transfers between devices: 5.23 us -> 0.01 us  [exchange(): return lax.all_to_all(values, 'sub', 0, 0)]
    dot_general x17, matrix products: 11.2 us -> 13.9 us  [matmul(): return jnp.dot(left, right, preferred_element_type=jnp.float32)]
    ppermute x20 -> x22, starting transfers between devices: 39.1 us -> 37.4 us  [send(): return lax.ppermute(values, AXES, pairs)]
    rev x1 -> x0, local copies, waits for them, and re-layouts: 1.51 us -> none  [per_device(): near_far = by_parity(send_rows[0, ::-1], send_rows[0])]
  transfers between devices with their start and end apart: 21 -> 23, of which waited for: 8 -> 9; matrix products, arithmetic and copies ran while one was open for 9% -> 9% of each run, Pallas kernels for 6% -> 5%
where the time goes in v3:
time: 143 us; the launch traced here: 142 us
  starting transfers between devices  44.7 us (31%)
  waiting for transfers between devices  33.1 us (23%)
  blocking collectives  19.9 us (14%)
  Pallas kernels  14.1 us (10%)
  matrix products  13.9 us (10%)
  local copies, waits for them, and re-layouts  8.01 us (6%)
  other arithmetic  7.02 us (5%)
    ppermute x22, starting transfers between devices, send(): return lax.ppermute(values, AXES, pairs)  37.4 us
    ppermute x22, waiting for transfers between devices, send(): return lax.ppermute(values, AXES, pairs)  33.1 us
    all_to_all x2, blocking collectives, exchange(): return lax.all_to_all(values, 'sub', 0, 0)  19.9 us
    dot_general x17, matrix products, matmul(): return jnp.dot(left, right, preferred_element_type=jnp.float32)  13.9 us
    pallas_call x2, Pallas kernels, coupling_rows(): pl.pallas_call(coupling_kernel, grid=(count,), in_specs=[pl.BlockSpec((sl...  7.78 us
    all_to_all x1, starting transfers between devices, exchange(): return lax.all_to_all(values, 'sub', 0, 0)  7.39 us
    unnamed x42, local copies, waits for them, and re-layouts  7.11 us
    pallas_call x2, Pallas kernels, operate(): pl.pallas_call(lambda *refs: operate_kernel(closing, *refs), in_specs=[in...  5.1 us
  transfers between devices with their start and end apart: 23, of which 9 were waited for; matrix products, arithmetic and copies ran while one was open for 9% of the time, Pallas kernels for 5%

profile of v3, /device:TPU:0, one launch (start us, length us, event | category | flops | bytes accessed | tf_op | source)
XLA Modules:
  0.0 142.1 jit_solution(17973418046244565923)
XLA Ops:
  0.6 1.4 multiply_reduce_fusion.1
  2.0 0.6 broadcast_in_dim.8
  2.6 7.4 %all-to-all-start = ((f32[16,2,128]{2,1,0:T(2,128)}), f32[16,2,128]{2,1,0:T(2,128)S(1)}, u32[]{:S(2)}, u32[]{:S(2)}) async-start(f32[16,2,128]{2,1,0:T(2,128)} %broadcast_in_dim.8), calls=%async_computation | async-start | bytes 32768 | tf_op jit(solution)/shard_map/all_to_all | solution.py:299
  10.0 0.8 fusion.138
  10.8 0.9 select_select_fusion.neighbours_ref
  12.0 4.5 %fusion.11 = bf16[768,896]{1,0:T(8,128)(2,1)} fusion(s32[768]{0:T(1024)S(1)} %pad_add_fusion, bf16[1,1792,896]{2,1,0:T(8,128)(2,1)} %param.23), kind=kOutput, calls=%fused_computation.12 | convolution fusion | flops 1410760704 | bytes 3214336 | tf_op jit(solution)/shard_map/dot_general | solution.py:198
  16.5 3.9 %shard_map.175.refs_9_.refs_10_ = bf16[512,1792]{1,0:T(8,128)(2,1)S(1)} custom-call(s32[16,1024]{1,0:T(8,128)S(1)} %select_select_fusion.neighbours_ref, f32[16,1024]{1,0:T(8,128)S(1)} %copy-done.10), custom_call_target="tpu_custom_call" | custom-call | flops 734003200 | bytes 1835008 | tf_op jit(solution)/shard_map/pallas_call | solution.py:62
  20.4 0.6 pad_maximum_fusion.refs_1_
  21.0 3.9 %shard_map.174.refs_8_.refs_9_ = bf16[512,1792]{1,0:T(8,128)(2,1)S(1)} custom-call(s32[16,1024]{1,0:T(8,128)S(1)} %select_select_fusion.neighbours_ref, f32[16,1024]{1,0:T(8,128)S(1)} %copy-done.10), custom_call_target="tpu_custom_call" | custom-call | flops 734003200 | bytes 1835008 | tf_op jit(solution)/shard_map/pallas_call | solution.py:62
  24.9 1.3 copy-done
  26.2 1.0 copy-done.3
  27.2 1.0 copy-done.6
  28.3 1.0 copy-done.7
  29.3 0.7 copy-done.11
  30.0 0.6 shard_map.173
  30.6 7.3 %collective-permute-start.4 = (bf16[384,128]{1,0:T(8,128)(2,1)S(1)}, bf16[384,128]{1,0:T(8,128)(2,1)S(1)}, u32[]{:S(2)}, u32[]{:S(2)}) collective-permute-start(bf16[384,128]{1,0:T(8,128)(2,1)S(1)} %get-tuple-element.75), channel_id=1, source_target_pairs={{0,31},{2,5},{4,3},{6,9},{8,7},{10,13},{12,11},{14,17},{16,15},{18... | collective-permute-start | bytes 294920 | tf_op jit(solution)/shard_map/ppermute | solution.py:22
  38.0 0.7 collective-permute-start
  38.6 1.3 collective-permute-start.5
  39.9 0.7 collective-permute-start.1
  40.6 0.6 fusion.85
  41.3 2.5 %collective-permute-start.2 = (bf16[1024,128]{1,0:T(8,128)(2,1)S(1)}, bf16[1024,128]{1,0:T(8,128)(2,1)S(1)}, u32[]{:S(2)}, u32[]{:S(2)}) collective-permute-start(bf16[1024,128]{1,0:T(8,128)(2,1)S(1)} %maximum_select_fusion), channel_id=1, source_target_pairs={{0,1},{1,0},{2,3},{3,2},{4,5},{5,4},{6,7},{7,6},{8,9},{9,8},{10,11... | collective-permute-start | bytes 786440 | tf_op jit(solution)/shard_map/ppermute | solution.py:22
  43.9 6.5 %collective-permute-done.2 = bf16[1024,128]{1,0:T(8,128)(2,1)S(1)} collective-permute-done((bf16[1024,128]{1,0:T(8,128)(2,1)S(1)}, bf16[1024,128]{1,0:T(8,128)(2,1)S(1)}, u32[]{:S(2)}, u32[]{:S(2)}) %collective-permute-start.2) | collective-permute-done | bytes 262176 | tf_op jit(solution)/shard_map/ppermute | solution.py:22
  50.4 0.6 fusion.88
  51.0 0.6 fusion.73
  51.7 1.3 copy-done.20
  53.0 0.6 fusion.79
  53.6 0.7 copy-done.12
  54.3 0.5 convolution_convert_fusion.2
  54.8 4.0 %collective-permute-start.3 = (bf16[896,128]{1,0:T(8,128)(2,1)S(1)}, bf16[896,128]{1,0:T(8,128)(2,1)S(1)}, u32[]{:S(2)}, u32[]{:S(2)}) collective-permute-start(bf16[896,128]{1,0:T(8,128)(2,1)S(1)} %fusion.88), channel_id=1, source_target_pairs={{0,1},{2,3},{4,5},{6,7},{8,9},{10,11},{12,13},{14,15},{16,17},{18,... | collective-permute-start | bytes 688136 | tf_op jit(solution)/shard_map/ppermute | solution.py:22
  59.0 2.2 %collective-permute-start.6 = (bf16[1024,128]{1,0:T(8,128)(2,1)S(1)}, bf16[1024,128]{1,0:T(8,128)(2,1)S(1)}, u32[]{:S(2)}, u32[]{:S(2)}) collective-permute-start(bf16[1024,128]{1,0:T(8,128)(2,1)S(1)} %fusion.79), channel_id=1, source_target_pairs={{0,1},{1,0},{2,3},{3,2},{4,5},{5,4},{6,7},{7,6},{8,9},{9,8},{10,11... | collective-permute-start | bytes 786440 | tf_op jit(solution)/shard_map/ppermute | solution.py:22
  61.3 5.4 %collective-permute-done.3 = bf16[896,128]{1,0:T(8,128)(2,1)S(1)} collective-permute-done((bf16[896,128]{1,0:T(8,128)(2,1)S(1)}, bf16[896,128]{1,0:T(8,128)(2,1)S(1)}, u32[]{:S(2)}, u32[]{:S(2)}) %collective-permute-start.3) | collective-permute-done | bytes 229408 | tf_op jit(solution)/shard_map/ppermute | solution.py:22
  66.6 0.6 fusion.76
  67.2 0.5 convolution_convert_fusion.3
  68.0 0.6 fusion.34.refs_0_
  68.6 4.7 %collective-permute-done.6.refs_1_ = bf16[1024,128]{1,0:T(8,128)(2,1)S(1)} collective-permute-done((bf16[1024,128]{1,0:T(8,128)(2,1)S(1)}, bf16[1024,128]{1,0:T(8,128)(2,1)S(1)}, u32[]{:S(2)}, u32[]{:S(2)}) %collective-permute-start.6) | collective-permute-done | bytes 262176 | tf_op jit(solution)/shard_map/ppermute | solution.py:22
  73.3 1.3 collective-permute-done.9.refs_4_
  74.9 2.5 %operate_second.1 = (f32[1024,128]{1,0:T(8,128)S(1)}, f32[1024,128]{1,0:T(8,128)S(1)}, f32[16,2,128]{2,1,0:T(2,128)S(1)}) custom-call(f32[1024,128]{1,0:T(8,128)S(1)} %fusion.34.refs_0_, bf16[1024,128]{1,0:T(8,128)(2,1)S(1)} %collective-permute-done.6.refs_1_, bf16[384,128]{1,0:T(8,128)(2,1)S(1)} %collective-permute-done.7.refs_2_, ...), custom_call_target="tpu_custom_call" | custom-call | flops 469762048 | bytes 3670016 | tf_op jit(solution)/shard_map/operate_second/pallas_call | solution.py:131
  77.4 9.1 %all_to_all.15.refs_0_ = f32[16,2,128]{2,1,0:T(2,128)S(1)} all-to-all(f32[16,2,128]{2,1,0:T(2,128)S(1)} %get-tuple-element.40), channel_id=1, replica_groups=mesh['sub'=16,'panel'=2] {'sub'}, dimensions={0} | all-to-all | bytes 32768 | tf_op jit(solution)/shard_map/all_to_all | solution.py:299
  86.5 0.6 shard_map.176
  87.1 4.0 %collective-permute-start.15 = (bf16[384,128]{1,0:T(8,128)(2,1)S(1)}, bf16[384,128]{1,0:T(8,128)(2,1)S(1)}, u32[]{:S(2)}, u32[]{:S(2)}) collective-permute-start(bf16[384,128]{1,0:T(8,128)(2,1)S(1)} %get-tuple-element.65), channel_id=1, source_target_pairs={{0,31},{2,5},{4,3},{6,9},{8,7},{10,13},{12,11},{14,17},{16,15},{18... | collective-permute-start | bytes 294920 | tf_op jit(solution)/shard_map/ppermute | solution.py:22
  91.2 0.7 collective-permute-start.11
  91.8 3.1 %collective-permute-start.16 = (bf16[384,128]{1,0:T(8,128)(2,1)S(1)}, bf16[384,128]{1,0:T(8,128)(2,1)S(1)}, u32[]{:S(2)}, u32[]{:S(2)}) collective-permute-start(bf16[384,128]{1,0:T(8,128)(2,1)S(1)} %get-tuple-element.66), channel_id=1, source_target_pairs={{0,3},{2,1},{4,7},{6,5},{8,11},{10,9},{12,15},{14,13},{16,19},{18,... | collective-permute-start | bytes 294920 | tf_op jit(solution)/shard_map/ppermute | solution.py:22
  94.9 0.8 collective-permute-start.12
  95.8 0.6 fusion.91
  96.5 1.1 collective-permute-start.13
  97.6 1.3 collective-permute-done.16
  98.9 6.0 %collective-permute-done.13 = bf16[1024,128]{1,0:T(8,128)(2,1)S(1)} collective-permute-done((bf16[1024,128]{1,0:T(8,128)(2,1)S(1)}, bf16[1024,128]{1,0:T(8,128)(2,1)S(1)}, u32[]{:S(2)}, u32[]{:S(2)}) %collective-permute-start.13) | collective-permute-done | bytes 262176 | tf_op jit(solution)/shard_map/ppermute | solution.py:22
  104.9 0.6 fusion.67
  105.5 0.5 convolution_convert_fusion
  106.1 3.4 %collective-permute-start.21 = (bf16[384,128]{1,0:T(8,128)(2,1)S(1)}, bf16[384,128]{1,0:T(8,128)(2,1)S(1)}, u32[]{:S(2)}, u32[]{:S(2)}) collective-permute-start(bf16[384,128]{1,0:T(8,128)(2,1)S(1)} %get-tuple-element.57), channel_id=1, source_target_pairs={{0,31},{1,30},{2,5},{3,4},{4,3},{5,2},{6,9},{7,8},{8,7},{9,6},{10,... | collective-permute-start | bytes 294920 | tf_op jit(solution)/shard_map/ppermute | solution.py:22
  109.5 0.6 fusion.94
  110.1 2.1 %collective-permute-start.14 = (bf16[896,128]{1,0:T(8,128)(2,1)S(1)}, bf16[896,128]{1,0:T(8,128)(2,1)S(1)}, u32[]{:S(2)}, u32[]{:S(2)}) collective-permute-start(bf16[896,128]{1,0:T(8,128)(2,1)S(1)} %fusion.94), channel_id=1, source_target_pairs={{0,1},{2,3},{4,5},{6,7},{8,9},{10,11},{12,13},{14,15},{16,17},{18,... | collective-permute-start | bytes 688136 | tf_op jit(solution)/shard_map/ppermute | solution.py:22
  112.2 0.7 fusion.82
  112.9 4.9 %collective-permute-done.14 = bf16[896,128]{1,0:T(8,128)(2,1)S(1)} collective-permute-done((bf16[896,128]{1,0:T(8,128)(2,1)S(1)}, bf16[896,128]{1,0:T(8,128)(2,1)S(1)}, u32[]{:S(2)}, u32[]{:S(2)}) %collective-permute-start.14) | collective-permute-done | bytes 229408 | tf_op jit(solution)/shard_map/ppermute | solution.py:22
  117.8 0.6 fusion.70
  118.4 0.5 convolution_convert_fusion.1
  119.0 3.1 %collective-permute-start.20 = (bf16[384,128]{1,0:T(8,128)(2,1)S(1)}, bf16[384,128]{1,0:T(8,128)(2,1)S(1)}, u32[]{:S(2)}, u32[]{:S(2)}) collective-permute-start(bf16[384,128]{1,0:T(8,128)(2,1)S(1)} %get-tuple-element.59), channel_id=1, source_target_pairs={{0,30},{1,31},{2,4},{3,5},{4,2},{5,3},{6,8},{7,9},{8,6},{9,7},{10,... | collective-permute-start | bytes 294920 | tf_op jit(solution)/shard_map/ppermute | solution.py:22
  122.1 0.6 fusion.31.refs_0_
  122.7 0.7 collective-permute-done.17.refs_1_
  123.4 2.3 %collective-permute-done.20.refs_4_ = bf16[384,128]{1,0:T(8,128)(2,1)S(1)} collective-permute-done((bf16[384,128]{1,0:T(8,128)(2,1)S(1)}, bf16[384,128]{1,0:T(8,128)(2,1)S(1)}, u32[]{:S(2)}, u32[]{:S(2)}) %collective-permute-start.20) | collective-permute-done | bytes 98336 | tf_op jit(solution)/shard_map/ppermute | solution.py:22
  125.8 2.6 %operate_closing.1 = (f32[1024,128]{1,0:T(8,128)S(1)}, f32[1024,128]{1,0:T(8,128)S(1)}, f32[16,4,128]{2,1,0:T(4,128)S(1)}) custom-call(f32[1024,128]{1,0:T(8,128)S(1)} %fusion.31.refs_0_, bf16[1024,128]{1,0:T(8,128)(2,1)S(1)} %collective-permute-done.17.refs_1_, bf16[384,128]{1,0:T(8,128)(2,1)S(1)} %collective-permute-done.18.refs_2_, ...), custom_call_target="tpu_custom_call" | custom-call | flops 469762048 | bytes 3670016 | tf_op jit(solution)/shard_map/operate_closing/pallas_call | solution.py:131
  128.4 10.8 %all_to_all.16 = f32[16,4,128]{2,1,0:T(4,128)S(1)} all-to-all(f32[16,4,128]{2,1,0:T(4,128)S(1)} %get-tuple-element.48), channel_id=1, replica_groups=mesh['sub'=16,'panel'=2] {'sub'}, dimensions={0} | all-to-all | bytes 65536 | tf_op jit(solution)/shard_map/all_to_all | solution.py:299
  139.3 0.5 fusion.140
  139.8 2.3 %multiply_subtract_fusion = (f32[1024,128]{1,0:T(8,128)}, f32[1024,128]{1,0:T(8,128)}) fusion(f32[1024,128]{1,0:T(8,128)} %copy-done.5, f32[1024,128]{1,0:T(8,128)S(1)} %get-tuple-element.50, f32[128]{0:T(128)S(1)} %get-tuple-element.56, f32[1024,128]{1,0:T(8,128)S(1)} %get-tuple-element.49, f32[1024,128]{1,0:T(8,128)} %param.14, ...), kind=kLoop, calls=%fused_computation.69 | loop fusion | flops 786432 | bytes 3671040 | tf_op jit(solution)/shard_map/sub | solution.py:331
  (80 shorter events, 1.4 us)
Async XLA Ops:
  2.6 23.6 %all-to-all-start = ((f32[16,2,128]{2,1,0:T(2,128)}), f32[16,2,128]{2,1,0:T(2,128)S(1)}, u32[]{:S(2)}, u32[]{:S(2)}) async-start(f32[16,2,128]{2,1,0:T(2,128)} %broadcast_in_dim.8), calls=%async_computation | async-start | bytes 32768 | tf_op jit(solution)/shard_map/all_to_all | solution.py:299
  12.0 4.5 %copy-start.10 = (f32[16,1024]{1,0:T(8,128)S(1)}, f32[16,1024]{1,0:T(8,128)}, u32[]{:S(2)}) copy-start(f32[16,1024]{1,0:T(8,128)} %weight_ref.3) | copy-start | bytes 196612
  16.5 3.9 %copy-start.16 = (f32[128]{0:T(128)S(1)}, f32[128]{0:T(128)}, u32[]{:S(2)}) copy-start(f32[128]{0:T(128)} %param.21) | copy-start | bytes 1540
  16.5 3.9 %copy-start.17 = (f32[128]{0:T(128)S(1)}, f32[128]{0:T(128)}, u32[]{:S(2)}) copy-start(f32[128]{0:T(128)} %param.20) | copy-start | bytes 1540
  16.5 3.9 %copy-start.18 = (f32[128]{0:T(128)S(1)}, f32[128]{0:T(128)}, u32[]{:S(2)}) copy-start(f32[128]{0:T(128)} %param.19) | copy-start | bytes 1540
  24.9 1.3 copy-start
  26.2 1.0 copy-start.3
  27.2 1.0 copy-start.6
  28.3 1.0 copy-start.7
  29.3 0.7 copy-start.11
  30.0 10.6 %copy-start.19 = (bf16[1,1792,896]{2,1,0:T(8,128)(2,1)S(1)}, bf16[1,1792,896]{2,1,0:T(8,128)(2,1)}, u32[]{:S(2)}) copy-start(bf16[1,1792,896]{2,1,0:T(8,128)(2,1)} %param.22) | copy-start | bytes 9633796
  30.6 13.2 %collective-permute-start.4 = (bf16[384,128]{1,0:T(8,128)(2,1)S(1)}, bf16[384,128]{1,0:T(8,128)(2,1)S(1)}, u32[]{:S(2)}, u32[]{:S(2)}) collective-permute-start(bf16[384,128]{1,0:T(8,128)(2,1)S(1)} %get-tuple-element.75), channel_id=1, source_target_pairs={{0,31},{2,5},{4,3},{6,9},{8,7},{10,13},{12,11},{14,17},{16,15},{18... | collective-permute-start | bytes 294920 | tf_op jit(solution)/shard_map/ppermute | solution.py:22
  38.0 5.9 %collective-permute-start = (bf16[384,128]{1,0:T(8,128)(2,1)S(1)}, bf16[384,128]{1,0:T(8,128)(2,1)S(1)}, u32[]{:S(2)}, u32[]{:S(2)}) collective-permute-start(bf16[384,128]{1,0:T(8,128)(2,1)S(1)} %get-tuple-element.75), channel_id=1, source_target_pairs={{1,31},{3,5},{5,3},{7,9},{9,7},{11,13},{13,11},{15,17},{17,15},{19... | collective-permute-start | bytes 294920 | tf_op jit(solution)/shard_map/ppermute | solution.py:22
  38.6 5.2 %collective-permute-start.5 = (bf16[384,128]{1,0:T(8,128)(2,1)S(1)}, bf16[384,128]{1,0:T(8,128)(2,1)S(1)}, u32[]{:S(2)}, u32[]{:S(2)}) collective-permute-start(bf16[384,128]{1,0:T(8,128)(2,1)S(1)} %get-tuple-element.76), channel_id=1, source_target_pairs={{0,3},{2,1},{4,7},{6,5},{8,11},{10,9},{12,15},{14,13},{16,19},{18,... | collective-permute-start | bytes 294920 | tf_op jit(solution)/shard_map/ppermute | solution.py:22
  39.9 3.9 %collective-permute-start.1 = (bf16[384,128]{1,0:T(8,128)(2,1)S(1)}, bf16[384,128]{1,0:T(8,128)(2,1)S(1)}, u32[]{:S(2)}, u32[]{:S(2)}) collective-permute-start(bf16[384,128]{1,0:T(8,128)(2,1)S(1)} %get-tuple-element.76), channel_id=1, source_target_pairs={{1,3},{3,1},{5,7},{7,5},{9,11},{11,9},{13,15},{15,13},{17,19},{19,... | collective-permute-start | bytes 294920 | tf_op jit(solution)/shard_map/ppermute | solution.py:22
  41.3 9.1 %collective-permute-start.2 = (bf16[1024,128]{1,0:T(8,128)(2,1)S(1)}, bf16[1024,128]{1,0:T(8,128)(2,1)S(1)}, u32[]{:S(2)}, u32[]{:S(2)}) collective-permute-start(bf16[1024,128]{1,0:T(8,128)(2,1)S(1)} %maximum_select_fusion), channel_id=1, source_target_pairs={{0,1},{1,0},{2,3},{3,2},{4,5},{5,4},{6,7},{7,6},{8,9},{9,8},{10,11... | collective-permute-start | bytes 786440 | tf_op jit(solution)/shard_map/ppermute | solution.py:22
  51.0 1.9 %copy-start.20 = (bf16[1,1792,896]{2,1,0:T(8,128)(2,1)S(1)}, bf16[1,1792,896]{2,1,0:T(8,128)(2,1)}, u32[]{:S(2)}) copy-start(bf16[1,1792,896]{2,1,0:T(8,128)(2,1)} %param.23) | copy-start | bytes 9633796
  52.9 1.3 copy-start.12
  54.3 7.0 %copy-start.13 = (f32[1024]{0:T(1024)S(1)}, f32[1024]{0:T(1024)}, u32[]{:S(2)}) copy-start(f32[1024]{0:T(1024)} %param.26) | copy-start | bytes 12292
  54.8 11.8 %collective-permute-start.3 = (bf16[896,128]{1,0:T(8,128)(2,1)S(1)}, bf16[896,128]{1,0:T(8,128)(2,1)S(1)}, u32[]{:S(2)}, u32[]{:S(2)}) collective-permute-start(bf16[896,128]{1,0:T(8,128)(2,1)S(1)} %fusion.88), channel_id=1, source_target_pairs={{0,1},{2,3},{4,5},{6,7},{8,9},{10,11},{12,13},{14,15},{16,17},{18,... | collective-permute-start | bytes 688136 | tf_op jit(solution)/shard_map/ppermute | solution.py:22
  58.9 14.4 %collective-permute-start.10 = (bf16[384,128]{1,0:T(8,128)(2,1)S(1)}, bf16[384,128]{1,0:T(8,128)(2,1)S(1)}, u32[]{:S(2)}, u32[]{:S(2)}) collective-permute-start(bf16[384,128]{1,0:T(8,128)(2,1)S(1)} %get-tuple-element.67), channel_id=1, source_target_pairs={{0,31},{1,30},{2,5},{3,4},{4,3},{5,2},{6,9},{7,8},{8,7},{9,6},{10,... | collective-permute-start | bytes 294920 | tf_op jit(solution)/shard_map/ppermute | solution.py:22
  58.9 14.4 %collective-permute-start.8 = (bf16[384,128]{1,0:T(8,128)(2,1)S(1)}, bf16[384,128]{1,0:T(8,128)(2,1)S(1)}, u32[]{:S(2)}, u32[]{:S(2)}) collective-permute-start(bf16[384,128]{1,0:T(8,128)(2,1)S(1)} %get-tuple-element.68), channel_id=1, source_target_pairs={{0,3},{1,2},{2,1},{3,0},{4,7},{5,6},{6,5},{7,4},{8,11},{9,10},{10,... | collective-permute-start | bytes 294920 | tf_op jit(solution)/shard_map/ppermute | solution.py:22
  59.0 14.3 %collective-permute-start.6 = (bf16[1024,128]{1,0:T(8,128)(2,1)S(1)}, bf16[1024,128]{1,0:T(8,128)(2,1)S(1)}, u32[]{:S(2)}, u32[]{:S(2)}) collective-permute-start(bf16[1024,128]{1,0:T(8,128)(2,1)S(1)} %fusion.79), channel_id=1, source_target_pairs={{0,1},{1,0},{2,3},{3,2},{4,5},{5,4},{6,7},{7,6},{8,9},{9,8},{10,11... | collective-permute-start | bytes 786440 | tf_op jit(solution)/shard_map/ppermute | solution.py:22
  67.8 7.0 %copy-start.1 = (bf16[512,1792]{1,0:T(8,128)(2,1)S(1)}, bf16[512,1792]{1,0:T(8,128)(2,1)}, u32[]{:S(2)}) copy-start(bf16[512,1792]{1,0:T(8,128)(2,1)} %copy-done) | copy-start | bytes 5505028
  67.8 7.0 %copy-start.2 = (f32[1024,128]{1,0:T(8,128)S(1)}, f32[1024,128]{1,0:T(8,128)}, u32[]{:S(2)}) copy-start(f32[1024,128]{1,0:T(8,128)} %refs_7_.3) | copy-start | bytes 1572868
  67.8 6.8 %collective-permute-start.9 = (bf16[384,128]{1,0:T(8,128)(2,1)S(1)}, bf16[384,128]{1,0:T(8,128)(2,1)S(1)}, u32[]{:S(2)}, u32[]{:S(2)}) collective-permute-start(bf16[384,128]{1,0:T(8,128)(2,1)S(1)} %get-tuple-element.69), channel_id=1, source_target_pairs={{0,30},{1,31},{2,4},{3,5},{4,2},{5,3},{6,8},{7,9},{8,6},{9,7},{10,... | collective-permute-start | bytes 294920 | tf_op jit(solution)/shard_map/ppermute | solution.py:22
  67.9 6.7 %collective-permute-start.7 = (bf16[384,128]{1,0:T(8,128)(2,1)S(1)}, bf16[384,128]{1,0:T(8,128)(2,1)S(1)}, u32[]{:S(2)}, u32[]{:S(2)}) collective-permute-start(bf16[384,128]{1,0:T(8,128)(2,1)S(1)} %get-tuple-element.70), channel_id=1, source_target_pairs={{0,2},{1,3},{2,0},{3,1},{4,6},{5,7},{6,4},{7,5},{8,10},{9,11},{10,... | collective-permute-start | bytes 294920 | tf_op jit(solution)/shard_map/ppermute | solution.py:22
  74.8 11.6 %copy-start.4 = (f32[1024,128]{1,0:T(8,128)S(1)}, f32[1024,128]{1,0:T(8,128)}, u32[]{:S(2)}) copy-start(f32[1024,128]{1,0:T(8,128)} %refs_2_.3) | copy-start | bytes 1572868
  77.4 19.0 %copy-start.8 = (f32[1024,128]{1,0:T(8,128)}, f32[1024,128]{1,0:T(8,128)S(1)}, u32[]{:S(2)}) copy-start(f32[1024,128]{1,0:T(8,128)S(1)} %get-tuple-element.44) | copy-start | bytes 1572868
  87.1 38.7 %copy-start.5 = (f32[1024,128]{1,0:T(8,128)}, f32[1024,128]{1,0:T(8,128)S(1)}, u32[]{:S(2)}) copy-start(f32[1024,128]{1,0:T(8,128)S(1)} %get-tuple-element.47.refs_8_) | copy-start | bytes 1572868
  87.1 10.4 %collective-permute-start.15 = (bf16[384,128]{1,0:T(8,128)(2,1)S(1)}, bf16[384,128]{1,0:T(8,128)(2,1)S(1)}, u32[]{:S(2)}, u32[]{:S(2)}) collective-permute-start(bf16[384,128]{1,0:T(8,128)(2,1)S(1)} %get-tuple-element.65), channel_id=1, source_target_pairs={{0,31},{2,5},{4,3},{6,9},{8,7},{10,13},{12,11},{14,17},{16,15},{18... | collective-permute-start | bytes 294920 | tf_op jit(solution)/shard_map/ppermute | solution.py:22
  91.2 7.7 %collective-permute-start.11 = (bf16[384,128]{1,0:T(8,128)(2,1)S(1)}, bf16[384,128]{1,0:T(8,128)(2,1)S(1)}, u32[]{:S(2)}, u32[]{:S(2)}) collective-permute-start(bf16[384,128]{1,0:T(8,128)(2,1)S(1)} %get-tuple-element.65), channel_id=1, source_target_pairs={{1,31},{3,5},{5,3},{7,9},{9,7},{11,13},{13,11},{15,17},{17,15},{19... | collective-permute-start | bytes 294920 | tf_op jit(solution)/shard_map/ppermute | solution.py:22
  91.8 7.0 %collective-permute-start.16 = (bf16[384,128]{1,0:T(8,128)(2,1)S(1)}, bf16[384,128]{1,0:T(8,128)(2,1)S(1)}, u32[]{:S(2)}, u32[]{:S(2)}) collective-permute-start(bf16[384,128]{1,0:T(8,128)(2,1)S(1)} %get-tuple-element.66), channel_id=1, source_target_pairs={{0,3},{2,1},{4,7},{6,5},{8,11},{10,9},{12,15},{14,13},{16,19},{18,... | collective-permute-start | bytes 294920 | tf_op jit(solution)/shard_map/ppermute | solution.py:22
  94.9 4.0 %collective-permute-start.12 = (bf16[384,128]{1,0:T(8,128)(2,1)S(1)}, bf16[384,128]{1,0:T(8,128)(2,1)S(1)}, u32[]{:S(2)}, u32[]{:S(2)}) collective-permute-start(bf16[384,128]{1,0:T(8,128)(2,1)S(1)} %get-tuple-element.66), channel_id=1, source_target_pairs={{1,3},{3,1},{5,7},{7,5},{9,11},{11,9},{13,15},{15,13},{17,19},{19,... | collective-permute-start | bytes 294920 | tf_op jit(solution)/shard_map/ppermute | solution.py:22
  96.5 8.4 %collective-permute-start.13 = (bf16[1024,128]{1,0:T(8,128)(2,1)S(1)}, bf16[1024,128]{1,0:T(8,128)(2,1)S(1)}, u32[]{:S(2)}, u32[]{:S(2)}) collective-permute-start(bf16[1024,128]{1,0:T(8,128)(2,1)S(1)} %maximum_select_fusion.1), channel_id=1, source_target_pairs={{0,1},{1,0},{2,3},{3,2},{4,5},{5,4},{6,7},{7,6},{8,9},{9,8},{10,11... | collective-permute-start | bytes 786440 | tf_op jit(solution)/shard_map/ppermute | solution.py:22
  106.1 16.7 %collective-permute-start.21 = (bf16[384,128]{1,0:T(8,128)(2,1)S(1)}, bf16[384,128]{1,0:T(8,128)(2,1)S(1)}, u32[]{:S(2)}, u32[]{:S(2)}) collective-permute-start(bf16[384,128]{1,0:T(8,128)(2,1)S(1)} %get-tuple-element.57), channel_id=1, source_target_pairs={{0,31},{1,30},{2,5},{3,4},{4,3},{5,2},{6,9},{7,8},{8,7},{9,6},{10,... | collective-permute-start | bytes 294920 | tf_op jit(solution)/shard_map/ppermute | solution.py:22
  109.5 13.3 %collective-permute-start.19 = (bf16[384,128]{1,0:T(8,128)(2,1)S(1)}, bf16[384,128]{1,0:T(8,128)(2,1)S(1)}, u32[]{:S(2)}, u32[]{:S(2)}) collective-permute-start(bf16[384,128]{1,0:T(8,128)(2,1)S(1)} %get-tuple-element.58), channel_id=1, source_target_pairs={{0,3},{1,2},{2,1},{3,0},{4,7},{5,6},{6,5},{7,4},{8,11},{9,10},{10,... | collective-permute-start | bytes 294920 | tf_op jit(solution)/shard_map/ppermute | solution.py:22
  110.1 7.7 %collective-permute-start.14 = (bf16[896,128]{1,0:T(8,128)(2,1)S(1)}, bf16[896,128]{1,0:T(8,128)(2,1)S(1)}, u32[]{:S(2)}, u32[]{:S(2)}) collective-permute-start(bf16[896,128]{1,0:T(8,128)(2,1)S(1)} %fusion.94), channel_id=1, source_target_pairs={{0,1},{2,3},{4,5},{6,7},{8,9},{10,11},{12,13},{14,15},{16,17},{18,... | collective-permute-start | bytes 688136 | tf_op jit(solution)/shard_map/ppermute | solution.py:22
  112.8 10.6 %collective-permute-start.17 = (bf16[1024,128]{1,0:T(8,128)(2,1)S(1)}, bf16[1024,128]{1,0:T(8,128)(2,1)S(1)}, u32[]{:S(2)}, u32[]{:S(2)}) collective-permute-start(bf16[1024,128]{1,0:T(8,128)(2,1)S(1)} %fusion.82), channel_id=1, source_target_pairs={{0,1},{1,0},{2,3},{3,2},{4,5},{5,4},{6,7},{7,6},{8,9},{9,8},{10,11... | collective-permute-start | bytes 786440 | tf_op jit(solution)/shard_map/ppermute | solution.py:22
  119.0 6.8 %collective-permute-start.20 = (bf16[384,128]{1,0:T(8,128)(2,1)S(1)}, bf16[384,128]{1,0:T(8,128)(2,1)S(1)}, u32[]{:S(2)}, u32[]{:S(2)}) collective-permute-start(bf16[384,128]{1,0:T(8,128)(2,1)S(1)} %get-tuple-element.59), channel_id=1, source_target_pairs={{0,30},{1,31},{2,4},{3,5},{4,2},{5,3},{6,8},{7,9},{8,6},{9,7},{10,... | collective-permute-start | bytes 294920 | tf_op jit(solution)/shard_map/ppermute | solution.py:22
  122.1 3.7 %collective-permute-start.18 = (bf16[384,128]{1,0:T(8,128)(2,1)S(1)}, bf16[384,128]{1,0:T(8,128)(2,1)S(1)}, u32[]{:S(2)}, u32[]{:S(2)}) collective-permute-start(bf16[384,128]{1,0:T(8,128)(2,1)S(1)} %get-tuple-element.60), channel_id=1, source_target_pairs={{0,2},{1,3},{2,0},{3,1},{4,6},{5,7},{6,4},{7,5},{8,10},{9,11},{10,... | collective-permute-start | bytes 294920 | tf_op jit(solution)/shard_map/ppermute | solution.py:22
  125.8 14.0 %copy-start.9 = (f32[1024,128]{1,0:T(8,128)S(1)}, f32[1024,128]{1,0:T(8,128)}, u32[]{:S(2)}) copy-start(f32[1024,128]{1,0:T(8,128)} %copy-done.8) | copy-start | bytes 1572868
  125.8 14.0 %copy-start.15 = (f32[1,128]{1,0:T(1,128)S(1)}, f32[1,128]{1,0:T(1,128)}, u32[]{:S(2)}) copy-start(f32[1,128]{1,0:T(1,128)} %get-tuple-element.43) | copy-start | bytes 1540
  139.8 2.3 %copy-start.14 = (f32[128]{0:T(128)}, f32[128]{0:T(128)S(1)}, u32[]{:S(2)}) copy-start(f32[128]{0:T(128)S(1)} %get-tuple-element.56) | copy-start | bytes 1540

commit v4 on v2

--- a/solution.py
+++ b/solution.py
@@ -163,6 +163,13 @@
     pl.when(panel[0] != 0)(lambda: put(payload_ref, mine_ref))
 
 
+def opening_kernel(panel, shadow, residual, sums_ref):
+    left = shadow[...]
+    pairs = (left * residual[...], left * left)
+    sums = jnp.concatenate([jnp.sum(p, axis=0, keepdims=True) for p in pairs], axis=0)
+    sums_ref[...] = jnp.broadcast_to(sums[None], sums_ref.shape)
+
+
 def direction_kernel(node_count, panel, sums, past, residual, direction, old_image, select, *outs):
     means_ref, mine_ref, payload_ref = outs
     means = jnp.sum(sums[...], axis=0) / node_count
@@ -234,14 +241,12 @@
     tail = own - half
 
     blocks = own // 128
-    cuts = (0, blocks // 2, blocks)
+    cuts = (0, blocks // 4, 5 * blocks // 8, blocks)
     coupling = []
 
-    def next_coupling(trigger):
+    def next_coupling():
         begin, end = cuts[len(coupling) : len(coupling) + 2]
-        trigger, links = lax.optimization_barrier((trigger, neighbours))
         coupling.append(coupling_rows(links, edge_weight, ext, begin, end - begin))
-        return trigger
 
     def meet(arrived, value):
         return lax.optimization_barrier((arrived, value))
@@ -251,10 +256,6 @@
     def by_parity(zero, one):
         return jnp.where(even, zero, one)
 
-    turned = jnp.where(neighbours < own + border, neighbours + border, neighbours - border)
-    ghost = even & (neighbours >= own) & (neighbours < ext)
-    neighbours = jnp.where(ghost, turned, neighbours)
-    near_far = by_parity(send_rows[0, ::-1], send_rows[0])
     rows = lax.broadcasted_iota(jnp.int32, (1, own), 1)
 
     def by_panel(zero, one):
@@ -264,28 +265,26 @@
 
     def precondition(mine, payload, chosen_upper):
         build = chosen_upper is None
-        if build:
-            payload = next_coupling(payload)
         received = send(payload, lambda s, p: (s, 1 - p))
         early = matmul(lower[half:], mine).astype(jnp.bfloat16)
         passed_others = send(early, lambda s, p: (s, 1) if p == 0 else None)
         if build:
+            next_coupling()
             received, coupling[-1] = meet(received, coupling[-1])
+        near_rows, far_rows = slice(tail, tail + border), slice(tail + border, half)
+
+        def both(part):
+            return jnp.concatenate([received[part], mine[part]], axis=1)
+
+        from_far = send(both(far_rows), lambda s, p: (far(s), 1) if p == 1 else None)
+        from_near = send(both(near_rows), lambda s, p: (near(s), 1) if p == 1 else None)
         late = matmul(lower[half:], received).astype(jnp.bfloat16)
         if build:
-            late, chosen = lax.optimization_barrier((next_coupling(late), select))
+            late, chosen = lax.optimization_barrier((late, select))
             chosen_upper = matmul(chosen, upper).astype(jnp.bfloat16)
         passed_mine = send(late, lambda s, p: (s, 1) if p == 0 else None)
-        near_rows, far_rows = slice(tail, tail + border), slice(tail + border, half)
-
-        def both(part):
-            return jnp.concatenate([received[part], mine[part]], axis=1)
-
-        from_far = send(both(far_rows), lambda s, p: (far(s), 1) if p == 1 else None)
-        from_near = send(both(near_rows), lambda s, p: (near(s), 1) if p == 1 else None)
-        if build:
-            passed_mine, coupling[-1] = meet(passed_mine, coupling[-1])
-            passed_mine, chosen_upper = meet(passed_mine, chosen_upper)
+        if build:
+            from_far, chosen_upper = meet(from_far, chosen_upper)
         from_lower, from_upper = by_parity(from_far, from_near), by_parity(from_near, from_far)
 
         def solve(kept, ghost_columns, passed):
@@ -296,20 +295,23 @@
 
         others = solve(received, slice(0, cols), passed_others)
         if build:
-            others, links = lax.optimization_barrier((others, neighbours))
-            present = jnp.where(links < ext, edge_weight, 0.0)
+            others, listed = lax.optimization_barrier((others, neighbours))
+            present = jnp.where(listed < ext, edge_weight, 0.0)
             scale = jnp.broadcast_to((node_shift + jnp.sum(present, axis=0))[:, None], (own, cols))
             diagonal.append(scale)
         other_part = matmul(upper, others).astype(jnp.bfloat16)
         swapped = send(other_part, lambda s, p: (s, 1 - p))
-        mine = solve(mine, slice(cols, 2 * cols), passed_mine)
         other_edge = matmul(chosen_upper, others).astype(jnp.bfloat16)
         cross_far = send(other_edge[border:], lambda s, p: (far(s), 1 - p))
+        cross_near = send(other_edge[:border], lambda s, p: (near(s), 1 - p))
+        mine = solve(mine, slice(cols, 2 * cols), passed_mine)
         edge = matmul(chosen_upper, mine).astype(jnp.bfloat16)
         part = matmul(upper, mine)
         same_far = send(edge[border:], lambda s, p: (far(s), p))
-        cross_near = send(other_edge[:border], lambda s, p: (near(s), 1 - p))
         same_near = send(edge[:border], lambda s, p: (near(s), p))
+        if build:
+            next_coupling()
+            swapped, coupling[-1] = meet(swapped, coupling[-1])
         return (part, swapped, same_near, cross_near, same_far, cross_far), chosen_upper
 
     copies = lax.axis_size("sub")
@@ -320,15 +322,25 @@
     diagonal = []
     vector = jax.ShapeDtypeStruct((own, cols), jnp.float32)
     panel_rows = jax.ShapeDtypeStruct((half, cols), jnp.bfloat16)
-    sums = jnp.stack([jnp.sum(shadow * residual, axis=0), jnp.sum(shadow * shadow, axis=0)])
-    sums = jnp.broadcast_to(sums[None], (copies, 2, cols))
-    sums, near_far = lax.optimization_barrier((sums, near_far))
-    select = (near_far.reshape(2 * border, 1) == rows).astype(jnp.bfloat16)
+    (sums,) = small_call(
+        opening_kernel,
+        panel,
+        (shadow, residual),
+        [jax.ShapeDtypeStruct((copies, 2, cols), jnp.float32)],
+    )
+    sums, lists, links = lax.optimization_barrier((sums, send_rows, neighbours))
+    turned = jnp.where(links < own + border, links + border, links - border)
+    ghost = even & (links >= own) & (links < ext)
+    links = jnp.where(ghost, turned, links)
+    next_coupling()
+    opening_sums, coupling[-1] = meet(exchange(sums), coupling[-1])
+    near_far = [by_parity(lists[0, 1], lists[0, 0]), by_parity(lists[0, 0], lists[0, 1])]
+    select = (jnp.concatenate(near_far)[:, None] == rows).astype(jnp.bfloat16)
     past = jnp.stack([rho_prev, alpha_prev, omega_prev])
     opening, mine, payload = small_call(
         lambda *refs: direction_kernel(node_count, *refs),
         panel,
-        (exchange(sums), past, residual, direction, old_image, select),
+        (opening_sums, past, residual, direction, old_image, select),
         [jax.ShapeDtypeStruct((2, cols), jnp.float32), panel_rows, panel_rows],
     )
     parts, chosen_upper = precondition(mine, payload, None)

time: 133 us -> 146 us (1.098)
  local copies, waits for them, and re-layouts: 3.87 us -> 10.3 us
  starting transfers between devices: 46.6 us -> 50.1 us
  Pallas kernels: 14.7 us -> 16.5 us
    unnamed x32 -> x52, local copies, waits for them, and re-layouts: 1.31 us -> 9.88 us
    ppermute x20, waiting for transfers between devices: 24.4 us -> 29.8 us  [send(): return lax.ppermute(values, AXES, pairs)]
    all_to_all x1, waiting for transfers between devices: 5.23 us -> 0.01 us  [exchange(): return lax.all_to_all(values, 'sub', 0, 0)]
    ppermute x20, starting transfers between devices: 39.1 us -> 42.7 us  [send(): return lax.ppermute(values, AXES, pairs)]
    rev x1 -> x0, local copies, waits for them, and re-layouts: 1.51 us -> none  [per_device(): near_far = by_parity(send_rows[0, ::-1], send_rows[0])]
    pallas_call x2 -> x3, Pallas kernels: 7.81 us -> 7.78 us  [coupling_rows(): pl.pallas_call(coupling_kernel, grid=(count,), in_specs=[pl.BlockSpec((sl...]
  transfers between devices with their start and end apart: 21 -> 21, of which waited for: 8 -> 5; matrix products, arithmetic and copies ran while one was open for 9% -> 9% of each run, Pallas kernels for 6% -> 5%
where the time goes in v4:
time: 146 us
  starting transfers between devices  50.1 us (34%)
  waiting for transfers between devices  29.8 us (20%)
  blocking collectives  20.9 us (14%)
  Pallas kernels  16.5 us (11%)
  matrix products  11.3 us (8%)
  local copies, waits for them, and re-layouts  10.3 us (7%)
  other arithmetic  5.38 us (4%)
    ppermute x20, starting transfers between devices, send(): return lax.ppermute(values, AXES, pairs)  42.7 us
    ppermute x20, waiting for transfers between devices, send(): return lax.ppermute(values, AXES, pairs)  29.8 us
    all_to_all x2, blocking collectives, exchange(): return lax.all_to_all(values, 'sub', 0, 0)  20.9 us
    dot_general x17, matrix products, matmul(): return jnp.dot(left, right, preferred_element_type=jnp.float32)  11.3 us
    unnamed x52, local copies, waits for them, and re-layouts  9.88 us
    pallas_call x3, Pallas kernels, coupling_rows(): pl.pallas_call(coupling_kernel, grid=(count,), in_specs=[pl.BlockSpec((sl...  7.78 us
    all_to_all x1, starting transfers between devices, exchange(): return lax.all_to_all(values, 'sub', 0, 0)  7.39 us
    pallas_call x2, Pallas kernels, operate(): pl.pallas_call(lambda *refs: operate_kernel(closing, *refs), in_specs=[in...  6.14 us
  transfers between devices with their start and end apart: 21, of which 5 were waited for; matrix products, arithmetic and copies ran while one was open for 9% of the time, Pallas kernels for 5%

profile of v4, /device:TPU:0, one launch (start us, length us, event | category | flops | bytes accessed | tf_op | source)
XLA Modules:
  0.0 145.6 jit_solution(11912974099310405125)
XLA Ops:
  0.6 1.0 copy-done.2
  1.7 1.0 copy-done.4
  2.7 0.8 shard_map.173
  3.5 7.4 %all-to-all-start = ((f32[16,2,128]{2,1,0:T(2,128)}), f32[16,2,128]{2,1,0:T(2,128)S(1)}, u32[]{:S(2)}, u32[]{:S(2)}) async-start(f32[16,2,128]{2,1,0:T(2,128)} %shard_map.173), calls=%async_computation | async-start | bytes 32768 | tf_op jit(solution)/shard_map/all_to_all | solution.py:320
  10.9 0.9 select_select_fusion.neighbours_ref
  11.8 0.8 copy-done.13
  12.6 2.9 %shard_map.177.refs_10_.refs_11_ = bf16[384,1792]{1,0:T(8,128)(2,1)S(1)} custom-call(s32[16,1024]{1,0:T(8,128)S(1)} %select_select_fusion.neighbours_ref, f32[16,1024]{1,0:T(8,128)S(1)} %copy-done.13), custom_call_target="tpu_custom_call" | custom-call | flops 550502400 | bytes 1376256 | tf_op jit(solution)/shard_map/pallas_call | solution.py:62
  15.6 2.9 %shard_map.176.refs_9_.refs_10_ = bf16[384,1792]{1,0:T(8,128)(2,1)S(1)} custom-call(s32[16,1024]{1,0:T(8,128)S(1)} %select_select_fusion.neighbours_ref, f32[16,1024]{1,0:T(8,128)S(1)} %copy-done.13), custom_call_target="tpu_custom_call" | custom-call | flops 550502400 | bytes 1376256 | tf_op jit(solution)/shard_map/pallas_call | solution.py:62
  18.5 1.1 copy-done
  19.7 0.3 fusion.refs_6_.refs_5_
  20.0 1.3 pad_maximum_fusion.4.refs_2_
  21.3 0.8 copy-done.16
  22.1 1.9 %shard_map.174.refs_8_.refs_9_ = bf16[256,1792]{1,0:T(8,128)(2,1)S(1)} custom-call(s32[16,1024]{1,0:T(8,128)S(1)} %copy-done.16, f32[16,1024]{1,0:T(8,128)S(1)} %copy-done.14), custom_call_target="tpu_custom_call" | custom-call | flops 367001600 | bytes 917504 | tf_op jit(solution)/shard_map/pallas_call | solution.py:62
  24.1 0.9 copy-done.6
  25.0 1.0 copy-done.9
  26.0 1.0 copy-done.10
  27.1 0.7 copy-done.17
  27.8 0.6 shard_map.175
  28.4 1.3 copy-done.24
  29.7 0.6 fusion.72
  30.3 3.4 %collective-permute-start.4 = (bf16[896,128]{1,0:T(8,128)(2,1)S(1)}, bf16[896,128]{1,0:T(8,128)(2,1)S(1)}, u32[]{:S(2)}, u32[]{:S(2)}) collective-permute-start(bf16[896,128]{1,0:T(8,128)(2,1)S(1)} %fusion.72), channel_id=1, source_target_pairs={{0,1},{2,3},{4,5},{6,7},{8,9},{10,11},{12,13},{14,15},{16,17},{18,... | collective-permute-start | bytes 688136 | tf_op jit(solution)/shard_map/ppermute | solution.py:22
  33.7 0.1 collective-permute-start
  33.8 10.2 %collective-permute-done = bf16[896,128]{1,0:T(8,128)(2,1)S(1)} collective-permute-done((bf16[896,128]{1,0:T(8,128)(2,1)S(1)}, bf16[896,128]{1,0:T(8,128)(2,1)S(1)}, u32[]{:S(2)}, u32[]{:S(2)}) %collective-permute-start) | collective-permute-done | bytes 229408 | tf_op jit(solution)/shard_map/ppermute | solution.py:22
  44.0 0.6 fusion.81
  44.7 0.7 collective-permute-start.2
  45.4 0.7 collective-permute-start.1
  46.1 11.3 %collective-permute-start.3 = (bf16[896,128]{0,1:T(8,128)(2,1)S(1)}, bf16[896,128]{0,1:T(8,128)(2,1)S(1)}, u32[]{:S(2)}, u32[]{:S(2)}) collective-permute-start(bf16[896,128]{0,1:T(8,128)(2,1)S(1)} %fusion.81), channel_id=1, source_target_pairs={{0,1},{2,3},{4,5},{6,7},{8,9},{10,11},{12,13},{14,15},{16,17},{18,... | collective-permute-start | bytes 688136 | tf_op jit(solution)/shard_map/ppermute | solution.py:22
  57.4 1.8 %fusion.11 = bf16[768,896]{1,0:T(8,128)(2,1)S(1)} fusion(bf16[768,1024]{1,0:T(8,128)(2,1)S(1)} %fusion.refs_6_.refs_5_, bf16[1,1792,896]{2,1,0:T(8,128)(2,1)S(1)} %copy-done.25), kind=kOutput, calls=%fused_computation.12 | convolution fusion | flops 1409974272 | bytes 4784128 | tf_op jit(solution)/shard_map/dot_general | solution.py:214
  59.4 0.6 fusion.63
  60.0 0.7 fusion.66
  60.7 0.5 convolution_convert_fusion.2
  61.2 3.5 %collective-permute-start.9 = (bf16[384,128]{1,0:T(8,128)(2,1)S(1)}, bf16[384,128]{1,0:T(8,128)(2,1)S(1)}, u32[]{:S(2)}, u32[]{:S(2)}) collective-permute-start(bf16[384,128]{1,0:T(8,128)(2,1)S(1)} %get-tuple-element.85), channel_id=1, source_target_pairs={{0,31},{1,30},{2,5},{3,4},{4,3},{5,2},{6,9},{7,8},{8,7},{9,6},{10,... | collective-permute-start | bytes 294920 | tf_op jit(solution)/shard_map/ppermute | solution.py:22
  64.8 0.6 add_convert_fusion.1
  65.4 0.5 convolution_convert_fusion.3
  66.0 2.2 %collective-permute-start.8 = (bf16[384,128]{1,0:T(8,128)(2,1)S(1)}, bf16[384,128]{1,0:T(8,128)(2,1)S(1)}, u32[]{:S(2)}, u32[]{:S(2)}) collective-permute-start(bf16[384,128]{1,0:T(8,128)(2,1)S(1)} %get-tuple-element.87), channel_id=1, source_target_pairs={{0,30},{1,31},{2,4},{3,5},{4,2},{5,3},{6,8},{7,9},{8,6},{9,7},{10,... | collective-permute-start | bytes 294920 | tf_op jit(solution)/shard_map/ppermute | solution.py:22
  68.3 0.6 fusion.30.refs_0_
  68.9 5.7 %collective-permute-done.5.refs_1_ = bf16[1024,128]{1,0:T(8,128)(2,1)S(1)} collective-permute-done((bf16[1024,128]{1,0:T(8,128)(2,1)S(1)}, bf16[1024,128]{1,0:T(8,128)(2,1)S(1)}, u32[]{:S(2)}, u32[]{:S(2)}) %collective-permute-start.5) | collective-permute-done | bytes 262176 | tf_op jit(solution)/shard_map/ppermute | solution.py:22
  74.7 0.2 broadcast_in_dim.7.refs_6_
  74.9 3.0 %operate_second.1 = (f32[1024,128]{1,0:T(8,128)S(1)}, f32[1024,128]{1,0:T(8,128)S(1)}, f32[16,2,128]{2,1,0:T(2,128)S(1)}) custom-call(f32[1024,128]{1,0:T(8,128)S(1)} %fusion.30.refs_0_, bf16[1024,128]{1,0:T(8,128)(2,1)S(1)} %collective-permute-done.5.refs_1_, bf16[384,128]{1,0:T(8,128)(2,1)S(1)} %collective-permute-done.6.refs_2_, ...), custom_call_target="tpu_custom_call" | custom-call | flops 469762048 | bytes 3670016 | tf_op jit(solution)/shard_map/operate_second/pallas_call | solution.py:131
  77.9 10.0 %all_to_all.15.refs_1_ = f32[16,2,128]{2,1,0:T(2,128)S(1)} all-to-all(f32[16,2,128]{2,1,0:T(2,128)S(1)} %get-tuple-element.50), channel_id=1, replica_groups=mesh['sub'=16,'panel'=2] {'sub'}, dimensions={0} | all-to-all | bytes 32768 | tf_op jit(solution)/shard_map/all_to_all | solution.py:320
  87.9 1.2 shard_map.178
  89.1 0.6 fusion.78
  89.7 3.1 %collective-permute-start.14 = (bf16[896,128]{1,0:T(8,128)(2,1)S(1)}, bf16[896,128]{1,0:T(8,128)(2,1)S(1)}, u32[]{:S(2)}, u32[]{:S(2)}) collective-permute-start(bf16[896,128]{1,0:T(8,128)(2,1)S(1)} %fusion.78), channel_id=1, source_target_pairs={{0,1},{2,3},{4,5},{6,7},{8,9},{10,11},{12,13},{14,15},{16,17},{18,... | collective-permute-start | bytes 688136 | tf_op jit(solution)/shard_map/ppermute | solution.py:22
  92.8 0.1 collective-permute-start.10
  92.9 9.4 %collective-permute-done.10 = bf16[896,128]{1,0:T(8,128)(2,1)S(1)} collective-permute-done((bf16[896,128]{1,0:T(8,128)(2,1)S(1)}, bf16[896,128]{1,0:T(8,128)(2,1)S(1)}, u32[]{:S(2)}, u32[]{:S(2)}) %collective-permute-start.10) | collective-permute-done | bytes 229408 | tf_op jit(solution)/shard_map/ppermute | solution.py:22
  102.3 0.7 collective-permute-start.12
  103.0 0.7 collective-permute-start.11
  103.7 0.6 fusion.75
  104.3 7.8 %collective-permute-start.13 = (bf16[896,128]{1,0:T(8,128)(2,1)S(1)}, bf16[896,128]{1,0:T(8,128)(2,1)S(1)}, u32[]{:S(2)}, u32[]{:S(2)}) collective-permute-start(bf16[896,128]{1,0:T(8,128)(2,1)S(1)} %fusion.75), channel_id=1, source_target_pairs={{0,1},{2,3},{4,5},{6,7},{8,9},{10,11},{12,13},{14,15},{16,17},{18,... | collective-permute-start | bytes 688136 | tf_op jit(solution)/shard_map/ppermute | solution.py:22
  112.3 0.6 fusion.60
  112.9 0.5 convolution_convert_fusion
  113.4 4.7 %collective-permute-start.19 = (bf16[384,128]{1,0:T(8,128)(2,1)S(1)}, bf16[384,128]{1,0:T(8,128)(2,1)S(1)}, u32[]{:S(2)}, u32[]{:S(2)}) collective-permute-start(bf16[384,128]{1,0:T(8,128)(2,1)S(1)} %get-tuple-element.77), channel_id=1, source_target_pairs={{0,31},{1,30},{2,5},{3,4},{4,3},{5,2},{6,9},{7,8},{8,7},{9,6},{10,... | collective-permute-start | bytes 294920 | tf_op jit(solution)/shard_map/ppermute | solution.py:22
  118.2 0.7 fusion.69
  118.8 1.1 collective-permute-start.15
  119.9 0.6 add_convert_fusion
  120.5 0.5 convolution_convert_fusion.1
  121.1 2.6 %collective-permute-start.18 = (bf16[384,128]{1,0:T(8,128)(2,1)S(1)}, bf16[384,128]{1,0:T(8,128)(2,1)S(1)}, u32[]{:S(2)}, u32[]{:S(2)}) collective-permute-start(bf16[384,128]{1,0:T(8,128)(2,1)S(1)} %get-tuple-element.79), channel_id=1, source_target_pairs={{0,30},{1,31},{2,4},{3,5},{4,2},{5,3},{6,8},{7,9},{8,6},{9,7},{10,... | collective-permute-start | bytes 294920 | tf_op jit(solution)/shard_map/ppermute | solution.py:22
  123.7 0.6 fusion.33.refs_0_
  124.4 3.5 %collective-permute-done.18.refs_4_ = bf16[384,128]{1,0:T(8,128)(2,1)S(1)} collective-permute-done((bf16[384,128]{1,0:T(8,128)(2,1)S(1)}, bf16[384,128]{1,0:T(8,128)(2,1)S(1)}, u32[]{:S(2)}, u32[]{:S(2)}) %collective-permute-start.18) | collective-permute-done | bytes 98336 | tf_op jit(solution)/shard_map/ppermute | solution.py:22
  127.9 1.0 collective-permute-done.15.refs_1_
  128.8 3.1 %operate_closing.1 = (f32[1024,128]{1,0:T(8,128)S(1)}, f32[1024,128]{1,0:T(8,128)S(1)}, f32[16,4,128]{2,1,0:T(4,128)S(1)}) custom-call(f32[1024,128]{1,0:T(8,128)S(1)} %fusion.33.refs_0_, bf16[1024,128]{1,0:T(8,128)(2,1)S(1)} %collective-permute-done.15.refs_1_, bf16[384,128]{1,0:T(8,128)(2,1)S(1)} %collective-permute-done.16.refs_2_, ...), custom_call_target="tpu_custom_call" | custom-call | flops 469762048 | bytes 3670016 | tf_op jit(solution)/shard_map/operate_closing/pallas_call | solution.py:131
  132.0 10.9 %all_to_all.16 = f32[16,4,128]{2,1,0:T(4,128)S(1)} all-to-all(f32[16,4,128]{2,1,0:T(4,128)S(1)} %get-tuple-element.58), channel_id=1, replica_groups=mesh['sub'=16,'panel'=2] {'sub'}, dimensions={0} | all-to-all | bytes 65536 | tf_op jit(solution)/shard_map/all_to_all | solution.py:320
  142.9 0.5 fusion.123
  143.5 2.1 %multiply_subtract_fusion = (f32[1024,128]{1,0:T(8,128)}, f32[1024,128]{1,0:T(8,128)}) fusion(f32[1024,128]{1,0:T(8,128)} %copy-done.8, f32[1024,128]{1,0:T(8,128)S(1)} %get-tuple-element.60, f32[128]{0:T(128)S(1)} %get-tuple-element.64, f32[1024,128]{1,0:T(8,128)S(1)} %get-tuple-element.59, f32[1024,128]{1,0:T(8,128)S(1)} %copy-done.18, ...), kind=kLoop, calls=%fused_computation.64 | loop fusion | flops 786432 | bytes 3671040 | tf_op jit(solution)/shard_map/sub | solution.py:360
  (90 shorter events, 0.6 us)
Async XLA Ops:
  0.6 1.0 copy-start.2
  1.7 1.0 copy-start.4
  3.5 21.5 %all-to-all-start = ((f32[16,2,128]{2,1,0:T(2,128)}), f32[16,2,128]{2,1,0:T(2,128)S(1)}, u32[]{:S(2)}, u32[]{:S(2)}) async-start(f32[16,2,128]{2,1,0:T(2,128)} %shard_map.173), calls=%async_computation | async-start | bytes 32768 | tf_op jit(solution)/shard_map/all_to_all | solution.py:320
  11.8 0.8 copy-start.13
  12.6 2.9 %copy-start.15 = (s32[16,1024]{1,0:T(8,128)}, s32[16,1024]{1,0:T(8,128)S(1)}, u32[]{:S(2)}) copy-start(s32[16,1024]{1,0:T(8,128)S(1)} %select_select_fusion.neighbours_ref) | copy-start | bytes 196612
  12.6 7.0 %copy-start.21 = (s32[1,2,384]{2,1,0:T(2,128)S(1)}, s32[1,2,384]{2,1,0:T(2,128)}, u32[]{:S(2)}) copy-start(s32[1,2,384]{2,1,0:T(2,128)} %param.27) | copy-start | bytes 9220
  15.6 5.7 %copy-start.14 = (f32[16,1024]{1,0:T(8,128)S(1)}, f32[16,1024]{1,0:T(8,128)}, u32[]{:S(2)}) copy-start(f32[16,1024]{1,0:T(8,128)} %weight_ref.5) | copy-start | bytes 196612
  18.5 1.1 copy-start
  19.6 5.4 %copy-start.5 = (f32[1024,128]{1,0:T(8,128)S(1)}, f32[1024,128]{1,0:T(8,128)}, u32[]{:S(2)}) copy-start(f32[1024,128]{1,0:T(8,128)} %refs_3_.3) | copy-start | bytes 1572868
  21.3 0.8 copy-start.16
  24.1 0.9 copy-start.6
  25.0 1.0 copy-start.9
  26.0 1.0 copy-start.10
  27.1 0.7 copy-start.17
  27.7 1.9 %copy-start.24 = (bf16[1,1792,896]{2,1,0:T(8,128)(2,1)S(1)}, bf16[1,1792,896]{2,1,0:T(8,128)(2,1)}, u32[]{:S(2)}) copy-start(bf16[1,1792,896]{2,1,0:T(8,128)(2,1)} %param.22) | copy-start | bytes 9633796
  30.3 29.1 %collective-permute-start.4 = (bf16[896,128]{1,0:T(8,128)(2,1)S(1)}, bf16[896,128]{1,0:T(8,128)(2,1)S(1)}, u32[]{:S(2)}, u32[]{:S(2)}) collective-permute-start(bf16[896,128]{1,0:T(8,128)(2,1)S(1)} %fusion.72), channel_id=1, source_target_pairs={{0,1},{2,3},{4,5},{6,7},{8,9},{10,11},{12,13},{14,15},{16,17},{18,... | collective-permute-start | bytes 688136 | tf_op jit(solution)/shard_map/ppermute | solution.py:22
  33.7 10.3 %collective-permute-start = (bf16[896,128]{1,0:T(8,128)(2,1)S(1)}, bf16[896,128]{1,0:T(8,128)(2,1)S(1)}, u32[]{:S(2)}, u32[]{:S(2)}) collective-permute-start(bf16[896,128]{1,0:T(8,128)(2,1)S(1)} %get-tuple-element.38), channel_id=1, source_target_pairs={{0,1},{1,0},{2,3},{3,2},{4,5},{5,4},{6,7},{7,6},{8,9},{9,8},{10,11... | collective-permute-start | bytes 688136 | tf_op jit(solution)/shard_map/ppermute | solution.py:22
  33.8 23.6 %copy-start.25 = (bf16[1,1792,896]{2,1,0:T(8,128)(2,1)S(1)}, bf16[1,1792,896]{2,1,0:T(8,128)(2,1)}, u32[]{:S(2)}) copy-start(bf16[1,1792,896]{2,1,0:T(8,128)(2,1)} %param.23) | copy-start | bytes 9633796
  44.7 14.6 %collective-permute-start.2 = (bf16[384,256]{1,0:T(8,128)(2,1)S(1)}, bf16[384,256]{1,0:T(8,128)(2,1)S(1)}, u32[]{:S(2)}, u32[]{:S(2)}) collective-permute-start(bf16[384,256]{1,0:T(8,128)(2,1)S(1)} %pad_maximum_fusion.1), channel_id=1, source_target_pairs={{1,3},{3,1},{5,7},{7,5},{9,11},{11,9},{13,15},{15,13},{17,19},{19,... | collective-permute-start | bytes 589832 | tf_op jit(solution)/shard_map/ppermute | solution.py:22
  45.4 13.8 %collective-permute-start.1 = (bf16[384,256]{1,0:T(8,128)(2,1)S(1)}, bf16[384,256]{1,0:T(8,128)(2,1)S(1)}, u32[]{:S(2)}, u32[]{:S(2)}) collective-permute-start(bf16[384,256]{1,0:T(8,128)(2,1)S(1)} %pad_maximum_fusion), channel_id=1, source_target_pairs={{1,31},{3,5},{5,3},{7,9},{9,7},{11,13},{13,11},{15,17},{17,15},{19... | collective-permute-start | bytes 589832 | tf_op jit(solution)/shard_map/ppermute | solution.py:22
  46.1 18.7 %collective-permute-start.3 = (bf16[896,128]{0,1:T(8,128)(2,1)S(1)}, bf16[896,128]{0,1:T(8,128)(2,1)S(1)}, u32[]{:S(2)}, u32[]{:S(2)}) collective-permute-start(bf16[896,128]{0,1:T(8,128)(2,1)S(1)} %fusion.81), channel_id=1, source_target_pairs={{0,1},{2,3},{4,5},{6,7},{8,9},{10,11},{12,13},{14,15},{16,17},{18,... | collective-permute-start | bytes 688136 | tf_op jit(solution)/shard_map/ppermute | solution.py:22
  60.6 4.1 %copy-start.19 = (s32[16,1024]{1,0:T(8,128)S(1)}, s32[16,1024]{1,0:T(8,128)}, u32[]{:S(2)}) copy-start(s32[16,1024]{1,0:T(8,128)} %param.24) | copy-start | bytes 196612
  60.6 4.1 %copy-start.20 = (f32[1024]{0:T(1024)S(1)}, f32[1024]{0:T(1024)}, u32[]{:S(2)}) copy-start(f32[1024]{0:T(1024)} %param.26) | copy-start | bytes 12292
  61.2 13.4 %collective-permute-start.9 = (bf16[384,128]{1,0:T(8,128)(2,1)S(1)}, bf16[384,128]{1,0:T(8,128)(2,1)S(1)}, u32[]{:S(2)}, u32[]{:S(2)}) collective-permute-start(bf16[384,128]{1,0:T(8,128)(2,1)S(1)} %get-tuple-element.85), channel_id=1, source_target_pairs={{0,31},{1,30},{2,5},{3,4},{4,3},{5,2},{6,9},{7,8},{8,7},{9,6},{10,... | collective-permute-start | bytes 294920 | tf_op jit(solution)/shard_map/ppermute | solution.py:22
  64.7 9.9 %collective-permute-start.7 = (bf16[384,128]{1,0:T(8,128)(2,1)S(1)}, bf16[384,128]{1,0:T(8,128)(2,1)S(1)}, u32[]{:S(2)}, u32[]{:S(2)}) collective-permute-start(bf16[384,128]{1,0:T(8,128)(2,1)S(1)} %get-tuple-element.86), channel_id=1, source_target_pairs={{0,3},{1,2},{2,1},{3,0},{4,7},{5,6},{6,5},{7,4},{8,11},{9,10},{10,... | collective-permute-start | bytes 294920 | tf_op jit(solution)/shard_map/ppermute | solution.py:22
  64.7 9.9 %collective-permute-start.5 = (bf16[1024,128]{1,0:T(8,128)(2,1)S(1)}, bf16[1024,128]{1,0:T(8,128)(2,1)S(1)}, u32[]{:S(2)}, u32[]{:S(2)}) collective-permute-start(bf16[1024,128]{1,0:T(8,128)(2,1)S(1)} %fusion.66), channel_id=1, source_target_pairs={{0,1},{1,0},{2,3},{3,2},{4,5},{5,4},{6,7},{7,6},{8,9},{9,8},{10,11... | collective-permute-start | bytes 786440 | tf_op jit(solution)/shard_map/ppermute | solution.py:22
  66.0 8.9 %copy-start.1 = (bf16[384,1792]{1,0:T(8,128)(2,1)S(1)}, bf16[384,1792]{1,0:T(8,128)(2,1)}, u32[]{:S(2)}) copy-start(bf16[384,1792]{1,0:T(8,128)(2,1)} %copy-done) | copy-start | bytes 4128772
  66.0 8.9 %copy-start.3 = (f32[1024,128]{1,0:T(8,128)S(1)}, f32[1024,128]{1,0:T(8,128)}, u32[]{:S(2)}) copy-start(f32[1024,128]{1,0:T(8,128)} %refs_7_.3) | copy-start | bytes 1572868
  66.0 8.9 %copy-start.7 = (bf16[256,1792]{1,0:T(8,128)(2,1)S(1)}, bf16[256,1792]{1,0:T(8,128)(2,1)}, u32[]{:S(2)}) copy-start(bf16[256,1792]{1,0:T(8,128)(2,1)} %copy-done.6) | copy-start | bytes 2752516
  66.0 8.6 %collective-permute-start.8 = (bf16[384,128]{1,0:T(8,128)(2,1)S(1)}, bf16[384,128]{1,0:T(8,128)(2,1)S(1)}, u32[]{:S(2)}, u32[]{:S(2)}) collective-permute-start(bf16[384,128]{1,0:T(8,128)(2,1)S(1)} %get-tuple-element.87), channel_id=1, source_target_pairs={{0,30},{1,31},{2,4},{3,5},{4,2},{5,3},{6,8},{7,9},{8,6},{9,7},{10,... | collective-permute-start | bytes 294920 | tf_op jit(solution)/shard_map/ppermute | solution.py:22
  68.3 6.4 %collective-permute-start.6 = (bf16[384,128]{1,0:T(8,128)(2,1)S(1)}, bf16[384,128]{1,0:T(8,128)(2,1)S(1)}, u32[]{:S(2)}, u32[]{:S(2)}) collective-permute-start(bf16[384,128]{1,0:T(8,128)(2,1)S(1)} %get-tuple-element.88), channel_id=1, source_target_pairs={{0,2},{1,3},{2,0},{3,1},{4,6},{5,7},{6,4},{7,5},{8,10},{9,11},{10,... | collective-permute-start | bytes 294920 | tf_op jit(solution)/shard_map/ppermute | solution.py:22
  77.9 11.8 %copy-start.11 = (f32[1024,128]{1,0:T(8,128)}, f32[1024,128]{1,0:T(8,128)S(1)}, u32[]{:S(2)}) copy-start(f32[1024,128]{1,0:T(8,128)S(1)} %get-tuple-element.54) | copy-start | bytes 1572868
  89.1 39.8 %copy-start.8 = (f32[1024,128]{1,0:T(8,128)}, f32[1024,128]{1,0:T(8,128)S(1)}, u32[]{:S(2)}) copy-start(f32[1024,128]{1,0:T(8,128)S(1)} %get-tuple-element.57.refs_8_) | copy-start | bytes 1572868
  89.7 22.6 %collective-permute-start.14 = (bf16[896,128]{1,0:T(8,128)(2,1)S(1)}, bf16[896,128]{1,0:T(8,128)(2,1)S(1)}, u32[]{:S(2)}, u32[]{:S(2)}) collective-permute-start(bf16[896,128]{1,0:T(8,128)(2,1)S(1)} %fusion.78), channel_id=1, source_target_pairs={{0,1},{2,3},{4,5},{6,7},{8,9},{10,11},{12,13},{14,15},{16,17},{18,... | collective-permute-start | bytes 688136 | tf_op jit(solution)/shard_map/ppermute | solution.py:22
  92.8 9.5 %collective-permute-start.10 = (bf16[896,128]{1,0:T(8,128)(2,1)S(1)}, bf16[896,128]{1,0:T(8,128)(2,1)S(1)}, u32[]{:S(2)}, u32[]{:S(2)}) collective-permute-start(bf16[896,128]{1,0:T(8,128)(2,1)S(1)} %get-tuple-element.56), channel_id=1, source_target_pairs={{0,1},{1,0},{2,3},{3,2},{4,5},{5,4},{6,7},{7,6},{8,9},{9,8},{10,11... | collective-permute-start | bytes 688136 | tf_op jit(solution)/shard_map/ppermute | solution.py:22
  102.3 9.9 %collective-permute-start.12 = (bf16[384,256]{1,0:T(8,128)(2,1)S(1)}, bf16[384,256]{1,0:T(8,128)(2,1)S(1)}, u32[]{:S(2)}, u32[]{:S(2)}) collective-permute-start(bf16[384,256]{1,0:T(8,128)(2,1)S(1)} %pad_maximum_fusion.3), channel_id=1, source_target_pairs={{1,3},{3,1},{5,7},{7,5},{9,11},{11,9},{13,15},{15,13},{17,19},{19,... | collective-permute-start | bytes 589832 | tf_op jit(solution)/shard_map/ppermute | solution.py:22
  103.0 9.2 %collective-permute-start.11 = (bf16[384,256]{1,0:T(8,128)(2,1)S(1)}, bf16[384,256]{1,0:T(8,128)(2,1)S(1)}, u32[]{:S(2)}, u32[]{:S(2)}) collective-permute-start(bf16[384,256]{1,0:T(8,128)(2,1)S(1)} %pad_maximum_fusion.2), channel_id=1, source_target_pairs={{1,31},{3,5},{5,3},{7,9},{9,7},{11,13},{13,11},{15,17},{17,15},{19... | collective-permute-start | bytes 589832 | tf_op jit(solution)/shard_map/ppermute | solution.py:22
  104.3 15.6 %collective-permute-start.13 = (bf16[896,128]{1,0:T(8,128)(2,1)S(1)}, bf16[896,128]{1,0:T(8,128)(2,1)S(1)}, u32[]{:S(2)}, u32[]{:S(2)}) collective-permute-start(bf16[896,128]{1,0:T(8,128)(2,1)S(1)} %fusion.75), channel_id=1, source_target_pairs={{0,1},{2,3},{4,5},{6,7},{8,9},{10,11},{12,13},{14,15},{16,17},{18,... | collective-permute-start | bytes 688136 | tf_op jit(solution)/shard_map/ppermute | solution.py:22
  113.4 10.9 %collective-permute-start.19 = (bf16[384,128]{1,0:T(8,128)(2,1)S(1)}, bf16[384,128]{1,0:T(8,128)(2,1)S(1)}, u32[]{:S(2)}, u32[]{:S(2)}) collective-permute-start(bf16[384,128]{1,0:T(8,128)(2,1)S(1)} %get-tuple-element.77), channel_id=1, source_target_pairs={{0,31},{1,30},{2,5},{3,4},{4,3},{5,2},{6,9},{7,8},{8,7},{9,6},{10,... | collective-permute-start | bytes 294920 | tf_op jit(solution)/shard_map/ppermute | solution.py:22
  118.2 6.2 %collective-permute-start.17 = (bf16[384,128]{1,0:T(8,128)(2,1)S(1)}, bf16[384,128]{1,0:T(8,128)(2,1)S(1)}, u32[]{:S(2)}, u32[]{:S(2)}) collective-permute-start(bf16[384,128]{1,0:T(8,128)(2,1)S(1)} %get-tuple-element.78), channel_id=1, source_target_pairs={{0,3},{1,2},{2,1},{3,0},{4,7},{5,6},{6,5},{7,4},{8,11},{9,10},{10,... | collective-permute-start | bytes 294920 | tf_op jit(solution)/shard_map/ppermute | solution.py:22
  118.8 10.0 %collective-permute-start.15 = (bf16[1024,128]{1,0:T(8,128)(2,1)S(1)}, bf16[1024,128]{1,0:T(8,128)(2,1)S(1)}, u32[]{:S(2)}, u32[]{:S(2)}) collective-permute-start(bf16[1024,128]{1,0:T(8,128)(2,1)S(1)} %fusion.69), channel_id=1, source_target_pairs={{0,1},{1,0},{2,3},{3,2},{4,5},{5,4},{6,7},{7,6},{8,9},{9,8},{10,11... | collective-permute-start | bytes 786440 | tf_op jit(solution)/shard_map/ppermute | solution.py:22
  121.1 6.8 %collective-permute-start.18 = (bf16[384,128]{1,0:T(8,128)(2,1)S(1)}, bf16[384,128]{1,0:T(8,128)(2,1)S(1)}, u32[]{:S(2)}, u32[]{:S(2)}) collective-permute-start(bf16[384,128]{1,0:T(8,128)(2,1)S(1)} %get-tuple-element.79), channel_id=1, source_target_pairs={{0,30},{1,31},{2,4},{3,5},{4,2},{5,3},{6,8},{7,9},{8,6},{9,7},{10,... | collective-permute-start | bytes 294920 | tf_op jit(solution)/shard_map/ppermute | solution.py:22
  123.7 4.2 %collective-permute-start.16 = (bf16[384,128]{1,0:T(8,128)(2,1)S(1)}, bf16[384,128]{1,0:T(8,128)(2,1)S(1)}, u32[]{:S(2)}, u32[]{:S(2)}) collective-permute-start(bf16[384,128]{1,0:T(8,128)(2,1)S(1)} %get-tuple-element.80), channel_id=1, source_target_pairs={{0,2},{1,3},{2,0},{3,1},{4,6},{5,7},{6,4},{7,5},{8,10},{9,11},{10,... | collective-permute-start | bytes 294920 | tf_op jit(solution)/shard_map/ppermute | solution.py:22
  128.8 14.6 %copy-start.12 = (f32[1024,128]{1,0:T(8,128)S(1)}, f32[1024,128]{1,0:T(8,128)}, u32[]{:S(2)}) copy-start(f32[1024,128]{1,0:T(8,128)} %copy-done.11) | copy-start | bytes 1572868
  128.8 14.6 %copy-start.18 = (f32[1024,128]{1,0:T(8,128)S(1)}, f32[1024,128]{1,0:T(8,128)}, u32[]{:S(2)}) copy-start(f32[1024,128]{1,0:T(8,128)} %param.14) | copy-start | bytes 1572868
  128.8 14.6 %copy-start.23 = (f32[1,128]{1,0:T(1,128)S(1)}, f32[1,128]{1,0:T(1,128)}, u32[]{:S(2)}) copy-start(f32[1,128]{1,0:T(1,128)} %get-tuple-element.53) | copy-start | bytes 1540
  143.5 2.2 %copy-start.22 = (f32[128]{0:T(128)}, f32[128]{0:T(128)S(1)}, u32[]{:S(2)}) copy-start(f32[128]{0:T(128)S(1)} %get-tuple-element.64) | copy-start | bytes 1540

commit v5 on v2

--- a/solution.py
+++ b/solution.py
@@ -237,11 +237,9 @@
     cuts = (0, blocks // 2, blocks)
     coupling = []
 
-    def next_coupling(trigger):
+    def next_coupling():
         begin, end = cuts[len(coupling) : len(coupling) + 2]
-        trigger, links = lax.optimization_barrier((trigger, neighbours))
-        coupling.append(coupling_rows(links, edge_weight, ext, begin, end - begin))
-        return trigger
+        coupling.append(coupling_rows(neighbours, edge_weight, ext, begin, end - begin))
 
     def meet(arrived, value):
         return lax.optimization_barrier((arrived, value))
@@ -254,7 +252,6 @@
     turned = jnp.where(neighbours < own + border, neighbours + border, neighbours - border)
     ghost = even & (neighbours >= own) & (neighbours < ext)
     neighbours = jnp.where(ghost, turned, neighbours)
-    near_far = by_parity(send_rows[0, ::-1], send_rows[0])
     rows = lax.broadcasted_iota(jnp.int32, (1, own), 1)
 
     def by_panel(zero, one):
@@ -262,20 +259,13 @@
 
     diagonal_rows = lax.dynamic_slice_in_dim(lower, panel * half, half, axis=0)
 
-    def precondition(mine, payload, chosen_upper):
-        build = chosen_upper is None
-        if build:
-            payload = next_coupling(payload)
+    def precondition(mine, payload, build):
         received = send(payload, lambda s, p: (s, 1 - p))
         early = matmul(lower[half:], mine).astype(jnp.bfloat16)
         passed_others = send(early, lambda s, p: (s, 1) if p == 0 else None)
         if build:
+            next_coupling()
             received, coupling[-1] = meet(received, coupling[-1])
-        late = matmul(lower[half:], received).astype(jnp.bfloat16)
-        if build:
-            late, chosen = lax.optimization_barrier((next_coupling(late), select))
-            chosen_upper = matmul(chosen, upper).astype(jnp.bfloat16)
-        passed_mine = send(late, lambda s, p: (s, 1) if p == 0 else None)
         near_rows, far_rows = slice(tail, tail + border), slice(tail + border, half)
 
         def both(part):
@@ -283,9 +273,8 @@
 
         from_far = send(both(far_rows), lambda s, p: (far(s), 1) if p == 1 else None)
         from_near = send(both(near_rows), lambda s, p: (near(s), 1) if p == 1 else None)
-        if build:
-            passed_mine, coupling[-1] = meet(passed_mine, coupling[-1])
-            passed_mine, chosen_upper = meet(passed_mine, chosen_upper)
+        late = matmul(lower[half:], received).astype(jnp.bfloat16)
+        passed_mine = send(late, lambda s, p: (s, 1) if p == 0 else None)
         from_lower, from_upper = by_parity(from_far, from_near), by_parity(from_near, from_far)
 
         def solve(kept, ghost_columns, passed):
@@ -302,15 +291,18 @@
             diagonal.append(scale)
         other_part = matmul(upper, others).astype(jnp.bfloat16)
         swapped = send(other_part, lambda s, p: (s, 1 - p))
-        mine = solve(mine, slice(cols, 2 * cols), passed_mine)
         other_edge = matmul(chosen_upper, others).astype(jnp.bfloat16)
         cross_far = send(other_edge[border:], lambda s, p: (far(s), 1 - p))
+        cross_near = send(other_edge[:border], lambda s, p: (near(s), 1 - p))
+        mine = solve(mine, slice(cols, 2 * cols), passed_mine)
         edge = matmul(chosen_upper, mine).astype(jnp.bfloat16)
         part = matmul(upper, mine)
         same_far = send(edge[border:], lambda s, p: (far(s), p))
-        cross_near = send(other_edge[:border], lambda s, p: (near(s), 1 - p))
         same_near = send(edge[:border], lambda s, p: (near(s), p))
-        return (part, swapped, same_near, cross_near, same_far, cross_far), chosen_upper
+        if build:
+            next_coupling()
+            swapped, coupling[-1] = meet(swapped, coupling[-1])
+        return part, swapped, same_near, cross_near, same_far, cross_far
 
     copies = lax.axis_size("sub")
 
@@ -322,16 +314,19 @@
     panel_rows = jax.ShapeDtypeStruct((half, cols), jnp.bfloat16)
     sums = jnp.stack([jnp.sum(shadow * residual, axis=0), jnp.sum(shadow * shadow, axis=0)])
     sums = jnp.broadcast_to(sums[None], (copies, 2, cols))
-    sums, near_far = lax.optimization_barrier((sums, near_far))
-    select = (near_far.reshape(2 * border, 1) == rows).astype(jnp.bfloat16)
+    sums, lists = lax.optimization_barrier((sums, send_rows))
+    near_far = [by_parity(lists[0, 1], lists[0, 0]), by_parity(lists[0, 0], lists[0, 1])]
+    select = (jnp.concatenate(near_far)[:, None] == rows).astype(jnp.bfloat16)
+    chosen_upper = matmul(select, upper).astype(jnp.bfloat16)
+    opening_sums, chosen_upper = meet(exchange(sums), chosen_upper)
     past = jnp.stack([rho_prev, alpha_prev, omega_prev])
     opening, mine, payload = small_call(
         lambda *refs: direction_kernel(node_count, *refs),
         panel,
-        (exchange(sums), past, residual, direction, old_image, select),
+        (opening_sums, past, residual, direction, old_image, select),
         [jax.ShapeDtypeStruct((2, cols), jnp.float32), panel_rows, panel_rows],
     )
-    parts, chosen_upper = precondition(mine, payload, None)
+    parts = precondition(mine, payload, True)
     direction_hat, image_new, sums = operate(parts, diagonal[0], shadow, None, coupling, copies)
     step_alpha, middle, mine, payload = small_call(
         lambda *refs: middle_kernel(node_count, *refs),
@@ -340,7 +335,7 @@
         [jax.ShapeDtypeStruct((1, cols), jnp.float32), vector, panel_rows, panel_rows],
     )
     step_alpha = step_alpha[0]
-    parts, _ = precondition(mine, payload, chosen_upper)
+    parts = precondition(mine, payload, False)
     middle_hat, tested, sums = operate(parts, diagonal[0], shadow, middle, coupling, copies)
     closing = jnp.sum(exchange(sums), axis=0) / node_count
     step_omega = closing[0] / (closing[1] + EPSILON)

time: 133 us -> 149 us (1.12)
  local copies, waits for them, and re-layouts: 3.87 us -> 9.33 us
  starting transfers between devices: 46.6 us -> 51.1 us
  matrix products: 11.2 us -> 13.9 us
  other arithmetic: 4.45 us -> 6.96 us
    unnamed x32 -> x42, local copies, waits for them, and re-layouts: 1.31 us -> 8.29 us
    all_to_all x1, waiting for transfers between devices: 5.23 us -> 0.01 us  [exchange(): return lax.all_to_all(values, 'sub', 0, 0)]
    ppermute x20, waiting for transfers between devices: 24.4 us -> 29.5 us  [send(): return lax.ppermute(values, AXES, pairs)]
    ppermute x20, starting transfers between devices: 39.1 us -> 43.7 us  [send(): return lax.ppermute(values, AXES, pairs)]
    dot_general x17, matrix products: 11.2 us -> 13.9 us  [matmul(): return jnp.dot(left, right, preferred_element_type=jnp.float32)]
    rev x1 -> x0, local copies, waits for them, and re-layouts: 1.51 us -> none  [per_device(): near_far = by_parity(send_rows[0, ::-1], send_rows[0])]
  transfers between devices with their start and end apart: 21 -> 21, of which waited for: 8 -> 5; matrix products, arithmetic and copies ran while one was open for 9% -> 11% of each run, Pallas kernels for 6% -> 5%
where the time goes in v5:
time: 149 us; the launch traced here: 148 us
  starting transfers between devices  51.1 us (34%)
  waiting for transfers between devices  29.5 us (20%)
  blocking collectives  20.8 us (14%)
  Pallas kernels  14.8 us (10%)
  matrix products  13.9 us (9%)
  local copies, waits for them, and re-layouts  9.33 us (6%)
  other arithmetic  6.96 us (5%)
    ppermute x20, starting transfers between devices, send(): return lax.ppermute(values, AXES, pairs)  43.7 us
    ppermute x20, waiting for transfers between devices, send(): return lax.ppermute(values, AXES, pairs)  29.5 us
    all_to_all x2, blocking collectives, exchange(): return lax.all_to_all(values, 'sub', 0, 0)  20.8 us
    dot_general x17, matrix products, matmul(): return jnp.dot(left, right, preferred_element_type=jnp.float32)  13.9 us
    unnamed x42, local copies, waits for them, and re-layouts  8.29 us
    pallas_call x2, Pallas kernels, coupling_rows(): pl.pallas_call(coupling_kernel, grid=(count,), in_specs=[pl.BlockSpec((sl...  7.78 us
    all_to_all x1, starting transfers between devices, exchange(): return lax.all_to_all(values, 'sub', 0, 0)  7.39 us
    pallas_call x2, Pallas kernels, operate(): pl.pallas_call(lambda *refs: operate_kernel(closing, *refs), in_specs=[in...  5.1 us
  transfers between devices with their start and end apart: 21, of which 5 were waited for; matrix products, arithmetic and copies ran while one was open for 11% of the time, Pallas kernels for 5%

profile of v5, /device:TPU:0, one launch (start us, length us, event | category | flops | bytes accessed | tf_op | source)
XLA Modules:
  0.0 147.7 jit_solution(17794423698835658377)
XLA Ops:
  0.6 1.4 multiply_reduce_fusion.1
  2.0 0.6 broadcast_in_dim.8
  2.6 7.4 %all-to-all-start = ((f32[16,2,128]{2,1,0:T(2,128)}), f32[16,2,128]{2,1,0:T(2,128)S(1)}, u32[]{:S(2)}, u32[]{:S(2)}) async-start(f32[16,2,128]{2,1,0:T(2,128)} %broadcast_in_dim.8), calls=%async_computation | async-start | bytes 32768 | tf_op jit(solution)/shard_map/all_to_all | solution.py:310
  10.0 0.8 fusion.122
  10.8 0.9 select_select_fusion.neighbours_ref
  11.7 0.3 fusion.refs_6_.refs_5_
  12.0 4.5 %fusion.11 = bf16[768,896]{1,0:T(8,128)(2,1)} fusion(s32[768]{0:T(1024)S(1)} %pad_add_fusion, bf16[1,1792,896]{2,1,0:T(8,128)(2,1)} %param.23), kind=kOutput, calls=%fused_computation.12 | convolution fusion | flops 1410760704 | bytes 3214336 | tf_op jit(solution)/shard_map/dot_general | solution.py:207
  16.5 3.9 %shard_map.175.refs_9_.refs_10_ = bf16[512,1792]{1,0:T(8,128)(2,1)S(1)} custom-call(s32[16,1024]{1,0:T(8,128)S(1)} %select_select_fusion.neighbours_ref, f32[16,1024]{1,0:T(8,128)S(1)} %copy-done.10), custom_call_target="tpu_custom_call" | custom-call | flops 734003200 | bytes 1835008 | tf_op jit(solution)/shard_map/pallas_call | solution.py:62
  20.4 0.6 pad_maximum_fusion.4.refs_2_
  21.0 3.9 %shard_map.174.refs_8_.refs_9_ = bf16[512,1792]{1,0:T(8,128)(2,1)S(1)} custom-call(s32[16,1024]{1,0:T(8,128)S(1)} %select_select_fusion.neighbours_ref, f32[16,1024]{1,0:T(8,128)S(1)} %copy-done.10), custom_call_target="tpu_custom_call" | custom-call | flops 734003200 | bytes 1835008 | tf_op jit(solution)/shard_map/pallas_call | solution.py:62
  24.9 1.3 copy-done
  26.2 1.0 copy-done.3
  27.2 1.0 copy-done.6
  28.3 1.0 copy-done.7
  29.3 0.7 copy-done.11
  30.0 0.6 shard_map.173
  30.6 1.3 copy-done.19
  31.9 0.6 fusion.76
  32.5 3.4 %collective-permute-start.4 = (bf16[896,128]{1,0:T(8,128)(2,1)S(1)}, bf16[896,128]{1,0:T(8,128)(2,1)S(1)}, u32[]{:S(2)}, u32[]{:S(2)}) collective-permute-start(bf16[896,128]{1,0:T(8,128)(2,1)S(1)} %fusion.76), channel_id=1, source_target_pairs={{0,1},{2,3},{4,5},{6,7},{8,9},{10,11},{12,13},{14,15},{16,17},{18,... | collective-permute-start | bytes 688136 | tf_op jit(solution)/shard_map/ppermute | solution.py:22
  35.9 0.1 collective-permute-start
  36.0 10.2 %collective-permute-done = bf16[896,128]{1,0:T(8,128)(2,1)S(1)} collective-permute-done((bf16[896,128]{1,0:T(8,128)(2,1)S(1)}, bf16[896,128]{1,0:T(8,128)(2,1)S(1)}, u32[]{:S(2)}, u32[]{:S(2)}) %collective-permute-start) | collective-permute-done | bytes 229408 | tf_op jit(solution)/shard_map/ppermute | solution.py:22
  46.3 0.7 collective-permute-start.2
  47.0 0.7 collective-permute-start.1
  47.7 0.6 fusion.73
  48.3 11.3 %collective-permute-start.3 = (bf16[896,128]{1,0:T(8,128)(2,1)S(1)}, bf16[896,128]{1,0:T(8,128)(2,1)S(1)}, u32[]{:S(2)}, u32[]{:S(2)}) collective-permute-start(bf16[896,128]{1,0:T(8,128)(2,1)S(1)} %fusion.73), channel_id=1, source_target_pairs={{0,1},{2,3},{4,5},{6,7},{8,9},{10,11},{12,13},{14,15},{16,17},{18,... | collective-permute-start | bytes 688136 | tf_op jit(solution)/shard_map/ppermute | solution.py:22
  59.8 0.6 fusion.64
  60.4 1.2 copy-done.20
  61.6 0.6 fusion.67
  62.2 0.7 copy-done.12
  62.9 0.5 convolution_convert_fusion.2
  63.5 4.7 %collective-permute-start.9 = (bf16[384,128]{1,0:T(8,128)(2,1)S(1)}, bf16[384,128]{1,0:T(8,128)(2,1)S(1)}, u32[]{:S(2)}, u32[]{:S(2)}) collective-permute-start(bf16[384,128]{1,0:T(8,128)(2,1)S(1)} %get-tuple-element.77), channel_id=1, source_target_pairs={{0,31},{1,30},{2,5},{3,4},{4,3},{5,2},{6,9},{7,8},{8,7},{9,6},{10,... | collective-permute-start | bytes 294920 | tf_op jit(solution)/shard_map/ppermute | solution.py:22
  68.3 0.6 add_convert_fusion.1
  68.9 0.5 convolution_convert_fusion.3
  69.5 1.8 %collective-permute-start.8 = (bf16[384,128]{1,0:T(8,128)(2,1)S(1)}, bf16[384,128]{1,0:T(8,128)(2,1)S(1)}, u32[]{:S(2)}, u32[]{:S(2)}) collective-permute-start(bf16[384,128]{1,0:T(8,128)(2,1)S(1)} %get-tuple-element.79), channel_id=1, source_target_pairs={{0,30},{1,31},{2,4},{3,5},{4,2},{5,3},{6,8},{7,9},{8,6},{9,7},{10,... | collective-permute-start | bytes 294920 | tf_op jit(solution)/shard_map/ppermute | solution.py:22
  71.2 0.2 collective-permute-start.6
  71.5 0.6 fusion.34.refs_0_
  72.1 5.3 %collective-permute-done.5.refs_1_ = bf16[1024,128]{1,0:T(8,128)(2,1)S(1)} collective-permute-done((bf16[1024,128]{1,0:T(8,128)(2,1)S(1)}, bf16[1024,128]{1,0:T(8,128)(2,1)S(1)}, u32[]{:S(2)}, u32[]{:S(2)}) %collective-permute-start.5) | collective-permute-done | bytes 262176 | tf_op jit(solution)/shard_map/ppermute | solution.py:22
  77.4 0.2 broadcast_in_dim.10.refs_6_
  77.6 2.5 %operate_second.1 = (f32[1024,128]{1,0:T(8,128)S(1)}, f32[1024,128]{1,0:T(8,128)S(1)}, f32[16,2,128]{2,1,0:T(2,128)S(1)}) custom-call(f32[1024,128]{1,0:T(8,128)S(1)} %fusion.34.refs_0_, bf16[1024,128]{1,0:T(8,128)(2,1)S(1)} %collective-permute-done.5.refs_1_, bf16[384,128]{1,0:T(8,128)(2,1)S(1)} %collective-permute-done.6.refs_2_, ...), custom_call_target="tpu_custom_call" | custom-call | flops 469762048 | bytes 3670016 | tf_op jit(solution)/shard_map/operate_second/pallas_call | solution.py:131
  80.2 9.8 %all_to_all.15.refs_1_ = f32[16,2,128]{2,1,0:T(2,128)S(1)} all-to-all(f32[16,2,128]{2,1,0:T(2,128)S(1)} %get-tuple-element.40), channel_id=1, replica_groups=mesh['sub'=16,'panel'=2] {'sub'}, dimensions={0} | all-to-all | bytes 32768 | tf_op jit(solution)/shard_map/all_to_all | solution.py:310
  90.0 1.3 shard_map.176
  91.4 0.6 fusion.82
  92.0 3.1 %collective-permute-start.14 = (bf16[896,128]{1,0:T(8,128)(2,1)S(1)}, bf16[896,128]{1,0:T(8,128)(2,1)S(1)}, u32[]{:S(2)}, u32[]{:S(2)}) collective-permute-start(bf16[896,128]{1,0:T(8,128)(2,1)S(1)} %fusion.82), channel_id=1, source_target_pairs={{0,1},{2,3},{4,5},{6,7},{8,9},{10,11},{12,13},{14,15},{16,17},{18,... | collective-permute-start | bytes 688136 | tf_op jit(solution)/shard_map/ppermute | solution.py:22
  95.1 0.1 collective-permute-start.10
  95.2 9.6 %collective-permute-done.10 = bf16[896,128]{1,0:T(8,128)(2,1)S(1)} collective-permute-done((bf16[896,128]{1,0:T(8,128)(2,1)S(1)}, bf16[896,128]{1,0:T(8,128)(2,1)S(1)}, u32[]{:S(2)}, u32[]{:S(2)}) %collective-permute-start.10) | collective-permute-done | bytes 229408 | tf_op jit(solution)/shard_map/ppermute | solution.py:22
  104.8 0.7 collective-permute-start.12
  105.5 0.7 collective-permute-start.11
  106.2 0.6 fusion.79
  106.8 7.8 %collective-permute-start.13 = (bf16[896,128]{1,0:T(8,128)(2,1)S(1)}, bf16[896,128]{1,0:T(8,128)(2,1)S(1)}, u32[]{:S(2)}, u32[]{:S(2)}) collective-permute-start(bf16[896,128]{1,0:T(8,128)(2,1)S(1)} %fusion.79), channel_id=1, source_target_pairs={{0,1},{2,3},{4,5},{6,7},{8,9},{10,11},{12,13},{14,15},{16,17},{18,... | collective-permute-start | bytes 688136 | tf_op jit(solution)/shard_map/ppermute | solution.py:22
  114.8 0.6 fusion.61
  115.4 0.5 convolution_convert_fusion
  116.0 4.7 %collective-permute-start.19 = (bf16[384,128]{1,0:T(8,128)(2,1)S(1)}, bf16[384,128]{1,0:T(8,128)(2,1)S(1)}, u32[]{:S(2)}, u32[]{:S(2)}) collective-permute-start(bf16[384,128]{1,0:T(8,128)(2,1)S(1)} %get-tuple-element.69), channel_id=1, source_target_pairs={{0,31},{1,30},{2,5},{3,4},{4,3},{5,2},{6,9},{7,8},{8,7},{9,6},{10,... | collective-permute-start | bytes 294920 | tf_op jit(solution)/shard_map/ppermute | solution.py:22
  120.7 0.6 fusion.70
  121.3 1.1 collective-permute-start.15
  122.4 0.6 add_convert_fusion
  123.0 0.5 convolution_convert_fusion.1
  123.5 2.7 %collective-permute-start.18 = (bf16[384,128]{1,0:T(8,128)(2,1)S(1)}, bf16[384,128]{1,0:T(8,128)(2,1)S(1)}, u32[]{:S(2)}, u32[]{:S(2)}) collective-permute-start(bf16[384,128]{1,0:T(8,128)(2,1)S(1)} %get-tuple-element.71), channel_id=1, source_target_pairs={{0,30},{1,31},{2,4},{3,5},{4,2},{5,3},{6,8},{7,9},{8,6},{9,7},{10,... | collective-permute-start | bytes 294920 | tf_op jit(solution)/shard_map/ppermute | solution.py:22
  126.2 0.6 fusion.31.refs_0_
  126.9 3.5 %collective-permute-done.18.refs_4_ = bf16[384,128]{1,0:T(8,128)(2,1)S(1)} collective-permute-done((bf16[384,128]{1,0:T(8,128)(2,1)S(1)}, bf16[384,128]{1,0:T(8,128)(2,1)S(1)}, u32[]{:S(2)}, u32[]{:S(2)}) %collective-permute-start.18) | collective-permute-done | bytes 98336 | tf_op jit(solution)/shard_map/ppermute | solution.py:22
  130.4 1.0 collective-permute-done.15.refs_1_
  131.3 2.6 %operate_closing.1 = (f32[1024,128]{1,0:T(8,128)S(1)}, f32[1024,128]{1,0:T(8,128)S(1)}, f32[16,4,128]{2,1,0:T(4,128)S(1)}) custom-call(f32[1024,128]{1,0:T(8,128)S(1)} %fusion.31.refs_0_, bf16[1024,128]{1,0:T(8,128)(2,1)S(1)} %collective-permute-done.15.refs_1_, bf16[384,128]{1,0:T(8,128)(2,1)S(1)} %collective-permute-done.16.refs_2_, ...), custom_call_target="tpu_custom_call" | custom-call | flops 469762048 | bytes 3670016 | tf_op jit(solution)/shard_map/operate_closing/pallas_call | solution.py:131
  133.9 10.9 %all_to_all.16 = f32[16,4,128]{2,1,0:T(4,128)S(1)} all-to-all(f32[16,4,128]{2,1,0:T(4,128)S(1)} %get-tuple-element.48), channel_id=1, replica_groups=mesh['sub'=16,'panel'=2] {'sub'}, dimensions={0} | all-to-all | bytes 65536 | tf_op jit(solution)/shard_map/all_to_all | solution.py:310
  144.9 0.5 fusion.124
  145.4 2.3 %multiply_subtract_fusion = (f32[1024,128]{1,0:T(8,128)}, f32[1024,128]{1,0:T(8,128)}) fusion(f32[1024,128]{1,0:T(8,128)} %copy-done.5, f32[1024,128]{1,0:T(8,128)S(1)} %get-tuple-element.50, f32[128]{0:T(128)S(1)} %get-tuple-element.56, f32[1024,128]{1,0:T(8,128)S(1)} %get-tuple-element.49, f32[1024,128]{1,0:T(8,128)} %param.14, ...), kind=kLoop, calls=%fused_computation.65 | loop fusion | flops 786432 | bytes 3671040 | tf_op jit(solution)/shard_map/sub | solution.py:343
  (81 shorter events, 0.6 us)
Async XLA Ops:
  2.6 23.6 %all-to-all-start = ((f32[16,2,128]{2,1,0:T(2,128)}), f32[16,2,128]{2,1,0:T(2,128)S(1)}, u32[]{:S(2)}, u32[]{:S(2)}) async-start(f32[16,2,128]{2,1,0:T(2,128)} %broadcast_in_dim.8), calls=%async_computation | async-start | bytes 32768 | tf_op jit(solution)/shard_map/all_to_all | solution.py:310
  12.0 4.5 %copy-start.10 = (f32[16,1024]{1,0:T(8,128)S(1)}, f32[16,1024]{1,0:T(8,128)}, u32[]{:S(2)}) copy-start(f32[16,1024]{1,0:T(8,128)} %weight_ref.3) | copy-start | bytes 196612
  16.5 3.9 %copy-start.16 = (f32[128]{0:T(128)S(1)}, f32[128]{0:T(128)}, u32[]{:S(2)}) copy-start(f32[128]{0:T(128)} %param.21) | copy-start | bytes 1540
  16.5 3.9 %copy-start.17 = (f32[128]{0:T(128)S(1)}, f32[128]{0:T(128)}, u32[]{:S(2)}) copy-start(f32[128]{0:T(128)} %param.20) | copy-start | bytes 1540
  16.5 3.9 %copy-start.18 = (f32[128]{0:T(128)S(1)}, f32[128]{0:T(128)}, u32[]{:S(2)}) copy-start(f32[128]{0:T(128)} %param.19) | copy-start | bytes 1540
  24.9 1.3 copy-start
  26.2 1.0 copy-start.3
  27.2 1.0 copy-start.6
  28.3 1.0 copy-start.7
  29.3 0.7 copy-start.11
  30.0 1.9 %copy-start.19 = (bf16[1,1792,896]{2,1,0:T(8,128)(2,1)S(1)}, bf16[1,1792,896]{2,1,0:T(8,128)(2,1)}, u32[]{:S(2)}) copy-start(bf16[1,1792,896]{2,1,0:T(8,128)(2,1)} %param.22) | copy-start | bytes 9633796
  32.5 27.3 %collective-permute-start.4 = (bf16[896,128]{1,0:T(8,128)(2,1)S(1)}, bf16[896,128]{1,0:T(8,128)(2,1)S(1)}, u32[]{:S(2)}, u32[]{:S(2)}) collective-permute-start(bf16[896,128]{1,0:T(8,128)(2,1)S(1)} %fusion.76), channel_id=1, source_target_pairs={{0,1},{2,3},{4,5},{6,7},{8,9},{10,11},{12,13},{14,15},{16,17},{18,... | collective-permute-start | bytes 688136 | tf_op jit(solution)/shard_map/ppermute | solution.py:22
  35.9 10.3 %collective-permute-start = (bf16[896,128]{1,0:T(8,128)(2,1)S(1)}, bf16[896,128]{1,0:T(8,128)(2,1)S(1)}, u32[]{:S(2)}, u32[]{:S(2)}) collective-permute-start(bf16[896,128]{1,0:T(8,128)(2,1)S(1)} %get-tuple-element.32), channel_id=1, source_target_pairs={{0,1},{1,0},{2,3},{3,2},{4,5},{5,4},{6,7},{7,6},{8,9},{9,8},{10,11... | collective-permute-start | bytes 688136 | tf_op jit(solution)/shard_map/ppermute | solution.py:22
  46.3 13.3 %collective-permute-start.2 = (bf16[384,256]{1,0:T(8,128)(2,1)S(1)}, bf16[384,256]{1,0:T(8,128)(2,1)S(1)}, u32[]{:S(2)}, u32[]{:S(2)}) collective-permute-start(bf16[384,256]{1,0:T(8,128)(2,1)S(1)} %pad_maximum_fusion.1), channel_id=1, source_target_pairs={{1,3},{3,1},{5,7},{7,5},{9,11},{11,9},{13,15},{15,13},{17,19},{19,... | collective-permute-start | bytes 589832 | tf_op jit(solution)/shard_map/ppermute | solution.py:22
  47.0 12.6 %collective-permute-start.1 = (bf16[384,256]{1,0:T(8,128)(2,1)S(1)}, bf16[384,256]{1,0:T(8,128)(2,1)S(1)}, u32[]{:S(2)}, u32[]{:S(2)}) collective-permute-start(bf16[384,256]{1,0:T(8,128)(2,1)S(1)} %pad_maximum_fusion), channel_id=1, source_target_pairs={{1,31},{3,5},{5,3},{7,9},{9,7},{11,13},{13,11},{15,17},{17,15},{19... | collective-permute-start | bytes 589832 | tf_op jit(solution)/shard_map/ppermute | solution.py:22
  48.3 20.0 %collective-permute-start.3 = (bf16[896,128]{1,0:T(8,128)(2,1)S(1)}, bf16[896,128]{1,0:T(8,128)(2,1)S(1)}, u32[]{:S(2)}, u32[]{:S(2)}) collective-permute-start(bf16[896,128]{1,0:T(8,128)(2,1)S(1)} %fusion.73), channel_id=1, source_target_pairs={{0,1},{2,3},{4,5},{6,7},{8,9},{10,11},{12,13},{14,15},{16,17},{18,... | collective-permute-start | bytes 688136 | tf_op jit(solution)/shard_map/ppermute | solution.py:22
  59.7 1.9 %copy-start.20 = (bf16[1,1792,896]{2,1,0:T(8,128)(2,1)S(1)}, bf16[1,1792,896]{2,1,0:T(8,128)(2,1)}, u32[]{:S(2)}) copy-start(bf16[1,1792,896]{2,1,0:T(8,128)(2,1)} %param.23) | copy-start | bytes 9633796
  61.6 1.3 copy-start.12
  62.9 5.3 %copy-start.13 = (f32[1024]{0:T(1024)S(1)}, f32[1024]{0:T(1024)}, u32[]{:S(2)}) copy-start(f32[1024]{0:T(1024)} %param.26) | copy-start | bytes 12292
  63.5 13.9 %collective-permute-start.9 = (bf16[384,128]{1,0:T(8,128)(2,1)S(1)}, bf16[384,128]{1,0:T(8,128)(2,1)S(1)}, u32[]{:S(2)}, u32[]{:S(2)}) collective-permute-start(bf16[384,128]{1,0:T(8,128)(2,1)S(1)} %get-tuple-element.77), channel_id=1, source_target_pairs={{0,31},{1,30},{2,5},{3,4},{4,3},{5,2},{6,9},{7,8},{8,7},{9,6},{10,... | collective-permute-start | bytes 294920 | tf_op jit(solution)/shard_map/ppermute | solution.py:22
  68.2 9.2 %collective-permute-start.7 = (bf16[384,128]{1,0:T(8,128)(2,1)S(1)}, bf16[384,128]{1,0:T(8,128)(2,1)S(1)}, u32[]{:S(2)}, u32[]{:S(2)}) collective-permute-start(bf16[384,128]{1,0:T(8,128)(2,1)S(1)} %get-tuple-element.78), channel_id=1, source_target_pairs={{0,3},{1,2},{2,1},{3,0},{4,7},{5,6},{6,5},{7,4},{8,11},{9,10},{10,... | collective-permute-start | bytes 294920 | tf_op jit(solution)/shard_map/ppermute | solution.py:22
  68.2 9.2 %collective-permute-start.5 = (bf16[1024,128]{1,0:T(8,128)(2,1)S(1)}, bf16[1024,128]{1,0:T(8,128)(2,1)S(1)}, u32[]{:S(2)}, u32[]{:S(2)}) collective-permute-start(bf16[1024,128]{1,0:T(8,128)(2,1)S(1)} %fusion.67), channel_id=1, source_target_pairs={{0,1},{1,0},{2,3},{3,2},{4,5},{5,4},{6,7},{7,6},{8,9},{9,8},{10,11... | collective-permute-start | bytes 786440 | tf_op jit(solution)/shard_map/ppermute | solution.py:22
  69.4 8.2 %copy-start.1 = (bf16[512,1792]{1,0:T(8,128)(2,1)S(1)}, bf16[512,1792]{1,0:T(8,128)(2,1)}, u32[]{:S(2)}) copy-start(bf16[512,1792]{1,0:T(8,128)(2,1)} %copy-done) | copy-start | bytes 5505028
  69.4 8.2 %copy-start.2 = (f32[1024,128]{1,0:T(8,128)S(1)}, f32[1024,128]{1,0:T(8,128)}, u32[]{:S(2)}) copy-start(f32[1024,128]{1,0:T(8,128)} %refs_7_.3) | copy-start | bytes 1572868
  69.5 7.9 %collective-permute-start.8 = (bf16[384,128]{1,0:T(8,128)(2,1)S(1)}, bf16[384,128]{1,0:T(8,128)(2,1)S(1)}, u32[]{:S(2)}, u32[]{:S(2)}) collective-permute-start(bf16[384,128]{1,0:T(8,128)(2,1)S(1)} %get-tuple-element.79), channel_id=1, source_target_pairs={{0,30},{1,31},{2,4},{3,5},{4,2},{5,3},{6,8},{7,9},{8,6},{9,7},{10,... | collective-permute-start | bytes 294920 | tf_op jit(solution)/shard_map/ppermute | solution.py:22
  71.2 6.2 %collective-permute-start.6 = (bf16[384,128]{1,0:T(8,128)(2,1)S(1)}, bf16[384,128]{1,0:T(8,128)(2,1)S(1)}, u32[]{:S(2)}, u32[]{:S(2)}) collective-permute-start(bf16[384,128]{1,0:T(8,128)(2,1)S(1)} %get-tuple-element.80), channel_id=1, source_target_pairs={{0,2},{1,3},{2,0},{3,1},{4,6},{5,7},{6,4},{7,5},{8,10},{9,11},{10,... | collective-permute-start | bytes 294920 | tf_op jit(solution)/shard_map/ppermute | solution.py:22
  77.6 12.4 %copy-start.4 = (f32[1024,128]{1,0:T(8,128)S(1)}, f32[1024,128]{1,0:T(8,128)}, u32[]{:S(2)}) copy-start(f32[1024,128]{1,0:T(8,128)} %refs_3_.3) | copy-start | bytes 1572868
  80.2 11.8 %copy-start.8 = (f32[1024,128]{1,0:T(8,128)}, f32[1024,128]{1,0:T(8,128)S(1)}, u32[]{:S(2)}) copy-start(f32[1024,128]{1,0:T(8,128)S(1)} %get-tuple-element.44) | copy-start | bytes 1572868
  91.4 40.0 %copy-start.5 = (f32[1024,128]{1,0:T(8,128)}, f32[1024,128]{1,0:T(8,128)S(1)}, u32[]{:S(2)}) copy-start(f32[1024,128]{1,0:T(8,128)S(1)} %get-tuple-element.47.refs_8_) | copy-start | bytes 1572868
  92.0 22.8 %collective-permute-start.14 = (bf16[896,128]{1,0:T(8,128)(2,1)S(1)}, bf16[896,128]{1,0:T(8,128)(2,1)S(1)}, u32[]{:S(2)}, u32[]{:S(2)}) collective-permute-start(bf16[896,128]{1,0:T(8,128)(2,1)S(1)} %fusion.82), channel_id=1, source_target_pairs={{0,1},{2,3},{4,5},{6,7},{8,9},{10,11},{12,13},{14,15},{16,17},{18,... | collective-permute-start | bytes 688136 | tf_op jit(solution)/shard_map/ppermute | solution.py:22
  95.1 9.7 %collective-permute-start.10 = (bf16[896,128]{1,0:T(8,128)(2,1)S(1)}, bf16[896,128]{1,0:T(8,128)(2,1)S(1)}, u32[]{:S(2)}, u32[]{:S(2)}) collective-permute-start(bf16[896,128]{1,0:T(8,128)(2,1)S(1)} %get-tuple-element.46), channel_id=1, source_target_pairs={{0,1},{1,0},{2,3},{3,2},{4,5},{5,4},{6,7},{7,6},{8,9},{9,8},{10,11... | collective-permute-start | bytes 688136 | tf_op jit(solution)/shard_map/ppermute | solution.py:22
  104.8 9.9 %collective-permute-start.12 = (bf16[384,256]{1,0:T(8,128)(2,1)S(1)}, bf16[384,256]{1,0:T(8,128)(2,1)S(1)}, u32[]{:S(2)}, u32[]{:S(2)}) collective-permute-start(bf16[384,256]{1,0:T(8,128)(2,1)S(1)} %pad_maximum_fusion.3), channel_id=1, source_target_pairs={{1,3},{3,1},{5,7},{7,5},{9,11},{11,9},{13,15},{15,13},{17,19},{19,... | collective-permute-start | bytes 589832 | tf_op jit(solution)/shard_map/ppermute | solution.py:22
  105.5 9.2 %collective-permute-start.11 = (bf16[384,256]{1,0:T(8,128)(2,1)S(1)}, bf16[384,256]{1,0:T(8,128)(2,1)S(1)}, u32[]{:S(2)}, u32[]{:S(2)}) collective-permute-start(bf16[384,256]{1,0:T(8,128)(2,1)S(1)} %pad_maximum_fusion.2), channel_id=1, source_target_pairs={{1,31},{3,5},{5,3},{7,9},{9,7},{11,13},{13,11},{15,17},{17,15},{19... | collective-permute-start | bytes 589832 | tf_op jit(solution)/shard_map/ppermute | solution.py:22
  106.8 15.6 %collective-permute-start.13 = (bf16[896,128]{1,0:T(8,128)(2,1)S(1)}, bf16[896,128]{1,0:T(8,128)(2,1)S(1)}, u32[]{:S(2)}, u32[]{:S(2)}) collective-permute-start(bf16[896,128]{1,0:T(8,128)(2,1)S(1)} %fusion.79), channel_id=1, source_target_pairs={{0,1},{2,3},{4,5},{6,7},{8,9},{10,11},{12,13},{14,15},{16,17},{18,... | collective-permute-start | bytes 688136 | tf_op jit(solution)/shard_map/ppermute | solution.py:22
  116.0 10.9 %collective-permute-start.19 = (bf16[384,128]{1,0:T(8,128)(2,1)S(1)}, bf16[384,128]{1,0:T(8,128)(2,1)S(1)}, u32[]{:S(2)}, u32[]{:S(2)}) collective-permute-start(bf16[384,128]{1,0:T(8,128)(2,1)S(1)} %get-tuple-element.69), channel_id=1, source_target_pairs={{0,31},{1,30},{2,5},{3,4},{4,3},{5,2},{6,9},{7,8},{8,7},{9,6},{10,... | collective-permute-start | bytes 294920 | tf_op jit(solution)/shard_map/ppermute | solution.py:22
  120.7 6.2 %collective-permute-start.17 = (bf16[384,128]{1,0:T(8,128)(2,1)S(1)}, bf16[384,128]{1,0:T(8,128)(2,1)S(1)}, u32[]{:S(2)}, u32[]{:S(2)}) collective-permute-start(bf16[384,128]{1,0:T(8,128)(2,1)S(1)} %get-tuple-element.70), channel_id=1, source_target_pairs={{0,3},{1,2},{2,1},{3,0},{4,7},{5,6},{6,5},{7,4},{8,11},{9,10},{10,... | collective-permute-start | bytes 294920 | tf_op jit(solution)/shard_map/ppermute | solution.py:22
  121.3 10.0 %collective-permute-start.15 = (bf16[1024,128]{1,0:T(8,128)(2,1)S(1)}, bf16[1024,128]{1,0:T(8,128)(2,1)S(1)}, u32[]{:S(2)}, u32[]{:S(2)}) collective-permute-start(bf16[1024,128]{1,0:T(8,128)(2,1)S(1)} %fusion.70), channel_id=1, source_target_pairs={{0,1},{1,0},{2,3},{3,2},{4,5},{5,4},{6,7},{7,6},{8,9},{9,8},{10,11... | collective-permute-start | bytes 786440 | tf_op jit(solution)/shard_map/ppermute | solution.py:22
  123.5 6.8 %collective-permute-start.18 = (bf16[384,128]{1,0:T(8,128)(2,1)S(1)}, bf16[384,128]{1,0:T(8,128)(2,1)S(1)}, u32[]{:S(2)}, u32[]{:S(2)}) collective-permute-start(bf16[384,128]{1,0:T(8,128)(2,1)S(1)} %get-tuple-element.71), channel_id=1, source_target_pairs={{0,30},{1,31},{2,4},{3,5},{4,2},{5,3},{6,8},{7,9},{8,6},{9,7},{10,... | collective-permute-start | bytes 294920 | tf_op jit(solution)/shard_map/ppermute | solution.py:22
  126.2 4.1 %collective-permute-start.16 = (bf16[384,128]{1,0:T(8,128)(2,1)S(1)}, bf16[384,128]{1,0:T(8,128)(2,1)S(1)}, u32[]{:S(2)}, u32[]{:S(2)}) collective-permute-start(bf16[384,128]{1,0:T(8,128)(2,1)S(1)} %get-tuple-element.72), channel_id=1, source_target_pairs={{0,2},{1,3},{2,0},{3,1},{4,6},{5,7},{6,4},{7,5},{8,10},{9,11},{10,... | collective-permute-start | bytes 294920 | tf_op jit(solution)/shard_map/ppermute | solution.py:22
  131.3 14.1 %copy-start.9 = (f32[1024,128]{1,0:T(8,128)S(1)}, f32[1024,128]{1,0:T(8,128)}, u32[]{:S(2)}) copy-start(f32[1024,128]{1,0:T(8,128)} %copy-done.8) | copy-start | bytes 1572868
  131.3 14.1 %copy-start.15 = (f32[1,128]{1,0:T(1,128)S(1)}, f32[1,128]{1,0:T(1,128)}, u32[]{:S(2)}) copy-start(f32[1,128]{1,0:T(1,128)} %get-tuple-element.43) | copy-start | bytes 1540
  145.4 2.3 %copy-start.14 = (f32[128]{0:T(128)}, f32[128]{0:T(128)S(1)}, u32[]{:S(2)}) copy-start(f32[128]{0:T(128)S(1)} %get-tuple-element.56) | copy-start | bytes 1540

commit v6 on v5

--- a/solution.py
+++ b/solution.py
@@ -259,7 +259,8 @@
 
     diagonal_rows = lax.dynamic_slice_in_dim(lower, panel * half, half, axis=0)
 
-    def precondition(mine, payload, build):
+    def precondition(mine, payload, chosen_upper):
+        build = chosen_upper is None
         received = send(payload, lambda s, p: (s, 1 - p))
         early = matmul(lower[half:], mine).astype(jnp.bfloat16)
         passed_others = send(early, lambda s, p: (s, 1) if p == 0 else None)
@@ -274,7 +275,12 @@
         from_far = send(both(far_rows), lambda s, p: (far(s), 1) if p == 1 else None)
         from_near = send(both(near_rows), lambda s, p: (near(s), 1) if p == 1 else None)
         late = matmul(lower[half:], received).astype(jnp.bfloat16)
+        if build:
+            late, chosen = lax.optimization_barrier((late, select))
+            chosen_upper = matmul(chosen, upper).astype(jnp.bfloat16)
         passed_mine = send(late, lambda s, p: (s, 1) if p == 0 else None)
+        if build:
+            from_far, chosen_upper = meet(from_far, chosen_upper)
         from_lower, from_upper = by_parity(from_far, from_near), by_parity(from_near, from_far)
 
         def solve(kept, ghost_columns, passed):
@@ -302,7 +308,7 @@
         if build:
             next_coupling()
             swapped, coupling[-1] = meet(swapped, coupling[-1])
-        return part, swapped, same_near, cross_near, same_far, cross_far
+        return (part, swapped, same_near, cross_near, same_far, cross_far), chosen_upper
 
     copies = lax.axis_size("sub")
 
@@ -317,16 +323,14 @@
     sums, lists = lax.optimization_barrier((sums, send_rows))
     near_far = [by_parity(lists[0, 1], lists[0, 0]), by_parity(lists[0, 0], lists[0, 1])]
     select = (jnp.concatenate(near_far)[:, None] == rows).astype(jnp.bfloat16)
-    chosen_upper = matmul(select, upper).astype(jnp.bfloat16)
-    opening_sums, chosen_upper = meet(exchange(sums), chosen_upper)
     past = jnp.stack([rho_prev, alpha_prev, omega_prev])
     opening, mine, payload = small_call(
         lambda *refs: direction_kernel(node_count, *refs),
         panel,
-        (opening_sums, past, residual, direction, old_image, select),
+        (exchange(sums), past, residual, direction, old_image, select),
         [jax.ShapeDtypeStruct((2, cols), jnp.float32), panel_rows, panel_rows],
     )
-    parts = precondition(mine, payload, True)
+    parts, chosen_upper = precondition(mine, payload, None)
     direction_hat, image_new, sums = operate(parts, diagonal[0], shadow, None, coupling, copies)
     step_alpha, middle, mine, payload = small_call(
         lambda *refs: middle_kernel(node_count, *refs),
@@ -335,7 +339,7 @@
         [jax.ShapeDtypeStruct((1, cols), jnp.float32), vector, panel_rows, panel_rows],
     )
     step_alpha = step_alpha[0]
-    parts = precondition(mine, payload, False)
+    parts, _ = precondition(mine, payload, chosen_upper)
     middle_hat, tested, sums = operate(parts, diagonal[0], shadow, middle, coupling, copies)
     closing = jnp.sum(exchange(sums), axis=0) / node_count
     step_omega = closing[0] / (closing[1] + EPSILON)

time: 149 us -> 143 us (0.960)
  matrix products: 13.9 us -> 11.3 us
  local copies, waits for them, and re-layouts: 9.33 us -> 7.43 us
    dot_general x17, matrix products: 13.9 us -> 11.3 us  [matmul(): return jnp.dot(left, right, preferred_element_type=jnp.float32)]
    unnamed x42 -> x40, local copies, waits for them, and re-layouts: 8.29 us -> 6.4 us
  transfers between devices with their start and end apart: 21 -> 21, of which waited for: 5 -> 5; matrix products, arithmetic and copies ran while one was open for 11% -> 9% of each run, Pallas kernels for 5% -> 5%
where the time goes in v6:
time: 143 us
  starting transfers between devices  49.9 us (35%)
  waiting for transfers between devices  30.2 us (21%)
  blocking collectives  20.8 us (15%)
  Pallas kernels  14.7 us (10%)
  matrix products  11.3 us (8%)
  local copies, waits for them, and re-layouts  7.43 us (5%)
  other arithmetic  6.99 us (5%)
    ppermute x20, starting transfers between devices, send(): return lax.ppermute(values, AXES, pairs)  42.5 us
    ppermute x20, waiting for transfers between devices, send(): return lax.ppermute(values, AXES, pairs)  30.2 us
    all_to_all x2, blocking collectives, exchange(): return lax.all_to_all(values, 'sub', 0, 0)  20.8 us
    dot_general x17, matrix products, matmul(): return jnp.dot(left, right, preferred_element_type=jnp.float32)  11.3 us
    pallas_call x2, Pallas kernels, coupling_rows(): pl.pallas_call(coupling_kernel, grid=(count,), in_specs=[pl.BlockSpec((sl...  7.78 us
    all_to_all x1, starting transfers between devices, exchange(): return lax.all_to_all(values, 'sub', 0, 0)  7.39 us
    unnamed x40, local copies, waits for them, and re-layouts  6.4 us
    pallas_call x2, Pallas kernels, operate(): pl.pallas_call(lambda *refs: operate_kernel(closing, *refs), in_specs=[in...  5.1 us
  transfers between devices with their start and end apart: 21, of which 5 were waited for; matrix products, arithmetic and copies ran while one was open for 9% of the time, Pallas kernels for 5%

profile of v6, /device:TPU:0, one launch (start us, length us, event | category | flops | bytes accessed | tf_op | source)
XLA Modules:
  0.0 142.5 jit_solution(10500900058634075492)
XLA Ops:
  0.6 1.4 multiply_reduce_fusion.1
  2.0 0.6 broadcast_in_dim.8
  2.6 7.4 %all-to-all-start = ((f32[16,2,128]{2,1,0:T(2,128)}), f32[16,2,128]{2,1,0:T(2,128)S(1)}, u32[]{:S(2)}, u32[]{:S(2)}) async-start(f32[16,2,128]{2,1,0:T(2,128)} %broadcast_in_dim.8), calls=%async_computation | async-start | bytes 32768 | tf_op jit(solution)/shard_map/all_to_all | solution.py:316
  10.1 0.8 fusion.121
  10.8 0.9 select_select_fusion.neighbours_ref
  11.7 0.0 copy-start.17
  11.8 0.3 fusion.refs_6_.refs_5_
  12.1 3.9 %shard_map.175.refs_9_.refs_10_ = bf16[512,1792]{1,0:T(8,128)(2,1)S(1)} custom-call(s32[16,1024]{1,0:T(8,128)S(1)} %select_select_fusion.neighbours_ref, f32[16,1024]{1,0:T(8,128)S(1)} %copy-done.10), custom_call_target="tpu_custom_call" | custom-call | flops 734003200 | bytes 1835008 | tf_op jit(solution)/shard_map/pallas_call | solution.py:62
  16.0 0.6 pad_maximum_fusion.4.refs_2_
  16.6 3.9 %shard_map.174.refs_8_.refs_9_ = bf16[512,1792]{1,0:T(8,128)(2,1)S(1)} custom-call(s32[16,1024]{1,0:T(8,128)S(1)} %select_select_fusion.neighbours_ref, f32[16,1024]{1,0:T(8,128)S(1)} %copy-done.10), custom_call_target="tpu_custom_call" | custom-call | flops 734003200 | bytes 1835008 | tf_op jit(solution)/shard_map/pallas_call | solution.py:62
  20.5 1.3 copy-done
  21.8 1.0 copy-done.3
  22.8 1.0 copy-done.6
  23.9 1.0 copy-done.7
  24.9 0.7 copy-done.11
  25.6 0.6 shard_map.173
  26.2 1.3 copy-done.18
  27.5 0.6 fusion.72
  28.1 3.4 %collective-permute-start.4 = (bf16[896,128]{1,0:T(8,128)(2,1)S(1)}, bf16[896,128]{1,0:T(8,128)(2,1)S(1)}, u32[]{:S(2)}, u32[]{:S(2)}) collective-permute-start(bf16[896,128]{1,0:T(8,128)(2,1)S(1)} %fusion.72), channel_id=1, source_target_pairs={{0,1},{2,3},{4,5},{6,7},{8,9},{10,11},{12,13},{14,15},{16,17},{18,... | collective-permute-start | bytes 688136 | tf_op jit(solution)/shard_map/ppermute | solution.py:22
  31.5 0.1 collective-permute-start
  31.6 10.2 %collective-permute-done = bf16[896,128]{1,0:T(8,128)(2,1)S(1)} collective-permute-done((bf16[896,128]{1,0:T(8,128)(2,1)S(1)}, bf16[896,128]{1,0:T(8,128)(2,1)S(1)}, u32[]{:S(2)}, u32[]{:S(2)}) %collective-permute-start) | collective-permute-done | bytes 229408 | tf_op jit(solution)/shard_map/ppermute | solution.py:22
  41.9 0.6 fusion.81
  42.5 0.7 collective-permute-start.2
  43.2 0.7 collective-permute-start.1
  43.9 11.3 %collective-permute-start.3 = (bf16[896,128]{0,1:T(8,128)(2,1)S(1)}, bf16[896,128]{0,1:T(8,128)(2,1)S(1)}, u32[]{:S(2)}, u32[]{:S(2)}) collective-permute-start(bf16[896,128]{0,1:T(8,128)(2,1)S(1)} %fusion.81), channel_id=1, source_target_pairs={{0,1},{2,3},{4,5},{6,7},{8,9},{10,11},{12,13},{14,15},{16,17},{18,... | collective-permute-start | bytes 688136 | tf_op jit(solution)/shard_map/ppermute | solution.py:22
  55.2 1.8 %fusion.11 = bf16[768,896]{1,0:T(8,128)(2,1)S(1)} fusion(bf16[768,1024]{1,0:T(8,128)(2,1)S(1)} %fusion.refs_6_.refs_5_, bf16[1,1792,896]{2,1,0:T(8,128)(2,1)S(1)} %copy-done.19), kind=kOutput, calls=%fused_computation.12 | convolution fusion | flops 1409974272 | bytes 4784128 | tf_op jit(solution)/shard_map/dot_general | solution.py:207
  57.1 0.1 fusion.144
  57.2 0.6 fusion.63
  57.8 0.7 fusion.66
  58.5 0.5 convolution_convert_fusion.2
  59.0 3.5 %collective-permute-start.9 = (bf16[384,128]{1,0:T(8,128)(2,1)S(1)}, bf16[384,128]{1,0:T(8,128)(2,1)S(1)}, u32[]{:S(2)}, u32[]{:S(2)}) collective-permute-start(bf16[384,128]{1,0:T(8,128)(2,1)S(1)} %get-tuple-element.81), channel_id=1, source_target_pairs={{0,31},{1,30},{2,5},{3,4},{4,3},{5,2},{6,9},{7,8},{8,7},{9,6},{10,... | collective-permute-start | bytes 294920 | tf_op jit(solution)/shard_map/ppermute | solution.py:22
  62.6 0.6 add_convert_fusion.1
  63.3 0.5 convolution_convert_fusion.3
  63.8 0.0 copy-start.2
  63.8 2.2 %collective-permute-start.8 = (bf16[384,128]{1,0:T(8,128)(2,1)S(1)}, bf16[384,128]{1,0:T(8,128)(2,1)S(1)}, u32[]{:S(2)}, u32[]{:S(2)}) collective-permute-start(bf16[384,128]{1,0:T(8,128)(2,1)S(1)} %get-tuple-element.83), channel_id=1, source_target_pairs={{0,30},{1,31},{2,4},{3,5},{4,2},{5,3},{6,8},{7,9},{8,6},{9,7},{10,... | collective-permute-start | bytes 294920 | tf_op jit(solution)/shard_map/ppermute | solution.py:22
  66.1 0.6 fusion.30.refs_0_
  66.7 5.7 %collective-permute-done.5.refs_1_ = bf16[1024,128]{1,0:T(8,128)(2,1)S(1)} collective-permute-done((bf16[1024,128]{1,0:T(8,128)(2,1)S(1)}, bf16[1024,128]{1,0:T(8,128)(2,1)S(1)}, u32[]{:S(2)}, u32[]{:S(2)}) %collective-permute-start.5) | collective-permute-done | bytes 262176 | tf_op jit(solution)/shard_map/ppermute | solution.py:22
  72.5 0.2 broadcast_in_dim.10.refs_6_
  72.7 2.5 %operate_second.1 = (f32[1024,128]{1,0:T(8,128)S(1)}, f32[1024,128]{1,0:T(8,128)S(1)}, f32[16,2,128]{2,1,0:T(2,128)S(1)}) custom-call(f32[1024,128]{1,0:T(8,128)S(1)} %fusion.30.refs_0_, bf16[1024,128]{1,0:T(8,128)(2,1)S(1)} %collective-permute-done.5.refs_1_, bf16[384,128]{1,0:T(8,128)(2,1)S(1)} %collective-permute-done.6.refs_2_, ...), custom_call_target="tpu_custom_call" | custom-call | flops 469762048 | bytes 3670016 | tf_op jit(solution)/shard_map/operate_second/pallas_call | solution.py:131
  75.2 10.0 %all_to_all.15.refs_1_ = f32[16,2,128]{2,1,0:T(2,128)S(1)} all-to-all(f32[16,2,128]{2,1,0:T(2,128)S(1)} %get-tuple-element.44), channel_id=1, replica_groups=mesh['sub'=16,'panel'=2] {'sub'}, dimensions={0} | all-to-all | bytes 32768 | tf_op jit(solution)/shard_map/all_to_all | solution.py:316
  85.2 1.2 shard_map.176
  86.4 0.6 fusion.78
  87.0 2.9 %collective-permute-start.14 = (bf16[896,128]{1,0:T(8,128)(2,1)S(1)}, bf16[896,128]{1,0:T(8,128)(2,1)S(1)}, u32[]{:S(2)}, u32[]{:S(2)}) collective-permute-start(bf16[896,128]{1,0:T(8,128)(2,1)S(1)} %fusion.78), channel_id=1, source_target_pairs={{0,1},{2,3},{4,5},{6,7},{8,9},{10,11},{12,13},{14,15},{16,17},{18,... | collective-permute-start | bytes 688136 | tf_op jit(solution)/shard_map/ppermute | solution.py:22
  89.9 0.1 collective-permute-start.10
  90.0 9.6 %collective-permute-done.10 = bf16[896,128]{1,0:T(8,128)(2,1)S(1)} collective-permute-done((bf16[896,128]{1,0:T(8,128)(2,1)S(1)}, bf16[896,128]{1,0:T(8,128)(2,1)S(1)}, u32[]{:S(2)}, u32[]{:S(2)}) %collective-permute-start.10) | collective-permute-done | bytes 229408 | tf_op jit(solution)/shard_map/ppermute | solution.py:22
  99.6 0.7 collective-permute-start.12
  100.3 0.9 collective-permute-start.11
  101.2 0.6 fusion.75
  101.8 7.9 %collective-permute-start.13 = (bf16[896,128]{1,0:T(8,128)(2,1)S(1)}, bf16[896,128]{1,0:T(8,128)(2,1)S(1)}, u32[]{:S(2)}, u32[]{:S(2)}) collective-permute-start(bf16[896,128]{1,0:T(8,128)(2,1)S(1)} %fusion.75), channel_id=1, source_target_pairs={{0,1},{2,3},{4,5},{6,7},{8,9},{10,11},{12,13},{14,15},{16,17},{18,... | collective-permute-start | bytes 688136 | tf_op jit(solution)/shard_map/ppermute | solution.py:22
  109.8 0.6 fusion.60
  110.4 0.5 convolution_convert_fusion
  110.9 4.5 %collective-permute-start.19 = (bf16[384,128]{1,0:T(8,128)(2,1)S(1)}, bf16[384,128]{1,0:T(8,128)(2,1)S(1)}, u32[]{:S(2)}, u32[]{:S(2)}) collective-permute-start(bf16[384,128]{1,0:T(8,128)(2,1)S(1)} %get-tuple-element.73), channel_id=1, source_target_pairs={{0,31},{1,30},{2,5},{3,4},{4,3},{5,2},{6,9},{7,8},{8,7},{9,6},{10,... | collective-permute-start | bytes 294920 | tf_op jit(solution)/shard_map/ppermute | solution.py:22
  115.5 0.6 fusion.69
  116.1 1.1 collective-permute-start.15
  117.2 0.6 add_convert_fusion
  117.8 0.5 convolution_convert_fusion.1
  118.3 2.6 %collective-permute-start.18 = (bf16[384,128]{1,0:T(8,128)(2,1)S(1)}, bf16[384,128]{1,0:T(8,128)(2,1)S(1)}, u32[]{:S(2)}, u32[]{:S(2)}) collective-permute-start(bf16[384,128]{1,0:T(8,128)(2,1)S(1)} %get-tuple-element.75), channel_id=1, source_target_pairs={{0,30},{1,31},{2,4},{3,5},{4,2},{5,3},{6,8},{7,9},{8,6},{9,7},{10,... | collective-permute-start | bytes 294920 | tf_op jit(solution)/shard_map/ppermute | solution.py:22
  121.0 0.6 fusion.33.refs_0_
  121.7 3.5 %collective-permute-done.18.refs_4_ = bf16[384,128]{1,0:T(8,128)(2,1)S(1)} collective-permute-done((bf16[384,128]{1,0:T(8,128)(2,1)S(1)}, bf16[384,128]{1,0:T(8,128)(2,1)S(1)}, u32[]{:S(2)}, u32[]{:S(2)}) %collective-permute-start.18) | collective-permute-done | bytes 98336 | tf_op jit(solution)/shard_map/ppermute | solution.py:22
  125.1 1.2 collective-permute-done.15.refs_1_
  126.3 2.6 %operate_closing.1 = (f32[1024,128]{1,0:T(8,128)S(1)}, f32[1024,128]{1,0:T(8,128)S(1)}, f32[16,4,128]{2,1,0:T(4,128)S(1)}) custom-call(f32[1024,128]{1,0:T(8,128)S(1)} %fusion.33.refs_0_, bf16[1024,128]{1,0:T(8,128)(2,1)S(1)} %collective-permute-done.15.refs_1_, bf16[384,128]{1,0:T(8,128)(2,1)S(1)} %collective-permute-done.16.refs_2_, ...), custom_call_target="tpu_custom_call" | custom-call | flops 469762048 | bytes 3670016 | tf_op jit(solution)/shard_map/operate_closing/pallas_call | solution.py:131
  128.9 10.8 %all_to_all.16 = f32[16,4,128]{2,1,0:T(4,128)S(1)} all-to-all(f32[16,4,128]{2,1,0:T(4,128)S(1)} %get-tuple-element.52), channel_id=1, replica_groups=mesh['sub'=16,'panel'=2] {'sub'}, dimensions={0} | all-to-all | bytes 65536 | tf_op jit(solution)/shard_map/all_to_all | solution.py:316
  139.7 0.5 fusion.123
  140.2 2.3 %multiply_subtract_fusion = (f32[1024,128]{1,0:T(8,128)}, f32[1024,128]{1,0:T(8,128)}) fusion(f32[1024,128]{1,0:T(8,128)} %copy-done.5, f32[1024,128]{1,0:T(8,128)S(1)} %get-tuple-element.54, f32[128]{0:T(128)S(1)} %get-tuple-element.60, f32[1024,128]{1,0:T(8,128)S(1)} %get-tuple-element.53, f32[1024,128]{1,0:T(8,128)} %param.14, ...), kind=kLoop, calls=%fused_computation.64 | loop fusion | flops 786432 | bytes 3671040 | tf_op jit(solution)/shard_map/sub | solution.py:347
  (79 shorter events, 0.5 us)
Async XLA Ops:
  0.6 11.5 %copy-start.10 = (f32[16,1024]{1,0:T(8,128)S(1)}, f32[16,1024]{1,0:T(8,128)}, u32[]{:S(2)}) copy-start(f32[16,1024]{1,0:T(8,128)} %weight_ref.3) | copy-start | bytes 196612
  2.6 19.1 %all-to-all-start = ((f32[16,2,128]{2,1,0:T(2,128)}), f32[16,2,128]{2,1,0:T(2,128)S(1)}, u32[]{:S(2)}, u32[]{:S(2)}) async-start(f32[16,2,128]{2,1,0:T(2,128)} %broadcast_in_dim.8), calls=%async_computation | async-start | bytes 32768 | tf_op jit(solution)/shard_map/all_to_all | solution.py:316
  11.7 4.3 %copy-start.15 = (f32[128]{0:T(128)S(1)}, f32[128]{0:T(128)}, u32[]{:S(2)}) copy-start(f32[128]{0:T(128)} %param.21) | copy-start | bytes 1540
  11.7 4.3 %copy-start.16 = (f32[128]{0:T(128)S(1)}, f32[128]{0:T(128)}, u32[]{:S(2)}) copy-start(f32[128]{0:T(128)} %param.20) | copy-start | bytes 1540
  11.7 4.3 %copy-start.17 = (f32[128]{0:T(128)S(1)}, f32[128]{0:T(128)}, u32[]{:S(2)}) copy-start(f32[128]{0:T(128)} %param.19) | copy-start | bytes 1540
  20.5 1.3 copy-start
  21.8 1.0 copy-start.3
  22.8 1.0 copy-start.6
  23.9 1.0 copy-start.7
  24.9 0.7 copy-start.11
  25.6 1.9 %copy-start.18 = (bf16[1,1792,896]{2,1,0:T(8,128)(2,1)S(1)}, bf16[1,1792,896]{2,1,0:T(8,128)(2,1)}, u32[]{:S(2)}) copy-start(bf16[1,1792,896]{2,1,0:T(8,128)(2,1)} %param.22) | copy-start | bytes 9633796
  28.1 29.1 %collective-permute-start.4 = (bf16[896,128]{1,0:T(8,128)(2,1)S(1)}, bf16[896,128]{1,0:T(8,128)(2,1)S(1)}, u32[]{:S(2)}, u32[]{:S(2)}) collective-permute-start(bf16[896,128]{1,0:T(8,128)(2,1)S(1)} %fusion.72), channel_id=1, source_target_pairs={{0,1},{2,3},{4,5},{6,7},{8,9},{10,11},{12,13},{14,15},{16,17},{18,... | collective-permute-start | bytes 688136 | tf_op jit(solution)/shard_map/ppermute | solution.py:22
  31.5 10.3 %collective-permute-start = (bf16[896,128]{1,0:T(8,128)(2,1)S(1)}, bf16[896,128]{1,0:T(8,128)(2,1)S(1)}, u32[]{:S(2)}, u32[]{:S(2)}) collective-permute-start(bf16[896,128]{1,0:T(8,128)(2,1)S(1)} %get-tuple-element.33), channel_id=1, source_target_pairs={{0,1},{1,0},{2,3},{3,2},{4,5},{5,4},{6,7},{7,6},{8,9},{9,8},{10,11... | collective-permute-start | bytes 688136 | tf_op jit(solution)/shard_map/ppermute | solution.py:22
  31.6 23.6 %copy-start.19 = (bf16[1,1792,896]{2,1,0:T(8,128)(2,1)S(1)}, bf16[1,1792,896]{2,1,0:T(8,128)(2,1)}, u32[]{:S(2)}) copy-start(bf16[1,1792,896]{2,1,0:T(8,128)(2,1)} %param.23) | copy-start | bytes 9633796
  42.5 14.6 %collective-permute-start.2 = (bf16[384,256]{1,0:T(8,128)(2,1)S(1)}, bf16[384,256]{1,0:T(8,128)(2,1)S(1)}, u32[]{:S(2)}, u32[]{:S(2)}) collective-permute-start(bf16[384,256]{1,0:T(8,128)(2,1)S(1)} %pad_maximum_fusion.1), channel_id=1, source_target_pairs={{1,3},{3,1},{5,7},{7,5},{9,11},{11,9},{13,15},{15,13},{17,19},{19,... | collective-permute-start | bytes 589832 | tf_op jit(solution)/shard_map/ppermute | solution.py:22
  43.2 13.8 %collective-permute-start.1 = (bf16[384,256]{1,0:T(8,128)(2,1)S(1)}, bf16[384,256]{1,0:T(8,128)(2,1)S(1)}, u32[]{:S(2)}, u32[]{:S(2)}) collective-permute-start(bf16[384,256]{1,0:T(8,128)(2,1)S(1)} %pad_maximum_fusion), channel_id=1, source_target_pairs={{1,31},{3,5},{5,3},{7,9},{9,7},{11,13},{13,11},{15,17},{17,15},{19... | collective-permute-start | bytes 589832 | tf_op jit(solution)/shard_map/ppermute | solution.py:22
  43.9 18.7 %collective-permute-start.3 = (bf16[896,128]{0,1:T(8,128)(2,1)S(1)}, bf16[896,128]{0,1:T(8,128)(2,1)S(1)}, u32[]{:S(2)}, u32[]{:S(2)}) collective-permute-start(bf16[896,128]{0,1:T(8,128)(2,1)S(1)} %fusion.81), channel_id=1, source_target_pairs={{0,1},{2,3},{4,5},{6,7},{8,9},{10,11},{12,13},{14,15},{16,17},{18,... | collective-permute-start | bytes 688136 | tf_op jit(solution)/shard_map/ppermute | solution.py:22
  58.5 4.1 %copy-start.12 = (f32[1024]{0:T(1024)S(1)}, f32[1024]{0:T(1024)}, u32[]{:S(2)}) copy-start(f32[1024]{0:T(1024)} %param.26) | copy-start | bytes 12292
  59.0 13.4 %collective-permute-start.9 = (bf16[384,128]{1,0:T(8,128)(2,1)S(1)}, bf16[384,128]{1,0:T(8,128)(2,1)S(1)}, u32[]{:S(2)}, u32[]{:S(2)}) collective-permute-start(bf16[384,128]{1,0:T(8,128)(2,1)S(1)} %get-tuple-element.81), channel_id=1, source_target_pairs={{0,31},{1,30},{2,5},{3,4},{4,3},{5,2},{6,9},{7,8},{8,7},{9,6},{10,... | collective-permute-start | bytes 294920 | tf_op jit(solution)/shard_map/ppermute | solution.py:22
  62.5 9.9 %collective-permute-start.7 = (bf16[384,128]{1,0:T(8,128)(2,1)S(1)}, bf16[384,128]{1,0:T(8,128)(2,1)S(1)}, u32[]{:S(2)}, u32[]{:S(2)}) collective-permute-start(bf16[384,128]{1,0:T(8,128)(2,1)S(1)} %get-tuple-element.82), channel_id=1, source_target_pairs={{0,3},{1,2},{2,1},{3,0},{4,7},{5,6},{6,5},{7,4},{8,11},{9,10},{10,... | collective-permute-start | bytes 294920 | tf_op jit(solution)/shard_map/ppermute | solution.py:22
  62.5 9.9 %collective-permute-start.5 = (bf16[1024,128]{1,0:T(8,128)(2,1)S(1)}, bf16[1024,128]{1,0:T(8,128)(2,1)S(1)}, u32[]{:S(2)}, u32[]{:S(2)}) collective-permute-start(bf16[1024,128]{1,0:T(8,128)(2,1)S(1)} %fusion.66), channel_id=1, source_target_pairs={{0,1},{1,0},{2,3},{3,2},{4,5},{5,4},{6,7},{7,6},{8,9},{9,8},{10,11... | collective-permute-start | bytes 786440 | tf_op jit(solution)/shard_map/ppermute | solution.py:22
  63.8 8.9 %copy-start.1 = (bf16[512,1792]{1,0:T(8,128)(2,1)S(1)}, bf16[512,1792]{1,0:T(8,128)(2,1)}, u32[]{:S(2)}) copy-start(bf16[512,1792]{1,0:T(8,128)(2,1)} %copy-done) | copy-start | bytes 5505028
  63.8 8.9 %copy-start.2 = (f32[1024,128]{1,0:T(8,128)S(1)}, f32[1024,128]{1,0:T(8,128)}, u32[]{:S(2)}) copy-start(f32[1024,128]{1,0:T(8,128)} %refs_7_.3) | copy-start | bytes 1572868
  63.8 8.6 %collective-permute-start.8 = (bf16[384,128]{1,0:T(8,128)(2,1)S(1)}, bf16[384,128]{1,0:T(8,128)(2,1)S(1)}, u32[]{:S(2)}, u32[]{:S(2)}) collective-permute-start(bf16[384,128]{1,0:T(8,128)(2,1)S(1)} %get-tuple-element.83), channel_id=1, source_target_pairs={{0,30},{1,31},{2,4},{3,5},{4,2},{5,3},{6,8},{7,9},{8,6},{9,7},{10,... | collective-permute-start | bytes 294920 | tf_op jit(solution)/shard_map/ppermute | solution.py:22
  66.1 6.4 %collective-permute-start.6 = (bf16[384,128]{1,0:T(8,128)(2,1)S(1)}, bf16[384,128]{1,0:T(8,128)(2,1)S(1)}, u32[]{:S(2)}, u32[]{:S(2)}) collective-permute-start(bf16[384,128]{1,0:T(8,128)(2,1)S(1)} %get-tuple-element.84), channel_id=1, source_target_pairs={{0,2},{1,3},{2,0},{3,1},{4,6},{5,7},{6,4},{7,5},{8,10},{9,11},{10,... | collective-permute-start | bytes 294920 | tf_op jit(solution)/shard_map/ppermute | solution.py:22
  72.7 12.6 %copy-start.4 = (f32[1024,128]{1,0:T(8,128)S(1)}, f32[1024,128]{1,0:T(8,128)}, u32[]{:S(2)}) copy-start(f32[1024,128]{1,0:T(8,128)} %refs_3_.3) | copy-start | bytes 1572868
  75.2 11.8 %copy-start.8 = (f32[1024,128]{1,0:T(8,128)}, f32[1024,128]{1,0:T(8,128)S(1)}, u32[]{:S(2)}) copy-start(f32[1024,128]{1,0:T(8,128)S(1)} %get-tuple-element.48) | copy-start | bytes 1572868
  86.4 39.9 %copy-start.5 = (f32[1024,128]{1,0:T(8,128)}, f32[1024,128]{1,0:T(8,128)S(1)}, u32[]{:S(2)}) copy-start(f32[1024,128]{1,0:T(8,128)S(1)} %get-tuple-element.51.refs_8_) | copy-start | bytes 1572868
  87.0 22.7 %collective-permute-start.14 = (bf16[896,128]{1,0:T(8,128)(2,1)S(1)}, bf16[896,128]{1,0:T(8,128)(2,1)S(1)}, u32[]{:S(2)}, u32[]{:S(2)}) collective-permute-start(bf16[896,128]{1,0:T(8,128)(2,1)S(1)} %fusion.78), channel_id=1, source_target_pairs={{0,1},{2,3},{4,5},{6,7},{8,9},{10,11},{12,13},{14,15},{16,17},{18,... | collective-permute-start | bytes 688136 | tf_op jit(solution)/shard_map/ppermute | solution.py:22
  89.9 9.7 %collective-permute-start.10 = (bf16[896,128]{1,0:T(8,128)(2,1)S(1)}, bf16[896,128]{1,0:T(8,128)(2,1)S(1)}, u32[]{:S(2)}, u32[]{:S(2)}) collective-permute-start(bf16[896,128]{1,0:T(8,128)(2,1)S(1)} %get-tuple-element.50), channel_id=1, source_target_pairs={{0,1},{1,0},{2,3},{3,2},{4,5},{5,4},{6,7},{7,6},{8,9},{9,8},{10,11... | collective-permute-start | bytes 688136 | tf_op jit(solution)/shard_map/ppermute | solution.py:22
  99.6 10.0 %collective-permute-start.12 = (bf16[384,256]{1,0:T(8,128)(2,1)S(1)}, bf16[384,256]{1,0:T(8,128)(2,1)S(1)}, u32[]{:S(2)}, u32[]{:S(2)}) collective-permute-start(bf16[384,256]{1,0:T(8,128)(2,1)S(1)} %pad_maximum_fusion.3), channel_id=1, source_target_pairs={{1,3},{3,1},{5,7},{7,5},{9,11},{11,9},{13,15},{15,13},{17,19},{19,... | collective-permute-start | bytes 589832 | tf_op jit(solution)/shard_map/ppermute | solution.py:22
  100.3 9.3 %collective-permute-start.11 = (bf16[384,256]{1,0:T(8,128)(2,1)S(1)}, bf16[384,256]{1,0:T(8,128)(2,1)S(1)}, u32[]{:S(2)}, u32[]{:S(2)}) collective-permute-start(bf16[384,256]{1,0:T(8,128)(2,1)S(1)} %pad_maximum_fusion.2), channel_id=1, source_target_pairs={{1,31},{3,5},{5,3},{7,9},{9,7},{11,13},{13,11},{15,17},{17,15},{19... | collective-permute-start | bytes 589832 | tf_op jit(solution)/shard_map/ppermute | solution.py:22
  101.8 15.4 %collective-permute-start.13 = (bf16[896,128]{1,0:T(8,128)(2,1)S(1)}, bf16[896,128]{1,0:T(8,128)(2,1)S(1)}, u32[]{:S(2)}, u32[]{:S(2)}) collective-permute-start(bf16[896,128]{1,0:T(8,128)(2,1)S(1)} %fusion.75), channel_id=1, source_target_pairs={{0,1},{2,3},{4,5},{6,7},{8,9},{10,11},{12,13},{14,15},{16,17},{18,... | collective-permute-start | bytes 688136 | tf_op jit(solution)/shard_map/ppermute | solution.py:22
  110.9 10.7 %collective-permute-start.19 = (bf16[384,128]{1,0:T(8,128)(2,1)S(1)}, bf16[384,128]{1,0:T(8,128)(2,1)S(1)}, u32[]{:S(2)}, u32[]{:S(2)}) collective-permute-start(bf16[384,128]{1,0:T(8,128)(2,1)S(1)} %get-tuple-element.73), channel_id=1, source_target_pairs={{0,31},{1,30},{2,5},{3,4},{4,3},{5,2},{6,9},{7,8},{8,7},{9,6},{10,... | collective-permute-start | bytes 294920 | tf_op jit(solution)/shard_map/ppermute | solution.py:22
  115.5 6.2 %collective-permute-start.17 = (bf16[384,128]{1,0:T(8,128)(2,1)S(1)}, bf16[384,128]{1,0:T(8,128)(2,1)S(1)}, u32[]{:S(2)}, u32[]{:S(2)}) collective-permute-start(bf16[384,128]{1,0:T(8,128)(2,1)S(1)} %get-tuple-element.74), channel_id=1, source_target_pairs={{0,3},{1,2},{2,1},{3,0},{4,7},{5,6},{6,5},{7,4},{8,11},{9,10},{10,... | collective-permute-start | bytes 294920 | tf_op jit(solution)/shard_map/ppermute | solution.py:22
  116.1 10.2 %collective-permute-start.15 = (bf16[1024,128]{1,0:T(8,128)(2,1)S(1)}, bf16[1024,128]{1,0:T(8,128)(2,1)S(1)}, u32[]{:S(2)}, u32[]{:S(2)}) collective-permute-start(bf16[1024,128]{1,0:T(8,128)(2,1)S(1)} %fusion.69), channel_id=1, source_target_pairs={{0,1},{1,0},{2,3},{3,2},{4,5},{5,4},{6,7},{7,6},{8,9},{9,8},{10,11... | collective-permute-start | bytes 786440 | tf_op jit(solution)/shard_map/ppermute | solution.py:22
  118.3 6.8 %collective-permute-start.18 = (bf16[384,128]{1,0:T(8,128)(2,1)S(1)}, bf16[384,128]{1,0:T(8,128)(2,1)S(1)}, u32[]{:S(2)}, u32[]{:S(2)}) collective-permute-start(bf16[384,128]{1,0:T(8,128)(2,1)S(1)} %get-tuple-element.75), channel_id=1, source_target_pairs={{0,30},{1,31},{2,4},{3,5},{4,2},{5,3},{6,8},{7,9},{8,6},{9,7},{10,... | collective-permute-start | bytes 294920 | tf_op jit(solution)/shard_map/ppermute | solution.py:22
  121.0 4.2 %collective-permute-start.16 = (bf16[384,128]{1,0:T(8,128)(2,1)S(1)}, bf16[384,128]{1,0:T(8,128)(2,1)S(1)}, u32[]{:S(2)}, u32[]{:S(2)}) collective-permute-start(bf16[384,128]{1,0:T(8,128)(2,1)S(1)} %get-tuple-element.76), channel_id=1, source_target_pairs={{0,2},{1,3},{2,0},{3,1},{4,6},{5,7},{6,4},{7,5},{8,10},{9,11},{10,... | collective-permute-start | bytes 294920 | tf_op jit(solution)/shard_map/ppermute | solution.py:22
  126.3 13.9 %copy-start.9 = (f32[1024,128]{1,0:T(8,128)S(1)}, f32[1024,128]{1,0:T(8,128)}, u32[]{:S(2)}) copy-start(f32[1024,128]{1,0:T(8,128)} %copy-done.8) | copy-start | bytes 1572868
  126.3 13.9 %copy-start.14 = (f32[1,128]{1,0:T(1,128)S(1)}, f32[1,128]{1,0:T(1,128)}, u32[]{:S(2)}) copy-start(f32[1,128]{1,0:T(1,128)} %get-tuple-element.47) | copy-start | bytes 1540
  140.2 2.3 %copy-start.13 = (f32[128]{0:T(128)}, f32[128]{0:T(128)S(1)}, u32[]{:S(2)}) copy-start(f32[128]{0:T(128)S(1)} %get-tuple-element.60) | copy-start | bytes 1540
